TPU v7x, 8 devices: a whole 2x2x1 slice. The times are simulated.
8 devices in a mesh: local: 4 (over z, y, x), data: 2 (over core).
Axes of the slice: x: 2, y: 2, z: 1, core: 2. Of those that a mesh axis runs over, the one named last changes fastest.
Arguments:
- x_in: bfloat16 [32768, 1024], P(('local', 'data'))
- grad_out: bfloat16 [32768, 1024], P(('local', 'data'))
- w_in: bfloat16 [5, 1024, 4096], P(None, ('local', 'data'))
- w_out: bfloat16 [5, 4096, 1024], P(None, ('local', 'data'))
Outputs:
- output 1: bfloat16 [32768, 1024], P(('local', 'data'))
- output 2: float32 [5, 1024, 4096], P(None, ('local', 'data'))
- output 3: float32 [5, 4096, 1024], P(None, ('local', 'data'))
- output 4: bfloat16 [32768, 1024], P(('local', 'data'))
All inputs are finite; a program needn't handle non-finite values.
Results may differ from a plain program's by a relative error of at most 0.02.
Values are sent between devices in bfloat16 or wider.
A program may use at most 1 GiB of HBM per device.

v0:
```python
import jax
import jax.numpy as jnp
from jax import lax
from jax.sharding import PartitionSpec as P, NamedSharding

NORM_EPS = 1e-6
LAST_LAST = (((1,), (1,)), ((), ()))
FIRST_FIRST = (((0,), (0,)), ((), ()))


def norm_rows(x_rows):
    x_wide = x_rows.astype(jnp.float32)
    inv_rms = lax.rsqrt(jnp.mean(x_wide * x_wide, axis=-1, keepdims=True) + NORM_EPS)
    return x_wide * inv_rms, inv_rms


def layer_forward(x_rows, w_in, w_out):
    unit_rows = norm_rows(x_rows)[0].astype(jnp.bfloat16)
    pre_act = jnp.dot(unit_rows, w_in, preferred_element_type=jnp.float32).astype(jnp.bfloat16)
    hidden = jax.nn.gelu(pre_act.astype(jnp.float32)).astype(jnp.bfloat16)
    branch = jnp.dot(hidden, w_out, preferred_element_type=jnp.float32)
    return (x_rows.astype(jnp.float32) + branch).astype(jnp.bfloat16)


def layer_backward(x_rows, grad_rows, w_in, w_out):
    unit_wide, inv_rms = norm_rows(x_rows)
    unit_rows = unit_wide.astype(jnp.bfloat16)
    pre_act = jnp.dot(unit_rows, w_in, preferred_element_type=jnp.float32).astype(jnp.bfloat16)
    gelu_val, gelu_back = jax.vjp(jax.nn.gelu, pre_act.astype(jnp.float32))
    hidden = gelu_val.astype(jnp.bfloat16)
    grad_hidden = lax.dot_general(grad_rows, w_out, LAST_LAST, preferred_element_type=jnp.float32)
    grad_pre = gelu_back(grad_hidden)[0].astype(jnp.bfloat16)
    grad_w_out = lax.dot_general(hidden, grad_rows, FIRST_FIRST, preferred_element_type=jnp.float32)
    grad_w_in = lax.dot_general(unit_rows, grad_pre, FIRST_FIRST, preferred_element_type=jnp.float32)
    grad_unit = lax.dot_general(grad_pre, w_in, LAST_LAST, preferred_element_type=jnp.float32)
    row_mean = jnp.mean(grad_unit * unit_wide, axis=-1, keepdims=True)
    grad_x = grad_rows.astype(jnp.float32) + inv_rms * (grad_unit - unit_wide * row_mean)
    return grad_x.astype(jnp.bfloat16), grad_w_in, grad_w_out


def solution(mesh):
    row_spec = P(('local', 'data'), None)
    weight_spec = P(None, ('local', 'data'), None)

    def device_step(x_rows, grad_rows, w_in_part, w_out_part):
        layers = w_in_part.shape[0]
        saved_x = []
        kept_in = []
        kept_out = []
        x_cur = x_rows
        for layer_idx in range(layers):
            sub_in = lax.all_gather(w_in_part[layer_idx], 'data', axis=0, tiled=True)
            sub_out = lax.all_gather(w_out_part[layer_idx], 'data', axis=0, tiled=True)
            full_in = lax.all_gather(sub_in, 'local', axis=0, tiled=True)
            full_out = lax.all_gather(sub_out, 'local', axis=0, tiled=True)
            saved_x.append(x_cur)
            kept_in.append(sub_in)
            kept_out.append(sub_out)
            x_cur = layer_forward(x_cur, full_in, full_out)
        grad_cur = grad_rows
        grads_in = []
        grads_out = []
        for layer_idx in reversed(range(layers)):
            sub_in, sub_out, grad_cur = lax.optimization_barrier((kept_in[layer_idx], kept_out[layer_idx], grad_cur))
            full_in = lax.all_gather(sub_in, 'local', axis=0, tiled=True)
            full_out = lax.all_gather(sub_out, 'local', axis=0, tiled=True)
            grad_cur, part_in, part_out = layer_backward(saved_x[layer_idx], grad_cur, full_in, full_out)
            grads_in.append(lax.psum_scatter(part_in, ('local', 'data'), scatter_dimension=0, tiled=True))
            grads_out.append(lax.psum_scatter(part_out, ('local', 'data'), scatter_dimension=0, tiled=True))
        return x_cur, jnp.stack(grads_in[::-1]), jnp.stack(grads_out[::-1]), grad_cur

    return jax.shard_map(device_step, mesh=mesh, in_specs=(row_spec, row_spec, weight_spec, weight_spec), out_specs=(row_spec, weight_spec, weight_spec, row_spec), check_vma=False)
```

profile of v0, /device:TPU:0, one launch (start us, length us, event | category | flops | bytes accessed | tf_op | source)
XLA Modules:
  0.0 3478.2 jit_solution(15135986662728728432)
XLA Ops:
  148.6 55.7 %all-gather.73.cloned.1.call-done = bf16[1,1024,4096]{2,1,0:T(8,128)(2,1)} async-done(((bf16[1,256,4096]{2,1,0:T(8,128)(2,1)}), bf16[1,1024,4096]{2,1,0:T(8,128)(2,1)}) %all-gather.73.cloned.1.call-update) | async-done | bytes 8388624 | tf_op jit(solution)/shard_map/all_gather | solution.py:54
  204.3 58.9 %fusion.180.clone.4 = bf16[4096,4096]{1,0:T(8,128)(2,1)} fusion(bf16[1,1024,4096]{2,1,0:T(8,128)(2,1)} %all-gather.73.cloned.1.call-done, bf16[4096,1024]{0,1:T(8,128)(2,1)} %copy.8, f32[4096]{0:T(1024)S(1)} %add_rsqrt_fusion.4), kind=kOutput, calls=%fused_computation.70.clone.clone.clone.clone.clone.clone.1 | convolution fusion | flops 34556870656 | bytes 50348032 | tf_op jit(solution)/shard_map/dot_general | solution.py:19
  371.4 58.5 %fusion.186.clone.2 = bf16[4096,4096]{1,0:T(8,128)(2,1)} fusion(bf16[1,1024,4096]{2,1,0:T(8,128)(2,1)} %all-gather.81.cloned.1.call-done, bf16[4096,1024]{0,1:T(8,128)(2,1)} %get-tuple-element.49, f32[4096]{0:T(1024)S(1)} %add_rsqrt_fusion.3), kind=kOutput, calls=%fused_computation.76.clone.clone.clone.clone.clone.clone | convolution fusion | flops 34556870656 | bytes 50348032 | tf_op jit(solution)/shard_map/dot_general | solution.py:19
  538.4 58.7 %fusion.192.clone.2 = bf16[4096,4096]{1,0:T(8,128)(2,1)} fusion(bf16[1,1024,4096]{2,1,0:T(8,128)(2,1)} %all-gather.89.cloned.1.call-done, bf16[4096,1024]{0,1:T(8,128)(2,1)} %get-tuple-element.51, f32[4096]{0:T(1024)S(1)} %add_rsqrt_fusion.2), kind=kOutput, calls=%fused_computation.82.clone.clone.clone.clone.clone.clone | convolution fusion | flops 34556870656 | bytes 50348032 | tf_op jit(solution)/shard_map/dot_general | solution.py:19
  705.4 58.5 %fusion.198.clone.2 = bf16[4096,4096]{1,0:T(8,128)(2,1)} fusion(bf16[1,1024,4096]{2,1,0:T(8,128)(2,1)} %all-gather.97.cloned.1.call-done, bf16[4096,1024]{0,1:T(8,128)(2,1)} %get-tuple-element.53, f32[4096]{0:T(1024)S(1)} %add_rsqrt_fusion.1), kind=kOutput, calls=%fused_computation.88.clone.clone.clone.clone.clone.clone | convolution fusion | flops 34556870656 | bytes 50348032 | tf_op jit(solution)/shard_map/dot_general | solution.py:19
  956.0 85.1 %fusion.19 = bf16[4096,4096]{1,0:T(8,128)(2,1)} fusion(bf16[4096,4096]{1,0:T(8,128)(2,1)} %convolution_convert_fusion.4, bf16[4096,1024]{1,0:T(8,128)(2,1)} %param.5, bf16[4096,1024]{1,0:T(8,128)(2,1)} %all-gather.51.cloned.1.call-done), kind=kOutput, calls=%fused_computation.64 | convolution fusion | flops 34712059904 | bytes 83886080 | tf_op jit(solution)/shard_map/dot_general | solution.py:31
  1041.0 44.5 %fusion.115 = (f32[4096]{0:T(1024)S(1)}, f32[4096,1024]{0,1:T(8,128)}) fusion(bf16[4096,1024]{0,1:T(8,128)(2,1)} %get-tuple-element.55, f32[4096]{0:T(1024)S(1)} %add_rsqrt_fusion, bf16[4096,4096]{1,0:T(8,128)(2,1)} %fusion.19, bf16[1024,4096]{1,0:T(8,128)(2,1)} %all-gather.53.cloned.1.call-done), kind=kOutput, calls=%fused_computation.170 | convolution fusion | flops 34376511488 | bytes 67141632 | tf_op jit(solution)/shard_map/dot_general | solution.py:35
  1099.4 81.2 %all-gather.57.cloned.1.call-done = bf16[1024,4096]{1,0:T(8,128)(2,1)} async-done(((bf16[256,4096]{1,0:T(8,128)(2,1)}), bf16[1024,4096]{1,0:T(8,128)(2,1)}) %all-gather.57.cloned.1.call-update) | async-done | bytes 8388624 | tf_op jit(solution)/shard_map/all_gather | solution.py:65
  1264.2 87.9 %fusion.16 = bf16[4096,4096]{1,0:T(8,128)(2,1)} fusion(bf16[4096,4096]{1,0:T(8,128)(2,1)} %convolution_convert_fusion.3, bf16[4096,1024]{0,1:T(8,128)(2,1)} %fusion.119, bf16[4096,1024]{1,0:T(8,128)(2,1)} %all-gather.55.cloned.1.call-done), kind=kOutput, calls=%fused_computation.61 | convolution fusion | flops 34712059904 | bytes 83886080 | tf_op jit(solution)/shard_map/dot_general | solution.py:31
  1352.1 44.3 %fusion.120 = (f32[4096]{0:T(1024)S(1)}, f32[4096,1024]{0,1:T(8,128)}) fusion(bf16[4096,1024]{0,1:T(8,128)(2,1)} %get-tuple-element.53, f32[4096]{0:T(1024)S(1)} %copy-done.17, bf16[4096,4096]{1,0:T(8,128)(2,1)} %fusion.16, bf16[1024,4096]{1,0:T(8,128)(2,1)} %all-gather.57.cloned.1.call-done), kind=kOutput, calls=%fused_computation.175 | convolution fusion | flops 34376511488 | bytes 67141632 | tf_op jit(solution)/shard_map/dot_general | solution.py:35
  1410.1 81.4 %all-gather.61.cloned.1.call-done = bf16[1024,4096]{1,0:T(8,128)(2,1)} async-done(((bf16[256,4096]{1,0:T(8,128)(2,1)}), bf16[1024,4096]{1,0:T(8,128)(2,1)}) %all-gather.61.cloned.1.call-update) | async-done | bytes 8388624 | tf_op jit(solution)/shard_map/all_gather | solution.py:65
  1491.5 43.7 %convolution_convert_fusion.2 = bf16[4096,4096]{1,0:T(8,128)(2,1)} fusion(bf16[1024,4096]{1,0:T(8,128)(2,1)} %all-gather.61.cloned.1.call-done, bf16[4096,1024]{0,1:T(8,128)(2,1)} %get-tuple-element.51, f32[4096]{0:T(1024)S(1)} %copy-done.14), kind=kOutput, calls=%fused_computation.137 | convolution fusion | flops 34389098496 | bytes 50348032 | tf_op jit(solution)/shard_map/dot_general | solution.py:28
  1575.0 87.9 %fusion.13 = bf16[4096,4096]{1,0:T(8,128)(2,1)} fusion(bf16[4096,4096]{1,0:T(8,128)(2,1)} %convolution_convert_fusion.2, bf16[4096,1024]{0,1:T(8,128)(2,1)} %fusion.124, bf16[4096,1024]{1,0:T(8,128)(2,1)} %all-gather.59.cloned.1.call-done), kind=kOutput, calls=%fused_computation.58 | convolution fusion | flops 34712059904 | bytes 83886080 | tf_op jit(solution)/shard_map/dot_general | solution.py:31
  1662.9 44.2 %fusion.125 = (f32[4096]{0:T(1024)S(1)}, f32[4096,1024]{0,1:T(8,128)}) fusion(bf16[4096,1024]{0,1:T(8,128)(2,1)} %get-tuple-element.51, f32[4096]{0:T(1024)S(1)} %copy-done.14, bf16[4096,4096]{1,0:T(8,128)(2,1)} %fusion.13, bf16[1024,4096]{1,0:T(8,128)(2,1)} %all-gather.61.cloned.1.call-done), kind=kOutput, calls=%fused_computation.180 | convolution fusion | flops 34376511488 | bytes 67141632 | tf_op jit(solution)/shard_map/dot_general | solution.py:35
  1720.9 81.3 %all-gather.65.cloned.1.call-done = bf16[1024,4096]{1,0:T(8,128)(2,1)} async-done(((bf16[256,4096]{1,0:T(8,128)(2,1)}), bf16[1024,4096]{1,0:T(8,128)(2,1)}) %all-gather.65.cloned.1.call-update) | async-done | bytes 8388624 | tf_op jit(solution)/shard_map/all_gather | solution.py:65
  1802.2 43.5 %convolution_convert_fusion.1 = bf16[4096,4096]{1,0:T(8,128)(2,1)} fusion(bf16[1024,4096]{1,0:T(8,128)(2,1)} %all-gather.65.cloned.1.call-done, bf16[4096,1024]{0,1:T(8,128)(2,1)} %get-tuple-element.49, f32[4096]{0:T(1024)S(1)} %copy-done.11), kind=kOutput, calls=%fused_computation.136 | convolution fusion | flops 34389098496 | bytes 50348032 | tf_op jit(solution)/shard_map/dot_general | solution.py:28
  1885.7 87.9 %fusion.10 = bf16[4096,4096]{1,0:T(8,128)(2,1)} fusion(bf16[4096,4096]{1,0:T(8,128)(2,1)} %convolution_convert_fusion.1, bf16[4096,1024]{0,1:T(8,128)(2,1)} %fusion.129, bf16[4096,1024]{1,0:T(8,128)(2,1)} %all-gather.63.cloned.1.call-done), kind=kOutput, calls=%fused_computation.55 | convolution fusion | flops 34712059904 | bytes 83886080 | tf_op jit(solution)/shard_map/dot_general | solution.py:31
  1973.6 44.4 %fusion.130 = (f32[4096]{0:T(1024)S(1)}, f32[4096,1024]{0,1:T(8,128)}) fusion(bf16[4096,1024]{0,1:T(8,128)(2,1)} %get-tuple-element.49, f32[4096]{0:T(1024)S(1)} %copy-done.11, bf16[4096,4096]{1,0:T(8,128)(2,1)} %fusion.10, bf16[1024,4096]{1,0:T(8,128)(2,1)} %all-gather.65.cloned.1.call-done), kind=kOutput, calls=%fused_computation.185 | convolution fusion | flops 34376511488 | bytes 67141632 | tf_op jit(solution)/shard_map/dot_general | solution.py:35
  2033.2 79.9 %all-gather.69.cloned.1.call-done = bf16[1024,4096]{1,0:T(8,128)(2,1)} async-done(((bf16[256,4096]{1,0:T(8,128)(2,1)}), bf16[1024,4096]{1,0:T(8,128)(2,1)}) %all-gather.69.cloned.1.call-update) | async-done | bytes 8388624 | tf_op jit(solution)/shard_map/all_gather | solution.py:65
  2156.6 53.6 %fusion.80 = f32[4096,1024]{1,0:T(8,128)} fusion(bf16[4096,1024]{0,1:T(8,128)(2,1)} %fusion.134, bf16[4096,4096]{1,0:T(8,128)(2,1)} %convolution_convert_fusion), kind=kOutput, calls=%fused_computation.125 | convolution fusion | flops 34527510528 | bytes 58720256 | tf_op jit(solution)/shard_map/dot_general | solution.py:33
  2210.2 53.6 %fusion.82 = f32[4096,1024]{1,0:T(8,128)} fusion(bf16[4096,1024]{0,1:T(8,128)(2,1)} %fusion.129, bf16[4096,4096]{1,0:T(8,128)(2,1)} %convolution_convert_fusion.1), kind=kOutput, calls=%fused_computation.126 | convolution fusion | flops 34527510528 | bytes 58720256 | tf_op jit(solution)/shard_map/dot_general | solution.py:33
  2263.9 53.8 %fusion.84 = f32[4096,1024]{1,0:T(8,128)} fusion(bf16[4096,1024]{0,1:T(8,128)(2,1)} %fusion.124, bf16[4096,4096]{1,0:T(8,128)(2,1)} %convolution_convert_fusion.2), kind=kOutput, calls=%fused_computation.127 | convolution fusion | flops 34527510528 | bytes 58720256 | tf_op jit(solution)/shard_map/dot_general | solution.py:33
  2317.8 53.6 %fusion.86 = f32[4096,1024]{1,0:T(8,128)} fusion(bf16[4096,1024]{0,1:T(8,128)(2,1)} %fusion.119, bf16[4096,4096]{1,0:T(8,128)(2,1)} %convolution_convert_fusion.3), kind=kOutput, calls=%fused_computation.128 | convolution fusion | flops 34527510528 | bytes 58720256 | tf_op jit(solution)/shard_map/dot_general | solution.py:33
  2371.5 55.3 %fusion.88 = f32[4096,1024]{1,0:T(8,128)} fusion(bf16[4096,1024]{1,0:T(8,128)(2,1)} %param.5, bf16[4096,4096]{1,0:T(8,128)(2,1)} %convolution_convert_fusion.4), kind=kOutput, calls=%fused_computation.129 | convolution fusion | flops 34527510528 | bytes 58720256 | tf_op jit(solution)/shard_map/dot_general | solution.py:33
  2426.9 88.2 %fusion.7 = bf16[4096,4096]{1,0:T(8,128)(2,1)} fusion(bf16[4096,4096]{1,0:T(8,128)(2,1)} %convolution_convert_fusion, bf16[4096,1024]{0,1:T(8,128)(2,1)} %fusion.134, bf16[4096,1024]{1,0:T(8,128)(2,1)} %all-gather.67.cloned.1.call-done), kind=kOutput, calls=%fused_computation.52 | convolution fusion | flops 34712059904 | bytes 83886080 | tf_op jit(solution)/shard_map/dot_general | solution.py:31
  2734.7 58.7 %fusion.351 = bf16[4096,4096]{1,0:T(8,128)(2,1)} fusion(bf16[1,1024,4096]{2,1,0:T(8,128)(2,1)} %all-gather.105.cloned.1.call-done, bf16[4096,1024]{0,1:T(8,128)(2,1)} %get-tuple-element.55, f32[4096]{0:T(1024)S(1)} %copy-done.9), kind=kOutput, calls=%fused_computation.94.clone.clone.clone.clone.1 | convolution fusion | flops 34556870656 | bytes 50348032 | tf_op jit(solution)/shard_map/dot_general | solution.py:19
  2847.8 44.1 %fusion.135 = (f32[4096]{0:T(1024)S(1)}, f32[4096,1024]{0,1:T(8,128)}) fusion(bf16[4096,1024]{0,1:T(8,128)(2,1)} %copy.8, f32[4096]{0:T(1024)S(1)} %copy-done.7, bf16[4096,4096]{1,0:T(8,128)(2,1)} %fusion.7, bf16[1024,4096]{1,0:T(8,128)(2,1)} %all-gather.69.cloned.1.call-done), kind=kOutput, calls=%fused_computation.190 | convolution fusion | flops 34376511488 | bytes 67141632 | tf_op jit(solution)/shard_map/dot_general | solution.py:35
  2934.9 91.4 %reduce-scatter.11.cloned.1.call-done = f32[128,4096]{1,0:T(8,128)} async-done(((f32[1024,4096]{1,0:T(8,128)}), f32[128,4096]{1,0:T(8,128)}) %reduce-scatter.11.cloned.1.call-update) | async-done | bytes 2097168 | tf_op jit(solution)/shard_map/reduce_scatter | solution.py:68
  3029.5 107.2 %reduce-scatter.13.cloned.1.call-done = f32[128,4096]{1,0:T(8,128)} async-done(((f32[1024,4096]{1,0:T(8,128)}), f32[128,4096]{1,0:T(8,128)}) %reduce-scatter.13.cloned.1.call-update) | async-done | bytes 2097168 | tf_op jit(solution)/shard_map/reduce_scatter | solution.py:68
  3139.8 107.4 %reduce-scatter.15.cloned.1.call-done = f32[128,4096]{1,0:T(8,128)} async-done(((f32[1024,4096]{1,0:T(8,128)}), f32[128,4096]{1,0:T(8,128)}) %reduce-scatter.15.cloned.1.call-update) | async-done | bytes 2097168 | tf_op jit(solution)/shard_map/reduce_scatter | solution.py:68
  3250.3 107.2 %reduce-scatter.17.cloned.1.call-done = f32[128,4096]{1,0:T(8,128)} async-done(((f32[1024,4096]{1,0:T(8,128)}), f32[128,4096]{1,0:T(8,128)}) %reduce-scatter.17.cloned.1.call-update) | async-done | bytes 2097168 | tf_op jit(solution)/shard_map/reduce_scatter | solution.py:68
  3360.6 107.4 %reduce-scatter.19.cloned.1.call-done = f32[128,4096]{1,0:T(8,128)} async-done(((f32[1024,4096]{1,0:T(8,128)}), f32[128,4096]{1,0:T(8,128)}) %reduce-scatter.19.cloned.1.call-update) | async-done | bytes 2097168 | tf_op jit(solution)/shard_map/reduce_scatter | solution.py:68
  (193 shorter events, 1254.0 us)
Async XLA Ops:
  21.1 87.4 %all-gather.103.cloned.1.call-start = ((), (), s32[]{:S(2)}) async-start(), calls=%async_computation.46 | async-start | bytes 3145728 | tf_op jit(solution)/shard_map/all_gather | solution.py:52
  21.8 97.6 %all-gather.107.cloned.1.call-start = ((), (), s32[]{:S(2)}) async-start(), calls=%async_computation.48 | async-start | bytes 3145728 | tf_op jit(solution)/shard_map/all_gather | solution.py:53
  22.4 181.9 %all-gather.73.cloned.1.call-start = ((), (), s32[]{:S(2)}) async-start(), calls=%async_computation.31 | async-start | bytes 10485760 | tf_op jit(solution)/shard_map/all_gather | solution.py:54
  23.2 264.6 %all-gather.77.cloned.1.call-start = ((), (), s32[]{:S(2)}) async-start(), calls=%async_computation.33 | async-start | bytes 10485760 | tf_op jit(solution)/shard_map/all_gather | solution.py:55
  34.1 337.4 %all-gather.81.cloned.1.call-start = ((), (), s32[]{:S(2)}) async-start(), calls=%async_computation.35 | async-start | bytes 10485760 | tf_op jit(solution)/shard_map/all_gather | solution.py:54
  44.6 410.3 %all-gather.85.cloned.1.call-start = ((), (), s32[]{:S(2)}) async-start(), calls=%async_computation.37 | async-start | bytes 10485760 | tf_op jit(solution)/shard_map/all_gather | solution.py:55
  55.6 482.8 %all-gather.89.cloned.1.call-start = ((), (), s32[]{:S(2)}) async-start(), calls=%async_computation.39 | async-start | bytes 10485760 | tf_op jit(solution)/shard_map/all_gather | solution.py:54
  66.0 555.9 %all-gather.93.cloned.1.call-start = ((), (), s32[]{:S(2)}) async-start(), calls=%async_computation.41 | async-start | bytes 10485760 | tf_op jit(solution)/shard_map/all_gather | solution.py:55
  76.9 628.4 %all-gather.97.cloned.1.call-start = ((), (), s32[]{:S(2)}) async-start(), calls=%async_computation.43 | async-start | bytes 10485760 | tf_op jit(solution)/shard_map/all_gather | solution.py:54
  87.5 701.4 %all-gather.101.cloned.1.call-start = ((), (), s32[]{:S(2)}) async-start(), calls=%async_computation.45 | async-start | bytes 10485760 | tf_op jit(solution)/shard_map/all_gather | solution.py:55
  98.0 774.5 %all-gather.53.cloned.1.call-start = ((), (), s32[]{:S(2)}) async-start(), calls=%async_computation.11 | async-start | bytes 10485760 | tf_op jit(solution)/shard_map/all_gather | solution.py:65
  119.5 836.4 %all-gather.51.cloned.1.call-start = ((), (), s32[]{:S(2)}) async-start(), calls=%async_computation.10 | async-start | bytes 10485760 | tf_op jit(solution)/shard_map/all_gather | solution.py:66
  148.5 1032.0 %all-gather.57.cloned.1.call-start = ((), (), s32[]{:S(2)}) async-start(), calls=%async_computation.13 | async-start | bytes 10485760 | tf_op jit(solution)/shard_map/all_gather | solution.py:65
  1098.6 165.6 %all-gather.55.cloned.1.call-start = ((), (), s32[]{:S(2)}) async-start(), calls=%async_computation.12 | async-start | bytes 10485760 | tf_op jit(solution)/shard_map/all_gather | solution.py:66
  1099.4 392.1 %all-gather.61.cloned.1.call-start = ((), (), s32[]{:S(2)}) async-start(), calls=%async_computation.15 | async-start | bytes 10485760 | tf_op jit(solution)/shard_map/all_gather | solution.py:65
  1409.5 165.5 %all-gather.59.cloned.1.call-start = ((), (), s32[]{:S(2)}) async-start(), calls=%async_computation.14 | async-start | bytes 10485760 | tf_op jit(solution)/shard_map/all_gather | solution.py:66
  1410.1 392.2 %all-gather.65.cloned.1.call-start = ((), (), s32[]{:S(2)}) async-start(), calls=%async_computation.17 | async-start | bytes 10485760 | tf_op jit(solution)/shard_map/all_gather | solution.py:65
  1720.2 165.5 %all-gather.63.cloned.1.call-start = ((), (), s32[]{:S(2)}) async-start(), calls=%async_computation.16 | async-start | bytes 10485760 | tf_op jit(solution)/shard_map/all_gather | solution.py:66
  1720.8 392.2 %all-gather.69.cloned.1.call-start = ((), (), s32[]{:S(2)}) async-start(), calls=%async_computation.19 | async-start | bytes 10485760 | tf_op jit(solution)/shard_map/all_gather | solution.py:65
  2031.1 395.8 %all-gather.67.cloned.1.call-start = ((), (), s32[]{:S(2)}) async-start(), calls=%async_computation.18 | async-start | bytes 10485760 | tf_op jit(solution)/shard_map/all_gather | solution.py:66
  2031.9 702.9 %all-gather.105.cloned.1.call-start = ((), (), s32[]{:S(2)}) async-start(), calls=%async_computation.47 | async-start | bytes 10485760 | tf_op jit(solution)/shard_map/all_gather | solution.py:54
  2032.6 760.9 %all-gather.109.cloned.1.call-start = ((), (), s32[]{:S(2)}) async-start(), calls=%async_computation.49 | async-start | bytes 10485760 | tf_op jit(solution)/shard_map/all_gather | solution.py:55
  2033.2 886.0 %reduce-scatter.21.cloned.1.call-start = ((), (), s32[]{:S(2)}) async-start(), calls=%async_computation.25 | async-start | bytes 18874368 | tf_op jit(solution)/shard_map/reduce_scatter | solution.py:69
  2210.2 712.1 %reduce-scatter.23.cloned.1.call-start = ((), (), s32[]{:S(2)}) async-start(), calls=%async_computation.26 | async-start | bytes 18874368 | tf_op jit(solution)/shard_map/reduce_scatter | solution.py:69
  2263.9 661.6 %reduce-scatter.25.cloned.1.call-start = ((), (), s32[]{:S(2)}) async-start(), calls=%async_computation.27 | async-start | bytes 18874368 | tf_op jit(solution)/shard_map/reduce_scatter | solution.py:69
  2317.8 610.8 %reduce-scatter.27.cloned.1.call-start = ((), (), s32[]{:S(2)}) async-start(), calls=%async_computation.28 | async-start | bytes 18874368 | tf_op jit(solution)/shard_map/reduce_scatter | solution.py:69
  2371.5 560.3 %reduce-scatter.29.cloned.1.call-start = ((), (), s32[]{:S(2)}) async-start(), calls=%async_computation.29 | async-start | bytes 18874368 | tf_op jit(solution)/shard_map/reduce_scatter | solution.py:69
  2426.8 599.5 %reduce-scatter.11.cloned.1.call-start = ((), (), s32[]{:S(2)}) async-start(), calls=%async_computation.20 | async-start | bytes 18874368 | tf_op jit(solution)/shard_map/reduce_scatter | solution.py:68
  2558.4 578.3 %reduce-scatter.13.cloned.1.call-start = ((), (), s32[]{:S(2)}) async-start(), calls=%async_computation.21 | async-start | bytes 18874368 | tf_op jit(solution)/shard_map/reduce_scatter | solution.py:68
  2602.4 644.8 %reduce-scatter.15.cloned.1.call-start = ((), (), s32[]{:S(2)}) async-start(), calls=%async_computation.22 | async-start | bytes 18874368 | tf_op jit(solution)/shard_map/reduce_scatter | solution.py:68
  2646.4 711.0 %reduce-scatter.17.cloned.1.call-start = ((), (), s32[]{:S(2)}) async-start(), calls=%async_computation.23 | async-start | bytes 18874368 | tf_op jit(solution)/shard_map/reduce_scatter | solution.py:68
  2690.5 777.5 %reduce-scatter.19.cloned.1.call-start = ((), (), s32[]{:S(2)}) async-start(), calls=%async_computation.24 | async-start | bytes 18874368 | tf_op jit(solution)/shard_map/reduce_scatter | solution.py:68
  (27 other events, 1691.7 us)
Sparse Core Ops, SparseCore 0:
  12.2 10.6 all-gather.70
  25.0 8.9 all-gather.74
  121.3 82.9 all-gather.72
  205.9 81.8 all-gather.76
  289.6 81.8 all-gather.80
  373.1 81.8 all-gather.84
  456.5 81.8 all-gather.88
  540.0 81.8 all-gather.92
  623.5 81.8 all-gather.96
  707.0 81.8 all-gather.100
  790.6 81.8 all-gather.52
  874.1 81.8 all-gather.50
  1098.7 81.8 all-gather.56
  1182.4 81.8 all-gather.54
  1409.6 81.8 all-gather.60
  1493.1 81.8 all-gather.58
  1720.4 81.8 all-gather.64
  1803.9 81.8 all-gather.62
  2031.2 81.8 all-gather.68
  2114.9 81.8 all-gather.66
  2198.5 81.8 all-gather.104
  2282.0 81.8 all-gather.108
  2367.3 106.9 reduce-scatter.20
  2477.8 106.9 reduce-scatter.22
  2588.1 106.9 reduce-scatter.24
  2698.6 106.9 reduce-scatter.26
  2809.1 106.9 reduce-scatter.28
  2919.4 106.9 reduce-scatter.10
  3029.7 106.9 reduce-scatter.12
  3140.2 106.9 reduce-scatter.14
  3250.5 106.9 reduce-scatter.16
  3361.0 106.9 reduce-scatter.18
  (8 shorter events, 71.5 us)
where the time goes:
time: 3480 us
  matrix products  1870 us (54%)
  waiting for transfers between devices  1430 us (41%)
  local copies, waits for them, and re-layouts  91.4 us (3%)
  other arithmetic  72.7 us (2%)
    all_gather x10, waiting for transfers between devices, device_step(): full_in = lax.all_gather(sub_in, 'local', axis=0, tiled=True)  541 us
    reduce_scatter x5, waiting for transfers between devices, device_step(): lax.psum_scatter(part_in, ('local', 'data'), scatter_dimension=0, tiled=T...  521 us
    dot_general x5, matrix products, layer_backward(): lax.dot_general(grad_rows, w_out, LAST_LAST, preferred_element_type=jnp.f...  437 us
    dot_general x5, matrix products, layer_forward(): jnp.dot(unit_rows, w_in, preferred_element_type=jnp.float32)  293 us
    dot_general x5, matrix products, layer_backward(): lax.dot_general(hidden, grad_rows, FIRST_FIRST, preferred_element_type=jn...  270 us
    all_gather x10, waiting for transfers between devices, device_step(): full_out = lax.all_gather(sub_out, 'local', axis=0, tiled=True)  260 us
    dot_general x5, matrix products, layer_backward(): lax.dot_general(grad_pre, w_in, LAST_LAST, preferred_element_type=jnp.flo...  222 us
    dot_general x5, matrix products, layer_backward(): jnp.dot(unit_rows, w_in, preferred_element_type=jnp.float32)  217 us
  transfers between devices with their start and end apart: 40, of which 32 were waited for; matrix products, arithmetic and copies ran while one was open for 42% of the time, Pallas kernels for 0%

commit v1 on v0

v1 whole, which is shorter than its diff:
```python
import functools

import jax
import jax.numpy as jnp
from jax import lax
from jax.experimental import pallas as pl
from jax.experimental.pallas import tpu as pltpu
from jax.sharding import PartitionSpec as P

NORM_EPS = 1e-6
GELU_A = 0.7978845608028654
GELU_B = GELU_A * 0.044715
LAST_LAST = (((1,), (1,)), ((), ()))
FIRST_FIRST = (((0,), (0,)), ((), ()))
BF16 = jnp.bfloat16
F32 = jnp.float32

CHIPS = 4
SHARDS = 8
LANES = 128
TOK_TILE = 256
CHUNK = 256
VMEM_LIMIT = 60 * 1024 * 1024


def unit_rows_of(x_tile):
    x_wide = x_tile.astype(F32)
    inv_rms = lax.rsqrt(jnp.mean(x_wide * x_wide, axis=-1, keepdims=True) + NORM_EPS)
    return x_wide, inv_rms


def lane_join(ref, first, count, rows=None):
    if rows is None:
        return jnp.concatenate([ref[first + b] for b in range(count)], axis=1)
    return jnp.concatenate([ref[first + b, rows, :] for b in range(count)], axis=1)


def weight_copies(order_ref, w_in_pieces, w_out_pieces, w_in_buf, w_out_buf, sem):
    hidden_blocks = w_in_buf.shape[0] // SHARDS
    depth = w_in_buf.shape[1] // SHARDS
    width = w_out_buf.shape[1] // SHARDS
    groups = []
    for p in range(SHARDS):
        block = order_ref[1, p] * hidden_blocks
        copies = []
        for q, (ref, at) in enumerate(w_in_pieces):
            row = pl.multiple_of(order_ref[0, q] * depth, depth)
            copies.append(
                pltpu.make_async_copy(
                    ref.at[at, pl.ds(block, hidden_blocks)],
                    w_in_buf.at[pl.ds(p * hidden_blocks, hidden_blocks), pl.ds(row, depth)],
                    sem.at[p],
                )
            )
        ref, at = w_out_pieces[p]
        copies.append(pltpu.make_async_copy(ref.at[at], w_out_buf.at[:, pl.ds(p * width, width)], sem.at[p]))
        groups.append(copies)
    return groups


def with_weights(order_ref, w_in_pieces, w_out_pieces, w_in_buf, w_out_buf, sem, body):
    step = pl.program_id(0)

    @pl.when(step == 0)
    def _():
        groups = weight_copies(order_ref, w_in_pieces, w_out_pieces, w_in_buf, w_out_buf, sem)
        for copies in groups:
            for copy in copies:
                copy.start()

        def wait(p):
            for copy in groups[p]:
                copy.wait()

        body(wait)

    @pl.when(step > 0)
    def _():
        body(lambda p: None)


def forward_kernel(pieces, order_ref, x_ref, *refs):
    n_in, n_out = len(pieces[0]), len(pieces[1])
    w_in_refs, w_out_refs = refs[:n_in], refs[n_in : n_in + n_out]
    y_ref, w_in_buf, w_out_buf, sem = refs[n_in + n_out :]
    w_in_pieces = [(w_in_refs[a], i) for a, i in piece_list(pieces[0])]
    w_out_pieces = [(w_out_refs[a], i) for a, i in piece_list(pieces[1])]
    hidden_size = w_out_buf.shape[1]
    per_group = hidden_size // SHARDS // CHUNK
    blocks = CHUNK // LANES
    d_blocks = w_out_buf.shape[0]

    def body(wait):
        x_wide, inv_rms = unit_rows_of(x_ref[...])
        unit = (x_wide * inv_rms).astype(BF16)
        total = None
        pending = []

        def finish(total):
            chunk, hidden = pending.pop(0)
            w_out = lane_join(w_out_buf, 0, d_blocks, pl.ds(chunk * CHUNK, CHUNK))
            part = jnp.dot(hidden, w_out, preferred_element_type=F32)
            return part if total is None else total + part

        for chunk in range(hidden_size // CHUNK):
            if chunk % per_group == 0:
                wait(chunk // per_group)
            w_in = lane_join(w_in_buf, chunk * blocks, blocks)
            pre = jnp.dot(unit, w_in, preferred_element_type=F32).astype(BF16).astype(F32)
            tanh = jnp.tanh(pre * (GELU_A + GELU_B * (pre * pre)))
            pending.append((chunk, (pre * (0.5 * tanh + 0.5)).astype(BF16)))
            if len(pending) > 2:
                total = finish(total)
        while pending:
            total = finish(total)
        y_ref[...] = (x_ref[...].astype(F32) + total).astype(BF16)

    with_weights(order_ref, w_in_pieces, w_out_pieces, w_in_buf, w_out_buf, sem, body)


def backward_kernel(pieces, order_ref, x_ref, dy_ref, *refs):
    n_in, n_out = len(pieces[0]), len(pieces[1])
    w_in_refs, w_out_refs = refs[:n_in], refs[n_in : n_in + n_out]
    unit_ref, hidden_ref, dpre_ref, dx_ref, w_in_buf, w_out_buf, sem = refs[n_in + n_out :]
    w_in_pieces = [(w_in_refs[a], i) for a, i in piece_list(pieces[0])]
    w_out_pieces = [(w_out_refs[a], i) for a, i in piece_list(pieces[1])]
    hidden_size = w_out_buf.shape[1]
    per_group = hidden_size // SHARDS // CHUNK
    blocks = CHUNK // LANES
    d_blocks = w_out_buf.shape[0]

    def body(wait):
        x_wide, inv_rms = unit_rows_of(x_ref[...])
        unit = (x_wide * inv_rms).astype(BF16)
        for b in range(d_blocks):
            unit_ref[b] = unit[:, b * LANES : (b + 1) * LANES]
        dy = dy_ref[...]
        total = None
        pending = []

        def finish(total):
            chunk, dpre = pending.pop(0)
            part = lax.dot_general(dpre, lane_join(w_in_buf, chunk * blocks, blocks), LAST_LAST, preferred_element_type=F32)
            return part if total is None else total + part

        for chunk in range(hidden_size // CHUNK):
            group = chunk // per_group
            if chunk % per_group == 0:
                wait(group)
            w_in = lane_join(w_in_buf, chunk * blocks, blocks)
            w_out = lane_join(w_out_buf, 0, d_blocks, pl.ds(chunk * CHUNK, CHUNK))
            pre = jnp.dot(unit, w_in, preferred_element_type=F32).astype(BF16).astype(F32)
            dhidden = lax.dot_general(dy, w_out, LAST_LAST, preferred_element_type=F32)
            poly = GELU_A + GELU_B * (pre * pre)
            cdf = 0.5 * jnp.tanh(pre * poly) + 0.5
            hidden = pre * cdf
            slope = cdf + (hidden * (6.0 * poly - 4.0 * GELU_A)) * (1.0 - cdf)
            hidden = hidden.astype(BF16)
            dpre = (slope * dhidden).astype(BF16)
            first = order_ref[1, group] * (per_group * blocks) + chunk % per_group * blocks
            for b in range(blocks):
                hidden_ref[first + b] = hidden[:, b * LANES : (b + 1) * LANES]
                dpre_ref[first + b] = dpre[:, b * LANES : (b + 1) * LANES]
            pending.append((chunk, dpre))
            if len(pending) > 2:
                total = finish(total)
        while pending:
            total = finish(total)
        value = x_ref[...].astype(F32) * inv_rms
        row_mean = jnp.mean(total * value, axis=-1, keepdims=True)
        dx_ref[...] = (dy_ref[...].astype(F32) + inv_rms * (total - value * row_mean)).astype(BF16)

    with_weights(order_ref, w_in_pieces, w_out_pieces, w_in_buf, w_out_buf, sem, body)


def piece_list(arrays):
    return [(a, i) for a, i in arrays.order]


class Pieces:
    def __init__(self, arrays, order):
        self.arrays, self.order = arrays, order

    def __len__(self):
        return len(self.arrays)


def layer_call(kernel, name, order, rows, w_in, w_out, outs, flops):
    tokens, width = rows[0].shape
    hidden_size = w_out.arrays[0].shape[2] * SHARDS
    blocks_d, blocks_f = width // LANES, hidden_size // LANES
    row_spec = pl.BlockSpec((TOK_TILE, width), lambda i, order: (i, 0))
    shapes, specs = [], []
    for kind in outs:
        if kind == "rows":
            shapes.append(jax.ShapeDtypeStruct((tokens, width), BF16))
            specs.append(row_spec)
        else:
            shapes.append(jax.ShapeDtypeStruct((kind // LANES, tokens, LANES), BF16))
            specs.append(pl.BlockSpec((kind // LANES, TOK_TILE, LANES), lambda i, order: (0, i, 0)))
    n_weights = len(w_in) + len(w_out)
    moved = 2 * (2 * width * hidden_size + tokens * width * len(rows) + sum(s.size for s in shapes))
    return pl.pallas_call(
        functools.partial(kernel, (w_in, w_out)),
        grid_spec=pltpu.PrefetchScalarGridSpec(
            num_scalar_prefetch=1,
            grid=(tokens // TOK_TILE,),
            in_specs=[row_spec] * len(rows) + [pl.BlockSpec(memory_space=pl.ANY)] * n_weights,
            out_specs=specs,
            scratch_shapes=[
                pltpu.VMEM((blocks_f, width, LANES), BF16),
                pltpu.VMEM((blocks_d, hidden_size, LANES), BF16),
                pltpu.SemaphoreType.DMA((SHARDS,)),
            ],
        ),
        out_shape=shapes,
        compiler_params=pltpu.CompilerParams(vmem_limit_bytes=VMEM_LIMIT),
        cost_estimate=pl.CostEstimate(flops=flops * 2 * tokens * width * hidden_size, bytes_accessed=moved, transcendentals=0),
        name=name,
    )(order, *rows, *w_in.arrays, *w_out.arrays)


def weight_grad_kernel(dy_lanes, half_ref, left_ref, right_ref, *refs):
    out_ref = refs[-1]
    left = lane_join(left_ref, 0, left_ref.shape[0])
    right = right_ref[...] if not dy_lanes else lane_join(right_ref, 0, right_ref.shape[0])
    total = lax.dot_general(left, right, FIRST_FIRST, preferred_element_type=F32)
    if len(refs) == 2:
        total = total + refs[0][...]
    out_ref[...] = total


def grad_w_out_half(half, hidden, dy, arrived):
    blocks_f, tokens, _ = hidden.shape
    width = dy.shape[1]
    per_shard = blocks_f // SHARDS
    hidden = hidden.reshape(CHIPS, 2, per_shard, tokens, LANES)
    out_spec = pl.BlockSpec((per_shard * LANES, width), lambda i, half: (i, 0))
    extra = [] if arrived is None else [arrived]
    return pl.pallas_call(
        functools.partial(weight_grad_kernel, False),
        grid_spec=pltpu.PrefetchScalarGridSpec(
            num_scalar_prefetch=1,
            grid=(CHIPS,),
            in_specs=[
                pl.BlockSpec((None, None, per_shard, tokens, LANES), lambda i, half: (i, half[0], 0, 0, 0)),
                pl.BlockSpec((tokens, width), lambda i, half: (0, 0), pipeline_mode=pl.Buffered(1)),
            ]
            + [out_spec] * len(extra),
            out_specs=out_spec,
        ),
        out_shape=jax.ShapeDtypeStruct((CHIPS * per_shard * LANES, width), F32),
        compiler_params=pltpu.CompilerParams(vmem_limit_bytes=VMEM_LIMIT),
        cost_estimate=pl.CostEstimate(
            flops=2 * tokens * width * CHIPS * per_shard * LANES,
            bytes_accessed=tokens * (blocks_f * LANES + 2 * width) + 2 * blocks_f * LANES * width * (1 + len(extra)),
            transcendentals=0,
        ),
        name="grad_w_out_half",
    )(half, hidden, dy, *extra)


def grad_w_in_half(half, unit, dpre, arrived):
    blocks_d, tokens, _ = unit.shape
    blocks_f = dpre.shape[0]
    per_shard = blocks_d // SHARDS
    step = 4
    unit = unit.reshape(CHIPS, 2, tokens, LANES)
    rows = CHIPS * per_shard * LANES
    out_spec = pl.BlockSpec((rows, step * LANES), lambda i, half: (0, i))
    extra = [] if arrived is None else [arrived]
    return pl.pallas_call(
        functools.partial(weight_grad_kernel, True),
        grid_spec=pltpu.PrefetchScalarGridSpec(
            num_scalar_prefetch=1,
            grid=(blocks_f // step,),
            in_specs=[
                pl.BlockSpec((CHIPS, None, tokens, LANES), lambda i, half: (0, half[0], 0, 0), pipeline_mode=pl.Buffered(1)),
                pl.BlockSpec((step, tokens, LANES), lambda i, half: (i, 0, 0)),
            ]
            + [out_spec] * len(extra),
            out_specs=out_spec,
        ),
        out_shape=jax.ShapeDtypeStruct((rows, blocks_f * LANES), F32),
        compiler_params=pltpu.CompilerParams(vmem_limit_bytes=VMEM_LIMIT),
        cost_estimate=pl.CostEstimate(
            flops=2 * tokens * rows * blocks_f * LANES,
            bytes_accessed=2 * tokens * (blocks_f * LANES + rows) + 4 * blocks_f * LANES * rows * (1 + len(extra)),
            transcendentals=0,
        ),
        name="grad_w_in_half",
    )(half, unit, dpre, *extra)


def to_lanes(w):
    rows, columns = w.shape
    return w.reshape(rows, columns // LANES, LANES).transpose(1, 0, 2)


def solution(mesh):
    row_spec = P(("local", "data"), None)
    weight_spec = P(None, ("local", "data"), None)
    swap_cores = [(0, 1), (1, 0)]
    swap_x = [(i, i ^ 1) for i in range(CHIPS)]
    swap_y = [(i, i ^ 2) for i in range(CHIPS)]

    def device_step(x_rows, grad_rows, w_in_part, w_out_part):
        layers = w_in_part.shape[0]
        core = lax.axis_index("data").astype(jnp.int32)
        chip = lax.axis_index("local").astype(jnp.int32)
        chip_x, chip_y = chip % 2, chip // 2
        mine, other = jnp.reshape(core, (1,)), jnp.reshape(1 - core, (1,))

        seq = [2 * (i // 2) + (core if i % 2 == 0 else 1 - core) for i in range(SHARDS)]
        order_fwd = jnp.stack([jnp.stack(seq), jnp.stack(seq)]).astype(jnp.int32)
        fwd_list = [(i % 2, i // 2) for i in range(SHARDS)]
        bwd_list = [(0, 0), (0, 1), (2, 0), (2, 1), (1, 0), (1, 1), (3, 0), (3, 1)]
        in_chips = [2 * chip_y, 2 * chip_y + 1, 2 - 2 * chip_y, 3 - 2 * chip_y]
        out_chips = [chip_x, chip_x + 2, 1 - chip_x, 3 - chip_x]

        def bwd_seq(chips):
            kept, got = chips[:2], chips[2:]
            return jnp.stack(
                [2 * c + core for c in kept] + [2 * c + 1 - core for c in kept] + [2 * c + core for c in got] + [2 * c + 1 - core for c in got]
            )

        order_bwd = jnp.stack([bwd_seq(in_chips), bwd_seq(out_chips)]).astype(jnp.int32)

        saved_x, kept_in, kept_out = [], [], []
        x_cur = x_rows
        for n in range(layers):
            half_in = lax.all_gather(to_lanes(w_in_part[n]), "local")
            half_out = lax.all_gather(to_lanes(w_out_part[n]), "local")
            twin_in = lax.ppermute(half_in, "data", swap_cores)
            twin_out = lax.ppermute(half_out, "data", swap_cores)
            saved_x.append(x_cur)
            keep_in = lax.dynamic_slice_in_dim(half_in, 2 * chip_y, 2, 0)
            pair_out = half_out.reshape((2, 2) + half_out.shape[1:])
            keep_out = lax.dynamic_slice_in_dim(pair_out, chip_x, 1, 1)[:, 0]
            (x_next,) = layer_call(
                forward_kernel, "layer_forward", order_fwd, [x_cur], Pieces([half_in, twin_in], fwd_list), Pieces([half_out, twin_out], fwd_list), ["rows"], 2
            )
            x_cur, keep_in, keep_out = lax.optimization_barrier((x_next, keep_in, keep_out))
            kept_in.append(keep_in)
            kept_out.append(keep_out)

        grad_cur = grad_rows
        grads_in, grads_out = [], []
        for n in reversed(range(layers)):
            keep_in, keep_out, grad_here = lax.optimization_barrier((kept_in[n], kept_out[n], grad_cur))
            got_in = lax.ppermute(keep_in, "local", swap_y)
            got_out = lax.ppermute(keep_out, "local", swap_x)
            twin_in = lax.ppermute(keep_in, "data", swap_cores)
            twin_out = lax.ppermute(keep_out, "data", swap_cores)
            twin_got_in = lax.ppermute(got_in, "data", swap_cores)
            twin_got_out = lax.ppermute(got_out, "data", swap_cores)
            if grads_in:
                grad_here, grads_in[-1], grads_out[-1] = lax.optimization_barrier((grad_here, grads_in[-1], grads_out[-1]))
                reduce(grads_in, grads_out)
            unit, hidden, dpre, grad_cur = layer_call(
                backward_kernel,
                "layer_backward",
                order_bwd,
                [saved_x[n], grad_here],
                Pieces([keep_in, got_in, twin_in, twin_got_in], bwd_list),
                Pieces([keep_out, got_out, twin_out, twin_got_out], bwd_list),
                [x_rows.shape[1], w_out_part.shape[1] * SHARDS, w_out_part.shape[1] * SHARDS, "rows"],
                3,
            )
            out_there = grad_w_out_half(other, hidden, grad_here, None)
            out_arrived = lax.ppermute(out_there, "data", swap_cores)
            in_there = grad_w_in_half(other, unit, dpre, None)
            in_arrived = lax.ppermute(in_there, "data", swap_cores)
            grads_out.append(grad_w_out_half(mine, hidden, grad_here, out_arrived))
            grads_in.append(grad_w_in_half(mine, unit, dpre, in_arrived))
        reduce(grads_in, grads_out)
        return x_cur, jnp.stack(grads_in[::-1]), jnp.stack(grads_out[::-1]), grad_cur

    def reduce(grads_in, grads_out):
        grads_out[-1] = lax.psum_scatter(grads_out[-1], "local", scatter_dimension=0, tiled=True)
        grads_in[-1] = lax.psum_scatter(grads_in[-1], "local", scatter_dimension=0, tiled=True)

    return jax.shard_map(
        device_step,
        mesh=mesh,
        in_specs=(row_spec, row_spec, weight_spec, weight_spec),
        out_specs=(row_spec, weight_spec, weight_spec, row_spec),
        check_vma=False,
    )
```

time: 3480 us -> 3070 us (0.88)
  matrix products: 1870 us -> 0 us
  Pallas kernels: 0 us -> 1490 us
  other arithmetic: 72.7 us -> 1.15 us
    dot_general x35 -> x0, matrix products: 1870 us -> none  [the longest x5 437 us: layer_backward(): lax.dot_general(grad_rows, w_out, LAST_LAST, preferred_element_type=jnp.f...]
    pallas_call x0 -> x30, Pallas kernels: none -> 1490 us  [the longest x10 1000 us: layer_call(): pl.pallas_call(functools.partial(kernel, (w_in, w_out)), grid_spec=pltpu....]
    all_gather x30 -> x10, waiting for transfers between devices: 897 us -> 424 us  [the longest x5 229 us: device_step(): half_out = lax.all_gather(to_lanes(w_out_part[n]), 'local')]
    ppermute x0 -> x50, waiting for transfers between devices: none -> 263 us  [the longest x5 228 us: device_step(): got_in = lax.ppermute(keep_in, 'local', swap_y)]
    reduce_scatter x10, waiting for transfers between devices: 521 us -> 737 us  [the longest x5 402 us: reduce(): lax.psum_scatter(grads_in[-1], 'local', scatter_dimension=0, tiled=True)]
    convert_element_type x5 -> x0, other arithmetic: 67.5 us -> none  [layer_backward(): return (grad_x.astype(jnp.bfloat16), grad_w_in, grad_w_out)]
  transfers between devices with their start and end apart: 40 -> 70, of which waited for: 32 -> 34; matrix products, arithmetic and copies ran while one was open for 42% -> 3% of each run, Pallas kernels for 0% -> 22%
where the time goes in v1:
time: 3070 us; the launch traced here: 3060 us
  Pallas kernels  1490 us (49%)
  waiting for transfers between devices  1430 us (47%)
  local copies, waits for them, and re-layouts  103 us (3%)
    pallas_call x10, Pallas kernels, layer_call(): pl.pallas_call(functools.partial(kernel, (w_in, w_out)), grid_spec=pltpu....  1000 us
    reduce_scatter x5, waiting for transfers between devices, reduce(): lax.psum_scatter(grads_in[-1], 'local', scatter_dimension=0, tiled=True)  402 us
    reduce_scatter x5, waiting for transfers between devices, reduce(): lax.psum_scatter(grads_out[-1], 'local', scatter_dimension=0, tiled=True)  334 us
    pallas_call x10, Pallas kernels, grad_w_in_half(): pl.pallas_call(functools.partial(weight_grad_kernel, True), grid_spec=plt...  248 us
    pallas_call x10, Pallas kernels, grad_w_out_half(): pl.pallas_call(functools.partial(weight_grad_kernel, False), grid_spec=pl...  244 us
    all_gather x5, waiting for transfers between devices, device_step(): half_out = lax.all_gather(to_lanes(w_out_part[n]), 'local')  229 us
    ppermute x5, waiting for transfers between devices, device_step(): got_in = lax.ppermute(keep_in, 'local', swap_y)  228 us
    all_gather x5, waiting for transfers between devices, device_step(): half_in = lax.all_gather(to_lanes(w_in_part[n]), 'local')  195 us
  transfers between devices with their start and end apart: 70, of which 34 were waited for; matrix products, arithmetic and copies ran while one was open for 3% of the time, Pallas kernels for 22%

profile of v1, /device:TPU:0, one launch (start us, length us, event | category | flops | bytes accessed | tf_op | source)
XLA Modules:
  0.0 3057.9 jit_solution(8127068879868857239)
XLA Ops:
  63.5 48.4 %all-gather.23.cloned.1.call-done = bf16[32,512,128]{2,1,0:T(8,128)(2,1)} async-done(((bf16[8,512,128]{2,1,0:T(8,128)(2,1)}), bf16[32,512,128]{2,1,0:T(8,128)(2,1)}) %all-gather.23.cloned.1.call-update) | async-done | bytes 4194320 | tf_op jit(solution)/shard_map/all_gather | solution.py:333
  112.6 48.4 %all-gather.25.cloned.1.call-done = bf16[128,128,128]{2,1,0:T(8,128)(2,1)} async-done(((bf16[32,128,128]{2,1,0:T(8,128)(2,1)}), bf16[128,128,128]{2,1,0:T(8,128)(2,1)}) %all-gather.25.cloned.1.call-update) | async-done | bytes 4194320 | tf_op jit(solution)/shard_map/all_gather | solution.py:332
  161.0 48.9 %all-gather.29.cloned.1.call-done = bf16[128,128,128]{2,1,0:T(8,128)(2,1)} async-done(((bf16[32,128,128]{2,1,0:T(8,128)(2,1)}), bf16[128,128,128]{2,1,0:T(8,128)(2,1)}) %all-gather.29.cloned.1.call-update) | async-done | bytes 4194320 | tf_op jit(solution)/shard_map/all_gather | solution.py:332
  209.9 48.3 %all-gather.33.cloned.1.call-done = bf16[128,128,128]{2,1,0:T(8,128)(2,1)} async-done(((bf16[32,128,128]{2,1,0:T(8,128)(2,1)}), bf16[128,128,128]{2,1,0:T(8,128)(2,1)}) %all-gather.33.cloned.1.call-update) | async-done | bytes 4194320 | tf_op jit(solution)/shard_map/all_gather | solution.py:332
  311.3 44.2 %all-gather.27.cloned.1.call-done = bf16[32,512,128]{2,1,0:T(8,128)(2,1)} async-done(((bf16[8,512,128]{2,1,0:T(8,128)(2,1)}), bf16[32,512,128]{2,1,0:T(8,128)(2,1)}) %all-gather.27.cloned.1.call-update) | async-done | bytes 4194320 | tf_op jit(solution)/shard_map/all_gather | solution.py:333
  358.7 45.3 %all-gather.31.cloned.1.call-done = bf16[32,512,128]{2,1,0:T(8,128)(2,1)} async-done(((bf16[8,512,128]{2,1,0:T(8,128)(2,1)}), bf16[32,512,128]{2,1,0:T(8,128)(2,1)}) %all-gather.31.cloned.1.call-update) | async-done | bytes 4194320 | tf_op jit(solution)/shard_map/all_gather | solution.py:333
  407.1 45.9 %all-gather.35.cloned.1.call-done = bf16[32,512,128]{2,1,0:T(8,128)(2,1)} async-done(((bf16[8,512,128]{2,1,0:T(8,128)(2,1)}), bf16[32,512,128]{2,1,0:T(8,128)(2,1)}) %all-gather.35.cloned.1.call-update) | async-done | bytes 4194320 | tf_op jit(solution)/shard_map/all_gather | solution.py:333
  456.1 45.2 %all-gather.39.cloned.1.call-done = bf16[32,512,128]{2,1,0:T(8,128)(2,1)} async-done(((bf16[8,512,128]{2,1,0:T(8,128)(2,1)}), bf16[32,512,128]{2,1,0:T(8,128)(2,1)}) %all-gather.39.cloned.1.call-update) | async-done | bytes 4194320 | tf_op jit(solution)/shard_map/all_gather | solution.py:333
  505.1 79.1 %layer_forward.5.x_ref = bf16[4096,1024]{1,0:T(8,128)(2,1)} custom-call(s32[2,8]{1,0:T(2,128)} %pad_add_fusion.order_ref, bf16[4096,1024]{1,0:T(8,128)(2,1)} %x_ref.3, bf16[4,32,128,128]{3,2,1,0:T(8,128)(2,1)} %bitcast.124, bf16[4,32,128,128]{3,2,1,0:T(8,128)(2,1)} %collective-permute-done.refs_1_, bf16[4,8,512,128]{3,2,1,0:T(8,128)(2,1)} %bitcast.135, ...), custom_call_target="tpu_custom_call" | custom-call | flops 68719476736 | bytes 33554432 | tf_op jit(solution)/shard_map/layer_forward/pallas_call | solution.py:203
  584.8 79.4 %layer_forward.6.x_ref = bf16[4096,1024]{1,0:T(8,128)(2,1)} custom-call(s32[2,8]{1,0:T(2,128)} %pad_add_fusion.order_ref, bf16[4096,1024]{1,0:T(8,128)(2,1)} %layer_forward.5.x_ref, bf16[4,32,128,128]{3,2,1,0:T(8,128)(2,1)} %bitcast.129, bf16[4,32,128,128]{3,2,1,0:T(8,128)(2,1)} %collective-permute-done.2.refs_1_, bf16[4,8,512,128]{3,2,1,0:T(8,128)(2,1)} %bitcast.22.refs_2_, ...), custom_call_target="tpu_custom_call" | custom-call | flops 68719476736 | bytes 33554432 | tf_op jit(solution)/shard_map/layer_forward/pallas_call | solution.py:203
  664.3 79.6 %layer_forward.7.x_ref = bf16[4096,1024]{1,0:T(8,128)(2,1)} custom-call(s32[2,8]{1,0:T(2,128)} %pad_add_fusion.order_ref, bf16[4096,1024]{1,0:T(8,128)(2,1)} %layer_forward.6.x_ref, bf16[4,32,128,128]{3,2,1,0:T(8,128)(2,1)} %bitcast.126, bf16[4,32,128,128]{3,2,1,0:T(8,128)(2,1)} %collective-permute-done.4.refs_1_, bf16[4,8,512,128]{3,2,1,0:T(8,128)(2,1)} %bitcast.139, ...), custom_call_target="tpu_custom_call" | custom-call | flops 68719476736 | bytes 33554432 | tf_op jit(solution)/shard_map/layer_forward/pallas_call | solution.py:203
  743.9 79.3 %layer_forward.8.x_ref = bf16[4096,1024]{1,0:T(8,128)(2,1)} custom-call(s32[2,8]{1,0:T(2,128)} %pad_add_fusion.order_ref, bf16[4096,1024]{1,0:T(8,128)(2,1)} %layer_forward.7.x_ref, bf16[4,32,128,128]{3,2,1,0:T(8,128)(2,1)} %bitcast.132, bf16[4,32,128,128]{3,2,1,0:T(8,128)(2,1)} %collective-permute-done.6.refs_1_, bf16[4,8,512,128]{3,2,1,0:T(8,128)(2,1)} %bitcast.142, ...), custom_call_target="tpu_custom_call" | custom-call | flops 68719476736 | bytes 33554432 | tf_op jit(solution)/shard_map/layer_forward/pallas_call | solution.py:203
  823.2 79.7 %layer_forward.9 = bf16[4096,1024]{1,0:T(8,128)(2,1)} custom-call(s32[2,8]{1,0:T(2,128)} %pad_add_fusion.order_ref, bf16[4096,1024]{1,0:T(8,128)(2,1)} %layer_forward.8.x_ref, bf16[4,32,128,128]{3,2,1,0:T(8,128)(2,1)} %bitcast.43.refs_0_, bf16[4,32,128,128]{3,2,1,0:T(8,128)(2,1)} %collective-permute-done.8.refs_1_, bf16[4,8,512,128]{3,2,1,0:T(8,128)(2,1)} %bitcast.145, ...), custom_call_target="tpu_custom_call" | custom-call | flops 68719476736 | bytes 33554432 | tf_op jit(solution)/shard_map/layer_forward/pallas_call | solution.py:203
  905.5 45.5 %collective-permute-done.10.refs_1_ = bf16[2,32,128,128]{3,2,1,0:T(8,128)(2,1)} collective-permute-done((bf16[2,32,128,128]{3,2,1,0:T(8,128)(2,1)S(1)}, bf16[2,32,128,128]{3,2,1,0:T(8,128)(2,1)}, u32[]{:S(2)}, u32[]{:S(2)}) %collective-permute-start.10) | collective-permute-done | bytes 2097184 | tf_op jit(solution)/shard_map/ppermute | solution.py:351
  958.1 120.6 %layer_backward.5 = (bf16[8,4096,128]{2,1,0:T(8,128)(2,1)}, bf16[32,4096,128]{2,1,0:T(8,128)(2,1)}, bf16[32,4096,128]{2,1,0:T(8,128)(2,1)}, bf16[4096,1024]{1,0:T(8,128)(2,1)}) custom-call(s32[2,8]{1,0:T(2,128)} %pad_add_fusion.1.order_ref, bf16[4096,1024]{1,0:T(8,128)(2,1)} %layer_forward.8.x_ref, bf16[4096,1024]{1,0:T(8,128)(2,1)} %right_ref.1, ...), custom_call_target="tpu_custom_call" | custom-call | flops 103079215104 | bytes 117440512 | tf_op jit(solution)/shard_map/layer_backward/pallas_call | solution.py:203
  1129.6 45.7 %collective-permute-done.18.refs_1_ = bf16[2,32,128,128]{3,2,1,0:T(8,128)(2,1)} collective-permute-done((bf16[2,32,128,128]{3,2,1,0:T(8,128)(2,1)S(1)}, bf16[2,32,128,128]{3,2,1,0:T(8,128)(2,1)}, u32[]{:S(2)}, u32[]{:S(2)}) %collective-permute-start.18) | collective-permute-done | bytes 2097184 | tf_op jit(solution)/shard_map/ppermute | solution.py:351
  1227.2 120.7 %layer_backward.6 = (bf16[8,4096,128]{2,1,0:T(8,128)(2,1)}, bf16[32,4096,128]{2,1,0:T(8,128)(2,1)}, bf16[32,4096,128]{2,1,0:T(8,128)(2,1)}, bf16[4096,1024]{1,0:T(8,128)(2,1)}) custom-call(s32[2,8]{1,0:T(2,128)} %pad_add_fusion.1.order_ref, bf16[4096,1024]{1,0:T(8,128)(2,1)} %layer_forward.7.x_ref, bf16[4096,1024]{1,0:T(8,128)(2,1)} %get-tuple-element.89.dy_ref.right_ref, ...), custom_call_target="tpu_custom_call" | custom-call | flops 103079215104 | bytes 117440512 | tf_op jit(solution)/shard_map/layer_backward/pallas_call | solution.py:203
  1398.8 45.5 %collective-permute-done.26.refs_1_ = bf16[2,32,128,128]{3,2,1,0:T(8,128)(2,1)} collective-permute-done((bf16[2,32,128,128]{3,2,1,0:T(8,128)(2,1)S(1)}, bf16[2,32,128,128]{3,2,1,0:T(8,128)(2,1)}, u32[]{:S(2)}, u32[]{:S(2)}) %collective-permute-start.26) | collective-permute-done | bytes 2097184 | tf_op jit(solution)/shard_map/ppermute | solution.py:351
  1495.4 120.5 %layer_backward.7 = (bf16[8,4096,128]{2,1,0:T(8,128)(2,1)}, bf16[32,4096,128]{2,1,0:T(8,128)(2,1)}, bf16[32,4096,128]{2,1,0:T(8,128)(2,1)}, bf16[4096,1024]{1,0:T(8,128)(2,1)}) custom-call(s32[2,8]{1,0:T(2,128)} %pad_add_fusion.1.order_ref, bf16[4096,1024]{1,0:T(8,128)(2,1)} %layer_forward.6.x_ref, bf16[4096,1024]{1,0:T(8,128)(2,1)} %get-tuple-element.97.dy_ref.right_ref, ...), custom_call_target="tpu_custom_call" | custom-call | flops 103079215104 | bytes 117440512 | tf_op jit(solution)/shard_map/layer_backward/pallas_call | solution.py:203
  1666.8 45.5 %collective-permute-done.34.refs_1_ = bf16[2,32,128,128]{3,2,1,0:T(8,128)(2,1)} collective-permute-done((bf16[2,32,128,128]{3,2,1,0:T(8,128)(2,1)S(1)}, bf16[2,32,128,128]{3,2,1,0:T(8,128)(2,1)}, u32[]{:S(2)}, u32[]{:S(2)}) %collective-permute-start.34) | collective-permute-done | bytes 2097184 | tf_op jit(solution)/shard_map/ppermute | solution.py:351
  1763.9 120.7 %layer_backward.8 = (bf16[8,4096,128]{2,1,0:T(8,128)(2,1)}, bf16[32,4096,128]{2,1,0:T(8,128)(2,1)}, bf16[32,4096,128]{2,1,0:T(8,128)(2,1)}, bf16[4096,1024]{1,0:T(8,128)(2,1)}) custom-call(s32[2,8]{1,0:T(2,128)} %pad_add_fusion.1.order_ref, bf16[4096,1024]{1,0:T(8,128)(2,1)} %layer_forward.5.x_ref, bf16[4096,1024]{1,0:T(8,128)(2,1)} %get-tuple-element.105.dy_ref.right_ref, ...), custom_call_target="tpu_custom_call" | custom-call | flops 103079215104 | bytes 117440512 | tf_op jit(solution)/shard_map/layer_backward/pallas_call | solution.py:203
  1935.5 45.5 %collective-permute-done.42.refs_1_ = bf16[2,32,128,128]{3,2,1,0:T(8,128)(2,1)} collective-permute-done((bf16[2,32,128,128]{3,2,1,0:T(8,128)(2,1)S(1)}, bf16[2,32,128,128]{3,2,1,0:T(8,128)(2,1)}, u32[]{:S(2)}, u32[]{:S(2)}) %collective-permute-start.42) | collective-permute-done | bytes 2097184 | tf_op jit(solution)/shard_map/ppermute | solution.py:351
  2032.2 120.6 %layer_backward.9 = (bf16[8,4096,128]{2,1,0:T(8,128)(2,1)}, bf16[32,4096,128]{2,1,0:T(8,128)(2,1)}, bf16[32,4096,128]{2,1,0:T(8,128)(2,1)}, bf16[4096,1024]{1,0:T(8,128)(2,1)}) custom-call(s32[2,8]{1,0:T(2,128)} %pad_add_fusion.1.order_ref, bf16[4096,1024]{1,0:T(8,128)(2,1)} %x_ref.3, bf16[4096,1024]{1,0:T(8,128)(2,1)} %get-tuple-element.113.dy_ref.right_ref, ...), custom_call_target="tpu_custom_call" | custom-call | flops 103079215104 | bytes 117440512 | tf_op jit(solution)/shard_map/layer_backward/pallas_call | solution.py:203
  2298.9 80.3 %reduce-scatter.23.cloned.1.call-done = f32[512,1024]{1,0:T(8,128)} async-done(((f32[2048,1024]{1,0:T(8,128)}), f32[512,1024]{1,0:T(8,128)}) %reduce-scatter.23.cloned.1.call-update) | async-done | bytes 2097168 | tf_op jit(solution)/shard_map/reduce_scatter | solution.py:380
  2382.3 80.4 %reduce-scatter.25.cloned.1.call-done = f32[512,1024]{1,0:T(8,128)} async-done(((f32[2048,1024]{1,0:T(8,128)}), f32[512,1024]{1,0:T(8,128)}) %reduce-scatter.25.cloned.1.call-update) | async-done | bytes 2097168 | tf_op jit(solution)/shard_map/reduce_scatter | solution.py:380
  2465.9 80.3 %reduce-scatter.27.cloned.1.call-done = f32[512,1024]{1,0:T(8,128)} async-done(((f32[2048,1024]{1,0:T(8,128)}), f32[512,1024]{1,0:T(8,128)}) %reduce-scatter.27.cloned.1.call-update) | async-done | bytes 2097168 | tf_op jit(solution)/shard_map/reduce_scatter | solution.py:380
  2549.3 80.8 %reduce-scatter.11.cloned.1.call-done = f32[128,4096]{1,0:T(8,128)} async-done(((f32[512,4096]{1,0:T(8,128)}), f32[128,4096]{1,0:T(8,128)}) %reduce-scatter.11.cloned.1.call-update) | async-done | bytes 2097168 | tf_op jit(solution)/shard_map/reduce_scatter | solution.py:381
  2633.3 80.3 %reduce-scatter.13.cloned.1.call-done = f32[128,4096]{1,0:T(8,128)} async-done(((f32[512,4096]{1,0:T(8,128)}), f32[128,4096]{1,0:T(8,128)}) %reduce-scatter.13.cloned.1.call-update) | async-done | bytes 2097168 | tf_op jit(solution)/shard_map/reduce_scatter | solution.py:381
  2716.7 80.3 %reduce-scatter.15.cloned.1.call-done = f32[128,4096]{1,0:T(8,128)} async-done(((f32[512,4096]{1,0:T(8,128)}), f32[128,4096]{1,0:T(8,128)}) %reduce-scatter.15.cloned.1.call-update) | async-done | bytes 2097168 | tf_op jit(solution)/shard_map/reduce_scatter | solution.py:381
  2800.2 80.3 %reduce-scatter.17.cloned.1.call-done = f32[128,4096]{1,0:T(8,128)} async-done(((f32[512,4096]{1,0:T(8,128)}), f32[128,4096]{1,0:T(8,128)}) %reduce-scatter.17.cloned.1.call-update) | async-done | bytes 2097168 | tf_op jit(solution)/shard_map/reduce_scatter | solution.py:381
  2883.6 80.5 %reduce-scatter.19.cloned.1.call-done = f32[128,4096]{1,0:T(8,128)} async-done(((f32[512,4096]{1,0:T(8,128)}), f32[128,4096]{1,0:T(8,128)}) %reduce-scatter.19.cloned.1.call-update) | async-done | bytes 2097168 | tf_op jit(solution)/shard_map/reduce_scatter | solution.py:381
  2967.2 80.3 %reduce-scatter.29.cloned.1.call-done = f32[512,1024]{1,0:T(8,128)} async-done(((f32[2048,1024]{1,0:T(8,128)}), f32[512,1024]{1,0:T(8,128)}) %reduce-scatter.29.cloned.1.call-update) | async-done | bytes 2097168 | tf_op jit(solution)/shard_map/reduce_scatter | solution.py:380
  (223 shorter events, 716.7 us)
Async XLA Ops:
  13.9 98.1 %all-gather.23.cloned.1.call-start = ((), (), s32[]{:S(2)}) async-start(), calls=%async_computation.21 | async-start | bytes 5242880 | tf_op jit(solution)/shard_map/all_gather | solution.py:333
  22.9 138.1 %all-gather.25.cloned.1.call-start = ((), (), s32[]{:S(2)}) async-start(), calls=%async_computation.22 | async-start | bytes 5242880 | tf_op jit(solution)/shard_map/all_gather | solution.py:332
  27.5 182.4 %all-gather.29.cloned.1.call-start = ((), (), s32[]{:S(2)}) async-start(), calls=%async_computation.24 | async-start | bytes 5242880 | tf_op jit(solution)/shard_map/all_gather | solution.py:332
  32.1 226.1 %all-gather.33.cloned.1.call-start = ((), (), s32[]{:S(2)}) async-start(), calls=%async_computation.26 | async-start | bytes 5242880 | tf_op jit(solution)/shard_map/all_gather | solution.py:332
  36.8 269.7 %all-gather.37.cloned.1.call-start = ((), (), s32[]{:S(2)}) async-start(), calls=%async_computation.28 | async-start | bytes 5242880 | tf_op jit(solution)/shard_map/all_gather | solution.py:332
  41.4 314.1 %all-gather.27.cloned.1.call-start = ((), (), s32[]{:S(2)}) async-start(), calls=%async_computation.23 | async-start | bytes 5242880 | tf_op jit(solution)/shard_map/all_gather | solution.py:333
  46.0 358.0 %all-gather.31.cloned.1.call-start = ((), (), s32[]{:S(2)}) async-start(), calls=%async_computation.25 | async-start | bytes 5242880 | tf_op jit(solution)/shard_map/all_gather | solution.py:333
  49.7 403.4 %all-gather.35.cloned.1.call-start = ((), (), s32[]{:S(2)}) async-start(), calls=%async_computation.27 | async-start | bytes 5242880 | tf_op jit(solution)/shard_map/all_gather | solution.py:333
  51.6 449.7 %all-gather.39.cloned.1.call-start = ((), (), s32[]{:S(2)}) async-start(), calls=%async_computation.29 | async-start | bytes 5242880 | tf_op jit(solution)/shard_map/all_gather | solution.py:333
  53.6 2242.1 %reduce-scatter.21.cloned.1.call-start = ((), (), s32[]{:S(2)}) async-start(), calls=%async_computation.15 | async-start | bytes 10485760 | tf_op jit(solution)/shard_map/reduce_scatter | solution.py:380
  63.5 441.0 %collective-permute-start = (bf16[4,32,128,128]{3,2,1,0:T(8,128)(2,1)}, bf16[4,32,128,128]{3,2,1,0:T(8,128)(2,1)}, u32[]{:S(2)}, u32[]{:S(2)}) collective-permute-start(bf16[4,32,128,128]{3,2,1,0:T(8,128)(2,1)} %bitcast.122), channel_id=1, source_target_pairs={{0,1},{1,0},{2,3},{3,2},{4,5},{5,4},{6,7},{7,6}} | collective-permute-start | bytes 12582920 | tf_op jit(solution)/shard_map/ppermute | solution.py:334
  112.0 392.6 %collective-permute-start.1 = (bf16[4,8,512,128]{3,2,1,0:T(8,128)(2,1)}, bf16[4,8,512,128]{3,2,1,0:T(8,128)(2,1)}, u32[]{:S(2)}, u32[]{:S(2)}) collective-permute-start(bf16[4,8,512,128]{3,2,1,0:T(8,128)(2,1)} %bitcast.134), channel_id=1, source_target_pairs={{0,1},{1,0},{2,3},{3,2},{4,5},{5,4},{6,7},{7,6}} | collective-permute-start | bytes 12582920 | tf_op jit(solution)/shard_map/ppermute | solution.py:335
  161.0 423.2 %collective-permute-start.2 = (bf16[4,32,128,128]{3,2,1,0:T(8,128)(2,1)}, bf16[4,32,128,128]{3,2,1,0:T(8,128)(2,1)}, u32[]{:S(2)}, u32[]{:S(2)}) collective-permute-start(bf16[4,32,128,128]{3,2,1,0:T(8,128)(2,1)} %bitcast.128), channel_id=1, source_target_pairs={{0,1},{1,0},{2,3},{3,2},{4,5},{5,4},{6,7},{7,6}} | collective-permute-start | bytes 12582920 | tf_op jit(solution)/shard_map/ppermute | solution.py:334
  209.9 454.3 %collective-permute-start.4 = (bf16[4,32,128,128]{3,2,1,0:T(8,128)(2,1)}, bf16[4,32,128,128]{3,2,1,0:T(8,128)(2,1)}, u32[]{:S(2)}, u32[]{:S(2)}) collective-permute-start(bf16[4,32,128,128]{3,2,1,0:T(8,128)(2,1)} %bitcast.125), channel_id=1, source_target_pairs={{0,1},{1,0},{2,3},{3,2},{4,5},{5,4},{6,7},{7,6}} | collective-permute-start | bytes 12582920 | tf_op jit(solution)/shard_map/ppermute | solution.py:334
  258.2 485.7 %collective-permute-start.6 = (bf16[4,32,128,128]{3,2,1,0:T(8,128)(2,1)}, bf16[4,32,128,128]{3,2,1,0:T(8,128)(2,1)}, u32[]{:S(2)}, u32[]{:S(2)}) collective-permute-start(bf16[4,32,128,128]{3,2,1,0:T(8,128)(2,1)} %bitcast.131), channel_id=1, source_target_pairs={{0,1},{1,0},{2,3},{3,2},{4,5},{5,4},{6,7},{7,6}} | collective-permute-start | bytes 12582920 | tf_op jit(solution)/shard_map/ppermute | solution.py:334
  504.6 318.6 %collective-permute-start.8 = (bf16[4,32,128,128]{3,2,1,0:T(8,128)(2,1)}, bf16[4,32,128,128]{3,2,1,0:T(8,128)(2,1)}, u32[]{:S(2)}, u32[]{:S(2)}) collective-permute-start(bf16[4,32,128,128]{3,2,1,0:T(8,128)(2,1)} %bitcast.43.refs_0_), channel_id=1, source_target_pairs={{0,1},{1,0},{2,3},{3,2},{4,5},{5,4},{6,7},{7,6}} | collective-permute-start | bytes 12582920 | tf_op jit(solution)/shard_map/ppermute | solution.py:334
  584.2 80.0 %collective-permute-start.5 = (bf16[4,8,512,128]{3,2,1,0:T(8,128)(2,1)}, bf16[4,8,512,128]{3,2,1,0:T(8,128)(2,1)}, u32[]{:S(2)}, u32[]{:S(2)}) collective-permute-start(bf16[4,8,512,128]{3,2,1,0:T(8,128)(2,1)} %bitcast.138), channel_id=1, source_target_pairs={{0,1},{1,0},{2,3},{3,2},{4,5},{5,4},{6,7},{7,6}} | collective-permute-start | bytes 12582920 | tf_op jit(solution)/shard_map/ppermute | solution.py:335
  584.3 159.6 %collective-permute-start.7 = (bf16[4,8,512,128]{3,2,1,0:T(8,128)(2,1)}, bf16[4,8,512,128]{3,2,1,0:T(8,128)(2,1)}, u32[]{:S(2)}, u32[]{:S(2)}) collective-permute-start(bf16[4,8,512,128]{3,2,1,0:T(8,128)(2,1)} %bitcast.141), channel_id=1, source_target_pairs={{0,1},{1,0},{2,3},{3,2},{4,5},{5,4},{6,7},{7,6}} | collective-permute-start | bytes 12582920 | tf_op jit(solution)/shard_map/ppermute | solution.py:335
  664.2 159.0 %collective-permute-start.9 = (bf16[4,8,512,128]{3,2,1,0:T(8,128)(2,1)}, bf16[4,8,512,128]{3,2,1,0:T(8,128)(2,1)}, u32[]{:S(2)}, u32[]{:S(2)}) collective-permute-start(bf16[4,8,512,128]{3,2,1,0:T(8,128)(2,1)} %bitcast.144), channel_id=1, source_target_pairs={{0,1},{1,0},{2,3},{3,2},{4,5},{5,4},{6,7},{7,6}} | collective-permute-start | bytes 12582920 | tf_op jit(solution)/shard_map/ppermute | solution.py:335
  1129.6 97.6 %collective-permute-start.19 = (bf16[2,32,128,128]{3,2,1,0:T(8,128)(2,1)S(1)}, bf16[2,32,128,128]{3,2,1,0:T(8,128)(2,1)}, u32[]{:S(2)}, u32[]{:S(2)}) collective-permute-start(bf16[2,32,128,128]{3,2,1,0:T(8,128)(2,1)S(1)} %copy-done.3), channel_id=1, source_target_pairs={{0,1},{1,0},{2,3},{3,2},{4,5},{5,4},{6,7},{7,6}} | collective-permute-start | bytes 6291464 | tf_op jit(solution)/shard_map/ppermute | solution.py:353
  1398.8 96.6 %collective-permute-start.27 = (bf16[2,32,128,128]{3,2,1,0:T(8,128)(2,1)S(1)}, bf16[2,32,128,128]{3,2,1,0:T(8,128)(2,1)}, u32[]{:S(2)}, u32[]{:S(2)}) collective-permute-start(bf16[2,32,128,128]{3,2,1,0:T(8,128)(2,1)S(1)} %copy-done.2), channel_id=1, source_target_pairs={{0,1},{1,0},{2,3},{3,2},{4,5},{5,4},{6,7},{7,6}} | collective-permute-start | bytes 6291464 | tf_op jit(solution)/shard_map/ppermute | solution.py:353
  1666.8 97.1 %collective-permute-start.35 = (bf16[2,32,128,128]{3,2,1,0:T(8,128)(2,1)S(1)}, bf16[2,32,128,128]{3,2,1,0:T(8,128)(2,1)}, u32[]{:S(2)}, u32[]{:S(2)}) collective-permute-start(bf16[2,32,128,128]{3,2,1,0:T(8,128)(2,1)S(1)} %copy-done.1), channel_id=1, source_target_pairs={{0,1},{1,0},{2,3},{3,2},{4,5},{5,4},{6,7},{7,6}} | collective-permute-start | bytes 6291464 | tf_op jit(solution)/shard_map/ppermute | solution.py:353
  1935.5 96.7 %collective-permute-start.43 = (bf16[2,32,128,128]{3,2,1,0:T(8,128)(2,1)S(1)}, bf16[2,32,128,128]{3,2,1,0:T(8,128)(2,1)}, u32[]{:S(2)}, u32[]{:S(2)}) collective-permute-start(bf16[2,32,128,128]{3,2,1,0:T(8,128)(2,1)S(1)} %copy-done), channel_id=1, source_target_pairs={{0,1},{1,0},{2,3},{3,2},{4,5},{5,4},{6,7},{7,6}} | collective-permute-start | bytes 6291464 | tf_op jit(solution)/shard_map/ppermute | solution.py:353
  2215.0 164.2 %reduce-scatter.23.cloned.1.call-start = ((), (), s32[]{:S(2)}) async-start(), calls=%async_computation.16 | async-start | bytes 10485760 | tf_op jit(solution)/shard_map/reduce_scatter | solution.py:380
  2215.5 247.2 %reduce-scatter.25.cloned.1.call-start = ((), (), s32[]{:S(2)}) async-start(), calls=%async_computation.17 | async-start | bytes 10485760 | tf_op jit(solution)/shard_map/reduce_scatter | solution.py:380
  2216.3 329.9 %reduce-scatter.27.cloned.1.call-start = ((), (), s32[]{:S(2)}) async-start(), calls=%async_computation.18 | async-start | bytes 10485760 | tf_op jit(solution)/shard_map/reduce_scatter | solution.py:380
  2216.9 413.3 %reduce-scatter.11.cloned.1.call-start = ((), (), s32[]{:S(2)}) async-start(), calls=%async_computation.10 | async-start | bytes 10485760 | tf_op jit(solution)/shard_map/reduce_scatter | solution.py:381
  2279.5 434.1 %reduce-scatter.13.cloned.1.call-start = ((), (), s32[]{:S(2)}) async-start(), calls=%async_computation.11 | async-start | bytes 10485760 | tf_op jit(solution)/shard_map/reduce_scatter | solution.py:381
  2280.1 516.9 %reduce-scatter.15.cloned.1.call-start = ((), (), s32[]{:S(2)}) async-start(), calls=%async_computation.12 | async-start | bytes 10485760 | tf_op jit(solution)/shard_map/reduce_scatter | solution.py:381
  2280.7 599.8 %reduce-scatter.17.cloned.1.call-start = ((), (), s32[]{:S(2)}) async-start(), calls=%async_computation.13 | async-start | bytes 10485760 | tf_op jit(solution)/shard_map/reduce_scatter | solution.py:381
  2281.3 682.8 %reduce-scatter.19.cloned.1.call-start = ((), (), s32[]{:S(2)}) async-start(), calls=%async_computation.14 | async-start | bytes 10485760 | tf_op jit(solution)/shard_map/reduce_scatter | solution.py:381
  2282.0 765.5 %reduce-scatter.29.cloned.1.call-start = ((), (), s32[]{:S(2)}) async-start(), calls=%async_computation.19 | async-start | bytes 10485760 | tf_op jit(solution)/shard_map/reduce_scatter | solution.py:380
  (47 other events, 2138.1 us)
Sparse Core Ops, SparseCore 0:
  14.0 49.4 all-gather.20
  65.3 46.6 all-gather.22
  114.3 46.6 all-gather.24
  163.2 46.6 all-gather.28
  211.5 46.6 all-gather.32
  259.8 46.6 all-gather.36
  308.9 46.6 all-gather.26
  357.3 46.6 all-gather.30
  406.3 46.6 all-gather.34
  454.6 46.6 all-gather.38
  2215.1 80.5 reduce-scatter.20
  2298.5 80.5 reduce-scatter.22
  2382.1 80.5 reduce-scatter.24
  2465.6 80.5 reduce-scatter.26
  2549.6 80.5 reduce-scatter.10
  2633.0 80.5 reduce-scatter.12
  2716.5 80.5 reduce-scatter.14
  2799.9 80.5 reduce-scatter.16
  2883.5 80.5 reduce-scatter.18
  2966.9 80.5 reduce-scatter.28

commit v2 on v1

--- a/solution.py
+++ b/solution.py
@@ -6,6 +6,7 @@
 from jax.experimental import pallas as pl
 from jax.experimental.pallas import tpu as pltpu
 from jax.sharding import PartitionSpec as P
+
 
 NORM_EPS = 1e-6
 GELU_A = 0.7978845608028654
@@ -185,7 +186,7 @@
         return len(self.arrays)
 
 
-def layer_call(kernel, name, order, rows, w_in, w_out, outs, flops):
+def layer_call(kernel, order, rows, w_in, w_out, outs, flops):
     tokens, width = rows[0].shape
     hidden_size = w_out.arrays[0].shape[2] * SHARDS
     blocks_d, blocks_f = width // LANES, hidden_size // LANES
@@ -216,7 +217,6 @@
         out_shape=shapes,
         compiler_params=pltpu.CompilerParams(vmem_limit_bytes=VMEM_LIMIT),
         cost_estimate=pl.CostEstimate(flops=flops * 2 * tokens * width * hidden_size, bytes_accessed=moved, transcendentals=0),
-        name=name,
     )(order, *rows, *w_in.arrays, *w_out.arrays)
 
 
@@ -326,59 +326,82 @@
 
         order_bwd = jnp.stack([bwd_seq(in_chips), bwd_seq(out_chips)]).astype(jnp.int32)
 
+        def gather(n, after):
+            own_in, own_out = to_lanes(w_in_part[n]), to_lanes(w_out_part[n])
+            if after is not None:
+                own_in, own_out, _ = lax.optimization_barrier((own_in, own_out, after))
+            half_in = lax.all_gather(own_in, "local")
+            half_out = lax.all_gather(own_out, "local")
+            return half_in, half_out
+
         saved_x, kept_in, kept_out = [], [], []
         x_cur = x_rows
+        halves = gather(0, None)
         for n in range(layers):
-            half_in = lax.all_gather(to_lanes(w_in_part[n]), "local")
-            half_out = lax.all_gather(to_lanes(w_out_part[n]), "local")
+            half_in, half_out = halves
             twin_in = lax.ppermute(half_in, "data", swap_cores)
             twin_out = lax.ppermute(half_out, "data", swap_cores)
             saved_x.append(x_cur)
+            if n + 1 < layers:
+                halves = gather(n + 1, half_in)
             keep_in = lax.dynamic_slice_in_dim(half_in, 2 * chip_y, 2, 0)
             pair_out = half_out.reshape((2, 2) + half_out.shape[1:])
             keep_out = lax.dynamic_slice_in_dim(pair_out, chip_x, 1, 1)[:, 0]
             (x_next,) = layer_call(
-                forward_kernel, "layer_forward", order_fwd, [x_cur], Pieces([half_in, twin_in], fwd_list), Pieces([half_out, twin_out], fwd_list), ["rows"], 2
+                forward_kernel, order_fwd, [x_cur], Pieces([half_in, twin_in], fwd_list), Pieces([half_out, twin_out], fwd_list), ["rows"], 2
             )
             x_cur, keep_in, keep_out = lax.optimization_barrier((x_next, keep_in, keep_out))
             kept_in.append(keep_in)
             kept_out.append(keep_out)
 
-        grad_cur = grad_rows
-        grads_in, grads_out = [], []
-        for n in reversed(range(layers)):
-            keep_in, keep_out, grad_here = lax.optimization_barrier((kept_in[n], kept_out[n], grad_cur))
+        def exchange(n, grad_cur):
+            keep_in, keep_out, grad_cur = lax.optimization_barrier((kept_in[n], kept_out[n], grad_cur))
             got_in = lax.ppermute(keep_in, "local", swap_y)
             got_out = lax.ppermute(keep_out, "local", swap_x)
             twin_in = lax.ppermute(keep_in, "data", swap_cores)
             twin_out = lax.ppermute(keep_out, "data", swap_cores)
-            twin_got_in = lax.ppermute(got_in, "data", swap_cores)
-            twin_got_out = lax.ppermute(got_out, "data", swap_cores)
-            if grads_in:
-                grad_here, grads_in[-1], grads_out[-1] = lax.optimization_barrier((grad_here, grads_in[-1], grads_out[-1]))
-                reduce(grads_in, grads_out)
-            unit, hidden, dpre, grad_cur = layer_call(
+            return [keep_in, got_in, twin_in], [keep_out, got_out, twin_out], grad_cur
+
+        def swap_got(in_arrays, out_arrays):
+            in_arrays.append(lax.ppermute(in_arrays[1], "data", swap_cores))
+            out_arrays.append(lax.ppermute(out_arrays[1], "data", swap_cores))
+
+        grad_cur = grad_rows
+        grads_in, grads_out = [None] * layers, [None] * layers
+        in_arrays, out_arrays, grad_cur = exchange(layers - 1, grad_cur)
+        swap_got(in_arrays, out_arrays)
+        for n in reversed(range(layers)):
+            if n + 1 < layers:
+                reduce(grads_in, grads_out, n + 1)
+            unit, hidden, dpre, grad_next = layer_call(
                 backward_kernel,
-                "layer_backward",
                 order_bwd,
-                [saved_x[n], grad_here],
-                Pieces([keep_in, got_in, twin_in, twin_got_in], bwd_list),
-                Pieces([keep_out, got_out, twin_out, twin_got_out], bwd_list),
+                [saved_x[n], grad_cur],
+                Pieces(in_arrays, bwd_list),
+                Pieces(out_arrays, bwd_list),
                 [x_rows.shape[1], w_out_part.shape[1] * SHARDS, w_out_part.shape[1] * SHARDS, "rows"],
                 3,
             )
-            out_there = grad_w_out_half(other, hidden, grad_here, None)
+            if n > 0:
+                in_arrays, out_arrays, grad_next = exchange(n - 1, grad_next)
+            out_there = grad_w_out_half(other, hidden, grad_cur, None)
             out_arrived = lax.ppermute(out_there, "data", swap_cores)
             in_there = grad_w_in_half(other, unit, dpre, None)
             in_arrived = lax.ppermute(in_there, "data", swap_cores)
-            grads_out.append(grad_w_out_half(mine, hidden, grad_here, out_arrived))
-            grads_in.append(grad_w_in_half(mine, unit, dpre, in_arrived))
-        reduce(grads_in, grads_out)
-        return x_cur, jnp.stack(grads_in[::-1]), jnp.stack(grads_out[::-1]), grad_cur
-
-    def reduce(grads_in, grads_out):
-        grads_out[-1] = lax.psum_scatter(grads_out[-1], "local", scatter_dimension=0, tiled=True)
-        grads_in[-1] = lax.psum_scatter(grads_in[-1], "local", scatter_dimension=0, tiled=True)
+            grad_out_half = grad_w_out_half(mine, hidden, grad_cur, out_arrived)
+            if n > 0:
+                in_arrays[1], out_arrays[1], grad_out_half = lax.optimization_barrier((in_arrays[1], out_arrays[1], grad_out_half))
+                swap_got(in_arrays, out_arrays)
+            grad_in_half = grad_w_in_half(mine, unit, dpre, in_arrived)
+            if n > 0:
+                grad_next, grad_out_half, grad_in_half = lax.optimization_barrier((grad_next, grad_out_half, grad_in_half))
+            grads_in[n], grads_out[n], grad_cur = grad_in_half, grad_out_half, grad_next
+        reduce(grads_in, grads_out, 0)
+        return x_cur, jnp.stack(grads_in), jnp.stack(grads_out), grad_cur
+
+    def reduce(grads_in, grads_out, n):
+        grads_out[n] = lax.psum_scatter(grads_out[n], "local", scatter_dimension=0, tiled=True)
+        grads_in[n] = lax.psum_scatter(grads_in[n], "local", scatter_dimension=0, tiled=True)
 
     return jax.shard_map(
         device_step,

time: 3070 us -> 2770 us (0.902)
  waiting for transfers between devices: 1430 us -> 1120 us
    all_gather x10, waiting for transfers between devices: 424 us -> 218 us  [the longest x5 130 us: gather(): half_in = lax.all_gather(own_in, 'local')]
    ppermute x30, waiting for transfers between devices: 237 us -> 138 us  [the longest x5 128 us: exchange(): got_in = lax.ppermute(keep_in, 'local', swap_y)]
  transfers between devices with their start and end apart: 70 -> 70, of which waited for: 34 -> 30; matrix products, arithmetic and copies ran while one was open for 3% -> 3% of each run, Pallas kernels for 22% -> 24%
where the time goes in v2:
time: 2770 us; the launch traced here: 2760 us
  Pallas kernels  1490 us (54%)
  waiting for transfers between devices  1120 us (40%)
  local copies, waits for them, and re-layouts  103 us (4%)
    pallas_call x10, Pallas kernels, layer_call(): pl.pallas_call(functools.partial(kernel, (w_in, w_out)), grid_spec=pltpu....  1000 us
    reduce_scatter x5, waiting for transfers between devices, reduce(): lax.psum_scatter(grads_in[n], 'local', scatter_dimension=0, tiled=True)  403 us
    reduce_scatter x5, waiting for transfers between devices, reduce(): lax.psum_scatter(grads_out[n], 'local', scatter_dimension=0, tiled=True)  333 us
    pallas_call x10, Pallas kernels, grad_w_in_half(): pl.pallas_call(functools.partial(weight_grad_kernel, True), grid_spec=plt...  250 us
    pallas_call x10, Pallas kernels, grad_w_out_half(): pl.pallas_call(functools.partial(weight_grad_kernel, False), grid_spec=pl...  244 us
    all_gather x5, waiting for transfers between devices, gather(): half_in = lax.all_gather(own_in, 'local')  130 us
    ppermute x5, waiting for transfers between devices, exchange(): got_in = lax.ppermute(keep_in, 'local', swap_y)  128 us
    all_gather x5, waiting for transfers between devices, gather(): half_out = lax.all_gather(own_out, 'local')  88.1 us
  transfers between devices with their start and end apart: 70, of which 30 were waited for; matrix products, arithmetic and copies ran while one was open for 3% of the time, Pallas kernels for 24%

profile of v2, /device:TPU:0, one launch (start us, length us, event | category | flops | bytes accessed | tf_op | source)
XLA Modules:
  0.0 2758.4 jit_solution(3120283916762605202)
XLA Ops:
  24.4 41.6 %all-gather.21.cloned.1.call-done = bf16[128,128,128]{2,1,0:T(8,128)(2,1)} async-done(((bf16[32,128,128]{2,1,0:T(8,128)(2,1)}), bf16[128,128,128]{2,1,0:T(8,128)(2,1)}) %all-gather.21.cloned.1.call-update) | async-done | bytes 4194320 | tf_op jit(solution)/shard_map/all_gather | solution.py:333
  72.9 42.5 %all-gather.25.cloned.1.call-done = bf16[128,128,128]{2,1,0:T(8,128)(2,1)} async-done(((bf16[32,128,128]{2,1,0:T(8,128)(2,1)}), bf16[128,128,128]{2,1,0:T(8,128)(2,1)}) %all-gather.25.cloned.1.call-update) | async-done | bytes 4194320 | tf_op jit(solution)/shard_map/all_gather | solution.py:333
  130.0 34.9 %all-gather.29.cloned.1.call-done = bf16[128,128,128]{2,1,0:T(8,128)(2,1)} async-done(((bf16[32,128,128]{2,1,0:T(8,128)(2,1)}), bf16[128,128,128]{2,1,0:T(8,128)(2,1)}) %all-gather.29.cloned.1.call-update) | async-done | bytes 4194320 | tf_op jit(solution)/shard_map/all_gather | solution.py:333
  167.3 46.9 %all-gather.23.cloned.1.call-done = bf16[32,512,128]{2,1,0:T(8,128)(2,1)} async-done(((bf16[8,512,128]{2,1,0:T(8,128)(2,1)}), bf16[32,512,128]{2,1,0:T(8,128)(2,1)}) %all-gather.23.cloned.1.call-update) | async-done | bytes 4194320 | tf_op jit(solution)/shard_map/all_gather | solution.py:334
  222.1 41.3 %all-gather.27.cloned.1.call-done = bf16[32,512,128]{2,1,0:T(8,128)(2,1)} async-done(((bf16[8,512,128]{2,1,0:T(8,128)(2,1)}), bf16[32,512,128]{2,1,0:T(8,128)(2,1)}) %all-gather.27.cloned.1.call-update) | async-done | bytes 4194320 | tf_op jit(solution)/shard_map/all_gather | solution.py:334
  265.0 80.1 %shard_map.75.x_ref = bf16[4096,1024]{1,0:T(8,128)(2,1)} custom-call(s32[2,8]{1,0:T(2,128)} %pad_add_fusion.order_ref, bf16[4096,1024]{1,0:T(8,128)(2,1)} %x_ref.3, bf16[4,32,128,128]{3,2,1,0:T(8,128)(2,1)} %bitcast.124, bf16[4,32,128,128]{3,2,1,0:T(8,128)(2,1)} %collective-permute-done.refs_1_, bf16[4,8,512,128]{3,2,1,0:T(8,128)(2,1)} %bitcast.132, ...), custom_call_target="tpu_custom_call" | custom-call | flops 68719476736 | bytes 33554432 | tf_op jit(solution)/shard_map/pallas_call | solution.py:204
  363.2 80.0 %shard_map.76.x_ref = bf16[4096,1024]{1,0:T(8,128)(2,1)} custom-call(s32[2,8]{1,0:T(2,128)} %pad_add_fusion.order_ref, bf16[4096,1024]{1,0:T(8,128)(2,1)} %shard_map.75.x_ref, bf16[4,32,128,128]{3,2,1,0:T(8,128)(2,1)} %bitcast.21.refs_0_, bf16[4,32,128,128]{3,2,1,0:T(8,128)(2,1)} %collective-permute-done.2.refs_1_, bf16[4,8,512,128]{3,2,1,0:T(8,128)(2,1)} %bitcast.129, ...), custom_call_target="tpu_custom_call" | custom-call | flops 68719476736 | bytes 33554432 | tf_op jit(solution)/shard_map/pallas_call | solution.py:204
  452.0 79.1 %shard_map.77.x_ref = bf16[4096,1024]{1,0:T(8,128)(2,1)} custom-call(s32[2,8]{1,0:T(2,128)} %pad_add_fusion.order_ref, bf16[4096,1024]{1,0:T(8,128)(2,1)} %shard_map.76.x_ref, bf16[4,32,128,128]{3,2,1,0:T(8,128)(2,1)} %bitcast.29.refs_0_, bf16[4,32,128,128]{3,2,1,0:T(8,128)(2,1)} %collective-permute-done.4.refs_1_, bf16[4,8,512,128]{3,2,1,0:T(8,128)(2,1)} %bitcast.127, ...), custom_call_target="tpu_custom_call" | custom-call | flops 68719476736 | bytes 33554432 | tf_op jit(solution)/shard_map/pallas_call | solution.py:204
  536.3 79.2 %shard_map.78.x_ref = bf16[4096,1024]{1,0:T(8,128)(2,1)} custom-call(s32[2,8]{1,0:T(2,128)} %pad_add_fusion.order_ref, bf16[4096,1024]{1,0:T(8,128)(2,1)} %shard_map.77.x_ref, bf16[4,32,128,128]{3,2,1,0:T(8,128)(2,1)} %bitcast.37.refs_0_, bf16[4,32,128,128]{3,2,1,0:T(8,128)(2,1)} %collective-permute-done.6.refs_1_, bf16[4,8,512,128]{3,2,1,0:T(8,128)(2,1)} %bitcast.135, ...), custom_call_target="tpu_custom_call" | custom-call | flops 68719476736 | bytes 33554432 | tf_op jit(solution)/shard_map/pallas_call | solution.py:204
  620.0 79.3 %shard_map.79 = bf16[4096,1024]{1,0:T(8,128)(2,1)} custom-call(s32[2,8]{1,0:T(2,128)} %pad_add_fusion.order_ref, bf16[4096,1024]{1,0:T(8,128)(2,1)} %shard_map.78.x_ref, bf16[4,32,128,128]{3,2,1,0:T(8,128)(2,1)} %bitcast.142, bf16[4,32,128,128]{3,2,1,0:T(8,128)(2,1)} %collective-permute-done.8.refs_1_, bf16[4,8,512,128]{3,2,1,0:T(8,128)(2,1)} %bitcast.138, ...), custom_call_target="tpu_custom_call" | custom-call | flops 68719476736 | bytes 33554432 | tf_op jit(solution)/shard_map/pallas_call | solution.py:204
  701.5 45.5 %collective-permute-done.10.refs_1_ = bf16[2,32,128,128]{3,2,1,0:T(8,128)(2,1)} collective-permute-done((bf16[2,32,128,128]{3,2,1,0:T(8,128)(2,1)S(1)}, bf16[2,32,128,128]{3,2,1,0:T(8,128)(2,1)}, u32[]{:S(2)}, u32[]{:S(2)}) %collective-permute-start.10) | collective-permute-done | bytes 2097184 | tf_op jit(solution)/shard_map/ppermute | solution.py:359
  754.4 120.6 %shard_map.80 = (bf16[8,4096,128]{2,1,0:T(8,128)(2,1)}, bf16[32,4096,128]{2,1,0:T(8,128)(2,1)}, bf16[32,4096,128]{2,1,0:T(8,128)(2,1)}, bf16[4096,1024]{1,0:T(8,128)(2,1)}) custom-call(s32[2,8]{1,0:T(2,128)} %pad_add_fusion.1.order_ref, bf16[4096,1024]{1,0:T(8,128)(2,1)} %shard_map.78.x_ref, bf16[4096,1024]{1,0:T(8,128)(2,1)} %right_ref.1, ...), custom_call_target="tpu_custom_call" | custom-call | flops 103079215104 | bytes 117440512 | tf_op jit(solution)/shard_map/pallas_call | solution.py:204
  973.6 25.4 grad_w_in_half.11
  999.0 120.7 %shard_map.81 = (bf16[8,4096,128]{2,1,0:T(8,128)(2,1)}, bf16[32,4096,128]{2,1,0:T(8,128)(2,1)}, bf16[32,4096,128]{2,1,0:T(8,128)(2,1)}, bf16[4096,1024]{1,0:T(8,128)(2,1)}) custom-call(s32[2,8]{1,0:T(2,128)} %pad_add_fusion.1.order_ref, bf16[4096,1024]{1,0:T(8,128)(2,1)} %shard_map.77.x_ref, bf16[4096,1024]{1,0:T(8,128)(2,1)} %get-tuple-element.120.dy_ref.right_ref, ...), custom_call_target="tpu_custom_call" | custom-call | flops 103079215104 | bytes 117440512 | tf_op jit(solution)/shard_map/pallas_call | solution.py:204
  1217.2 25.4 grad_w_in_half.13
  1242.6 120.4 %shard_map.82 = (bf16[8,4096,128]{2,1,0:T(8,128)(2,1)}, bf16[32,4096,128]{2,1,0:T(8,128)(2,1)}, bf16[32,4096,128]{2,1,0:T(8,128)(2,1)}, bf16[4096,1024]{1,0:T(8,128)(2,1)}) custom-call(s32[2,8]{1,0:T(2,128)} %pad_add_fusion.1.order_ref, bf16[4096,1024]{1,0:T(8,128)(2,1)} %shard_map.76.x_ref, bf16[4096,1024]{1,0:T(8,128)(2,1)} %get-tuple-element.131.dy_ref.right_ref, ...), custom_call_target="tpu_custom_call" | custom-call | flops 103079215104 | bytes 117440512 | tf_op jit(solution)/shard_map/pallas_call | solution.py:204
  1461.4 25.4 grad_w_in_half.15
  1486.8 120.6 %shard_map.83 = (bf16[8,4096,128]{2,1,0:T(8,128)(2,1)}, bf16[32,4096,128]{2,1,0:T(8,128)(2,1)}, bf16[32,4096,128]{2,1,0:T(8,128)(2,1)}, bf16[4096,1024]{1,0:T(8,128)(2,1)}) custom-call(s32[2,8]{1,0:T(2,128)} %pad_add_fusion.1.order_ref, bf16[4096,1024]{1,0:T(8,128)(2,1)} %shard_map.75.x_ref, bf16[4096,1024]{1,0:T(8,128)(2,1)} %get-tuple-element.142.dy_ref.right_ref, ...), custom_call_target="tpu_custom_call" | custom-call | flops 103079215104 | bytes 117440512 | tf_op jit(solution)/shard_map/pallas_call | solution.py:204
  1704.9 25.4 grad_w_in_half.17
  1730.3 120.5 %shard_map.84 = (bf16[8,4096,128]{2,1,0:T(8,128)(2,1)}, bf16[32,4096,128]{2,1,0:T(8,128)(2,1)}, bf16[32,4096,128]{2,1,0:T(8,128)(2,1)}, bf16[4096,1024]{1,0:T(8,128)(2,1)}) custom-call(s32[2,8]{1,0:T(2,128)} %pad_add_fusion.1.order_ref, bf16[4096,1024]{1,0:T(8,128)(2,1)} %x_ref.3, bf16[4096,1024]{1,0:T(8,128)(2,1)} %get-tuple-element.153.dy_ref.right_ref, ...), custom_call_target="tpu_custom_call" | custom-call | flops 103079215104 | bytes 117440512 | tf_op jit(solution)/shard_map/pallas_call | solution.py:204
  1888.5 24.8 grad_w_out_half.19
  1915.3 25.1 grad_w_in_half.18
  1954.0 26.2 grad_w_in_half.19
  1997.4 80.5 %reduce-scatter.23.cloned.1.call-done = f32[512,1024]{1,0:T(8,128)} async-done(((f32[2048,1024]{1,0:T(8,128)}), f32[512,1024]{1,0:T(8,128)}) %reduce-scatter.23.cloned.1.call-update) | async-done | bytes 2097168 | tf_op jit(solution)/shard_map/reduce_scatter | solution.py:403
  2081.0 80.6 %reduce-scatter.25.cloned.1.call-done = f32[512,1024]{1,0:T(8,128)} async-done(((f32[2048,1024]{1,0:T(8,128)}), f32[512,1024]{1,0:T(8,128)}) %reduce-scatter.25.cloned.1.call-update) | async-done | bytes 2097168 | tf_op jit(solution)/shard_map/reduce_scatter | solution.py:403
  2164.8 80.5 %reduce-scatter.27.cloned.1.call-done = f32[512,1024]{1,0:T(8,128)} async-done(((f32[2048,1024]{1,0:T(8,128)}), f32[512,1024]{1,0:T(8,128)}) %reduce-scatter.27.cloned.1.call-update) | async-done | bytes 2097168 | tf_op jit(solution)/shard_map/reduce_scatter | solution.py:403
  2248.5 81.0 %reduce-scatter.11.cloned.1.call-done = f32[128,4096]{1,0:T(8,128)} async-done(((f32[512,4096]{1,0:T(8,128)}), f32[128,4096]{1,0:T(8,128)}) %reduce-scatter.11.cloned.1.call-update) | async-done | bytes 2097168 | tf_op jit(solution)/shard_map/reduce_scatter | solution.py:404
  2332.6 80.6 %reduce-scatter.13.cloned.1.call-done = f32[128,4096]{1,0:T(8,128)} async-done(((f32[512,4096]{1,0:T(8,128)}), f32[128,4096]{1,0:T(8,128)}) %reduce-scatter.13.cloned.1.call-update) | async-done | bytes 2097168 | tf_op jit(solution)/shard_map/reduce_scatter | solution.py:404
  2416.3 80.5 %reduce-scatter.15.cloned.1.call-done = f32[128,4096]{1,0:T(8,128)} async-done(((f32[512,4096]{1,0:T(8,128)}), f32[128,4096]{1,0:T(8,128)}) %reduce-scatter.15.cloned.1.call-update) | async-done | bytes 2097168 | tf_op jit(solution)/shard_map/reduce_scatter | solution.py:404
  2499.9 80.6 %reduce-scatter.17.cloned.1.call-done = f32[128,4096]{1,0:T(8,128)} async-done(((f32[512,4096]{1,0:T(8,128)}), f32[128,4096]{1,0:T(8,128)}) %reduce-scatter.17.cloned.1.call-update) | async-done | bytes 2097168 | tf_op jit(solution)/shard_map/reduce_scatter | solution.py:404
  2583.6 80.7 %reduce-scatter.19.cloned.1.call-done = f32[128,4096]{1,0:T(8,128)} async-done(((f32[512,4096]{1,0:T(8,128)}), f32[128,4096]{1,0:T(8,128)}) %reduce-scatter.19.cloned.1.call-update) | async-done | bytes 2097168 | tf_op jit(solution)/shard_map/reduce_scatter | solution.py:404
  2667.4 80.5 %reduce-scatter.29.cloned.1.call-done = f32[512,1024]{1,0:T(8,128)} async-done(((f32[2048,1024]{1,0:T(8,128)}), f32[512,1024]{1,0:T(8,128)}) %reduce-scatter.29.cloned.1.call-update) | async-done | bytes 2097168 | tf_op jit(solution)/shard_map/reduce_scatter | solution.py:403
  (225 shorter events, 587.2 us)
Async XLA Ops:
  16.0 99.4 %all-gather.25.cloned.1.call-start = ((), (), s32[]{:S(2)}) async-start(), calls=%async_computation.22 | async-start | bytes 5242880 | tf_op jit(solution)/shard_map/all_gather | solution.py:333
  68.3 96.6 %all-gather.29.cloned.1.call-start = ((), (), s32[]{:S(2)}) async-start(), calls=%async_computation.24 | async-start | bytes 5242880 | tf_op jit(solution)/shard_map/all_gather | solution.py:333
  117.8 96.4 %all-gather.23.cloned.1.call-start = ((), (), s32[]{:S(2)}) async-start(), calls=%async_computation.21 | async-start | bytes 5242880 | tf_op jit(solution)/shard_map/all_gather | solution.py:334
  122.4 141.0 %all-gather.27.cloned.1.call-start = ((), (), s32[]{:S(2)}) async-start(), calls=%async_computation.23 | async-start | bytes 5242880 | tf_op jit(solution)/shard_map/all_gather | solution.py:334
  124.8 225.7 %all-gather.31.cloned.1.call-start = ((), (), s32[]{:S(2)}) async-start(), calls=%async_computation.25 | async-start | bytes 5242880 | tf_op jit(solution)/shard_map/all_gather | solution.py:334
  127.1 234.3 %all-gather.33.cloned.1.call-start = ((), (), s32[]{:S(2)}) async-start(), calls=%async_computation.26 | async-start | bytes 5242880 | tf_op jit(solution)/shard_map/all_gather | solution.py:333
  167.2 283.7 %all-gather.35.cloned.1.call-start = ((), (), s32[]{:S(2)}) async-start(), calls=%async_computation.27 | async-start | bytes 5242880 | tf_op jit(solution)/shard_map/all_gather | solution.py:334
  167.3 97.7 %collective-permute-start = (bf16[4,32,128,128]{3,2,1,0:T(8,128)(2,1)}, bf16[4,32,128,128]{3,2,1,0:T(8,128)(2,1)}, u32[]{:S(2)}, u32[]{:S(2)}) collective-permute-start(bf16[4,32,128,128]{3,2,1,0:T(8,128)(2,1)} %bitcast.122), channel_id=1, source_target_pairs={{0,1},{1,0},{2,3},{3,2},{4,5},{5,4},{6,7},{7,6}} | collective-permute-start | bytes 12582920 | tf_op jit(solution)/shard_map/ppermute | solution.py:342
  221.6 141.5 %collective-permute-start.2 = (bf16[4,32,128,128]{3,2,1,0:T(8,128)(2,1)}, bf16[4,32,128,128]{3,2,1,0:T(8,128)(2,1)}, u32[]{:S(2)}, u32[]{:S(2)}) collective-permute-start(bf16[4,32,128,128]{3,2,1,0:T(8,128)(2,1)} %bitcast.21.refs_0_), channel_id=1, source_target_pairs={{0,1},{1,0},{2,3},{3,2},{4,5},{5,4},{6,7},{7,6}} | collective-permute-start | bytes 12582920 | tf_op jit(solution)/shard_map/ppermute | solution.py:342
  263.4 99.7 %collective-permute-start.3 = (bf16[4,8,512,128]{3,2,1,0:T(8,128)(2,1)}, bf16[4,8,512,128]{3,2,1,0:T(8,128)(2,1)}, u32[]{:S(2)}, u32[]{:S(2)}) collective-permute-start(bf16[4,8,512,128]{3,2,1,0:T(8,128)(2,1)} %bitcast.128), channel_id=1, source_target_pairs={{0,1},{1,0},{2,3},{3,2},{4,5},{5,4},{6,7},{7,6}} | collective-permute-start | bytes 12582920 | tf_op jit(solution)/shard_map/ppermute | solution.py:343
  264.7 271.1 %all-gather.39.cloned.1.call-start = ((), (), s32[]{:S(2)}) async-start(), calls=%async_computation.29 | async-start | bytes 5242880 | tf_op jit(solution)/shard_map/all_gather | solution.py:334
  349.9 102.0 %collective-permute-start.4 = (bf16[4,32,128,128]{3,2,1,0:T(8,128)(2,1)}, bf16[4,32,128,128]{3,2,1,0:T(8,128)(2,1)}, u32[]{:S(2)}, u32[]{:S(2)}) collective-permute-start(bf16[4,32,128,128]{3,2,1,0:T(8,128)(2,1)} %bitcast.29.refs_0_), channel_id=1, source_target_pairs={{0,1},{1,0},{2,3},{3,2},{4,5},{5,4},{6,7},{7,6}} | collective-permute-start | bytes 12582920 | tf_op jit(solution)/shard_map/ppermute | solution.py:342
  350.5 101.5 %collective-permute-start.5 = (bf16[4,8,512,128]{3,2,1,0:T(8,128)(2,1)}, bf16[4,8,512,128]{3,2,1,0:T(8,128)(2,1)}, u32[]{:S(2)}, u32[]{:S(2)}) collective-permute-start(bf16[4,8,512,128]{3,2,1,0:T(8,128)(2,1)} %bitcast.125), channel_id=1, source_target_pairs={{0,1},{1,0},{2,3},{3,2},{4,5},{5,4},{6,7},{7,6}} | collective-permute-start | bytes 12582920 | tf_op jit(solution)/shard_map/ppermute | solution.py:343
  362.8 173.0 %all-gather.37.cloned.1.call-start = ((), (), s32[]{:S(2)}) async-start(), calls=%async_computation.28 | async-start | bytes 5242880 | tf_op jit(solution)/shard_map/all_gather | solution.py:333
  449.6 86.7 %collective-permute-start.6 = (bf16[4,32,128,128]{3,2,1,0:T(8,128)(2,1)}, bf16[4,32,128,128]{3,2,1,0:T(8,128)(2,1)}, u32[]{:S(2)}, u32[]{:S(2)}) collective-permute-start(bf16[4,32,128,128]{3,2,1,0:T(8,128)(2,1)} %bitcast.37.refs_0_), channel_id=1, source_target_pairs={{0,1},{1,0},{2,3},{3,2},{4,5},{5,4},{6,7},{7,6}} | collective-permute-start | bytes 12582920 | tf_op jit(solution)/shard_map/ppermute | solution.py:342
  450.9 85.4 %collective-permute-start.7 = (bf16[4,8,512,128]{3,2,1,0:T(8,128)(2,1)}, bf16[4,8,512,128]{3,2,1,0:T(8,128)(2,1)}, u32[]{:S(2)}, u32[]{:S(2)}) collective-permute-start(bf16[4,8,512,128]{3,2,1,0:T(8,128)(2,1)} %bitcast.134), channel_id=1, source_target_pairs={{0,1},{1,0},{2,3},{3,2},{4,5},{5,4},{6,7},{7,6}} | collective-permute-start | bytes 12582920 | tf_op jit(solution)/shard_map/ppermute | solution.py:343
  451.4 1542.8 %reduce-scatter.21.cloned.1.call-start = ((), (), s32[]{:S(2)}) async-start(), calls=%async_computation.15 | async-start | bytes 10485760 | tf_op jit(solution)/shard_map/reduce_scatter | solution.py:403
  535.8 84.2 %collective-permute-start.9 = (bf16[4,8,512,128]{3,2,1,0:T(8,128)(2,1)}, bf16[4,8,512,128]{3,2,1,0:T(8,128)(2,1)}, u32[]{:S(2)}, u32[]{:S(2)}) collective-permute-start(bf16[4,8,512,128]{3,2,1,0:T(8,128)(2,1)} %bitcast.137), channel_id=1, source_target_pairs={{0,1},{1,0},{2,3},{3,2},{4,5},{5,4},{6,7},{7,6}} | collective-permute-start | bytes 12582920 | tf_op jit(solution)/shard_map/ppermute | solution.py:343
  535.8 84.2 %collective-permute-start.8 = (bf16[4,32,128,128]{3,2,1,0:T(8,128)(2,1)}, bf16[4,32,128,128]{3,2,1,0:T(8,128)(2,1)}, u32[]{:S(2)}, u32[]{:S(2)}) collective-permute-start(bf16[4,32,128,128]{3,2,1,0:T(8,128)(2,1)} %bitcast.140), channel_id=1, source_target_pairs={{0,1},{1,0},{2,3},{3,2},{4,5},{5,4},{6,7},{7,6}} | collective-permute-start | bytes 12582920 | tf_op jit(solution)/shard_map/ppermute | solution.py:342
  925.7 73.3 %collective-permute-start.20 = (bf16[2,32,128,128]{3,2,1,0:T(8,128)(2,1)S(1)}, bf16[2,32,128,128]{3,2,1,0:T(8,128)(2,1)}, u32[]{:S(2)}, u32[]{:S(2)}) collective-permute-start(bf16[2,32,128,128]{3,2,1,0:T(8,128)(2,1)S(1)} %copy-done.4), channel_id=1, source_target_pairs={{0,1},{1,0},{2,3},{3,2},{4,5},{5,4},{6,7},{7,6}} | collective-permute-start | bytes 6291464 | tf_op jit(solution)/shard_map/ppermute | solution.py:361
  925.7 73.3 %collective-permute-start.22 = (bf16[2,8,512,128]{3,2,1,0:T(8,128)(2,1)}, bf16[2,8,512,128]{3,2,1,0:T(8,128)(2,1)}, u32[]{:S(2)}, u32[]{:S(2)}) collective-permute-start(bf16[2,8,512,128]{3,2,1,0:T(8,128)(2,1)} %dynamic-slice_bitcast_fusion.1.refs_4_), channel_id=1, source_target_pairs={{0,1},{1,0},{2,3},{3,2},{4,5},{5,4},{6,7},{7,6}} | collective-permute-start | bytes 6291464 | tf_op jit(solution)/shard_map/ppermute | solution.py:362
  1413.6 73.2 %collective-permute-start.36 = (bf16[2,32,128,128]{3,2,1,0:T(8,128)(2,1)S(1)}, bf16[2,32,128,128]{3,2,1,0:T(8,128)(2,1)}, u32[]{:S(2)}, u32[]{:S(2)}) collective-permute-start(bf16[2,32,128,128]{3,2,1,0:T(8,128)(2,1)S(1)} %copy-done.2), channel_id=1, source_target_pairs={{0,1},{1,0},{2,3},{3,2},{4,5},{5,4},{6,7},{7,6}} | collective-permute-start | bytes 6291464 | tf_op jit(solution)/shard_map/ppermute | solution.py:361
  1413.6 73.2 %collective-permute-start.38 = (bf16[2,8,512,128]{3,2,1,0:T(8,128)(2,1)}, bf16[2,8,512,128]{3,2,1,0:T(8,128)(2,1)}, u32[]{:S(2)}, u32[]{:S(2)}) collective-permute-start(bf16[2,8,512,128]{3,2,1,0:T(8,128)(2,1)} %dynamic-slice_bitcast_fusion.3.refs_4_), channel_id=1, source_target_pairs={{0,1},{1,0},{2,3},{3,2},{4,5},{5,4},{6,7},{7,6}} | collective-permute-start | bytes 6291464 | tf_op jit(solution)/shard_map/ppermute | solution.py:362
  1913.3 164.6 %reduce-scatter.23.cloned.1.call-start = ((), (), s32[]{:S(2)}) async-start(), calls=%async_computation.16 | async-start | bytes 10485760 | tf_op jit(solution)/shard_map/reduce_scatter | solution.py:403
  1913.9 247.8 %reduce-scatter.25.cloned.1.call-start = ((), (), s32[]{:S(2)}) async-start(), calls=%async_computation.17 | async-start | bytes 10485760 | tf_op jit(solution)/shard_map/reduce_scatter | solution.py:403
  1914.6 330.7 %reduce-scatter.27.cloned.1.call-start = ((), (), s32[]{:S(2)}) async-start(), calls=%async_computation.18 | async-start | bytes 10485760 | tf_op jit(solution)/shard_map/reduce_scatter | solution.py:403
  1915.2 414.3 %reduce-scatter.11.cloned.1.call-start = ((), (), s32[]{:S(2)}) async-start(), calls=%async_computation.10 | async-start | bytes 10485760 | tf_op jit(solution)/shard_map/reduce_scatter | solution.py:404
  1980.2 433.0 %reduce-scatter.13.cloned.1.call-start = ((), (), s32[]{:S(2)}) async-start(), calls=%async_computation.11 | async-start | bytes 10485760 | tf_op jit(solution)/shard_map/reduce_scatter | solution.py:404
  1980.8 516.1 %reduce-scatter.15.cloned.1.call-start = ((), (), s32[]{:S(2)}) async-start(), calls=%async_computation.12 | async-start | bytes 10485760 | tf_op jit(solution)/shard_map/reduce_scatter | solution.py:404
  1981.3 599.1 %reduce-scatter.17.cloned.1.call-start = ((), (), s32[]{:S(2)}) async-start(), calls=%async_computation.13 | async-start | bytes 10485760 | tf_op jit(solution)/shard_map/reduce_scatter | solution.py:404
  1981.9 682.4 %reduce-scatter.19.cloned.1.call-start = ((), (), s32[]{:S(2)}) async-start(), calls=%async_computation.14 | async-start | bytes 10485760 | tf_op jit(solution)/shard_map/reduce_scatter | solution.py:404
  1982.7 765.3 %reduce-scatter.29.cloned.1.call-start = ((), (), s32[]{:S(2)}) async-start(), calls=%async_computation.19 | async-start | bytes 10485760 | tf_op jit(solution)/shard_map/reduce_scatter | solution.py:403
  (48 other events, 1722.6 us)
Sparse Core Ops, SparseCore 0:
  16.2 49.7 all-gather.20
  68.4 47.0 all-gather.24
  117.9 46.9 all-gather.28
  167.1 46.9 all-gather.22
  216.4 46.9 all-gather.26
  265.0 46.9 all-gather.30
  314.4 47.0 all-gather.32
  363.8 47.0 all-gather.34
  412.7 46.9 all-gather.38
  461.3 46.9 all-gather.36
  1913.4 80.7 reduce-scatter.20
  1997.1 80.7 reduce-scatter.22
  2080.9 80.7 reduce-scatter.24
  2164.5 80.7 reduce-scatter.26
  2248.8 80.7 reduce-scatter.10
  2332.4 80.7 reduce-scatter.12
  2416.0 80.7 reduce-scatter.14
  2499.7 80.7 reduce-scatter.16
  2583.5 80.7 reduce-scatter.18
  2667.1 80.7 reduce-scatter.28

commit v3 on v2

--- a/solution.py
+++ b/solution.py
@@ -22,6 +22,7 @@
 TOK_TILE = 256
 CHUNK = 256
 VMEM_LIMIT = 60 * 1024 * 1024
+MESH = pl.DeviceIdType.MESH
 
 
 def unit_rows_of(x_tile):
@@ -78,45 +79,6 @@
     @pl.when(step > 0)
     def _():
         body(lambda p: None)
-
-
-def forward_kernel(pieces, order_ref, x_ref, *refs):
-    n_in, n_out = len(pieces[0]), len(pieces[1])
-    w_in_refs, w_out_refs = refs[:n_in], refs[n_in : n_in + n_out]
-    y_ref, w_in_buf, w_out_buf, sem = refs[n_in + n_out :]
-    w_in_pieces = [(w_in_refs[a], i) for a, i in piece_list(pieces[0])]
-    w_out_pieces = [(w_out_refs[a], i) for a, i in piece_list(pieces[1])]
-    hidden_size = w_out_buf.shape[1]
-    per_group = hidden_size // SHARDS // CHUNK
-    blocks = CHUNK // LANES
-    d_blocks = w_out_buf.shape[0]
-
-    def body(wait):
-        x_wide, inv_rms = unit_rows_of(x_ref[...])
-        unit = (x_wide * inv_rms).astype(BF16)
-        total = None
-        pending = []
-
-        def finish(total):
-            chunk, hidden = pending.pop(0)
-            w_out = lane_join(w_out_buf, 0, d_blocks, pl.ds(chunk * CHUNK, CHUNK))
-            part = jnp.dot(hidden, w_out, preferred_element_type=F32)
-            return part if total is None else total + part
-
-        for chunk in range(hidden_size // CHUNK):
-            if chunk % per_group == 0:
-                wait(chunk // per_group)
-            w_in = lane_join(w_in_buf, chunk * blocks, blocks)
-            pre = jnp.dot(unit, w_in, preferred_element_type=F32).astype(BF16).astype(F32)
-            tanh = jnp.tanh(pre * (GELU_A + GELU_B * (pre * pre)))
-            pending.append((chunk, (pre * (0.5 * tanh + 0.5)).astype(BF16)))
-            if len(pending) > 2:
-                total = finish(total)
-        while pending:
-            total = finish(total)
-        y_ref[...] = (x_ref[...].astype(F32) + total).astype(BF16)
-
-    with_weights(order_ref, w_in_pieces, w_out_pieces, w_in_buf, w_out_buf, sem, body)
 
 
 def backward_kernel(pieces, order_ref, x_ref, dy_ref, *refs):
@@ -187,7 +149,7 @@
 
 
 def layer_call(kernel, order, rows, w_in, w_out, outs, flops):
-    tokens, width = rows[0].shape
+    tokens, width = rows[0][0].shape[1:]
     hidden_size = w_out.arrays[0].shape[2] * SHARDS
     blocks_d, blocks_f = width // LANES, hidden_size // LANES
     row_spec = pl.BlockSpec((TOK_TILE, width), lambda i, order: (i, 0))
@@ -206,7 +168,8 @@
         grid_spec=pltpu.PrefetchScalarGridSpec(
             num_scalar_prefetch=1,
             grid=(tokens // TOK_TILE,),
-            in_specs=[row_spec] * len(rows) + [pl.BlockSpec(memory_space=pl.ANY)] * n_weights,
+            in_specs=[pl.BlockSpec((None, TOK_TILE, width), lambda i, order, at=at: (at, i, 0)) for _, at in rows]
+            + [pl.BlockSpec(memory_space=pl.ANY)] * n_weights,
             out_specs=specs,
             scratch_shapes=[
                 pltpu.VMEM((blocks_f, width, LANES), BF16),
@@ -217,7 +180,7 @@
         out_shape=shapes,
         compiler_params=pltpu.CompilerParams(vmem_limit_bytes=VMEM_LIMIT),
         cost_estimate=pl.CostEstimate(flops=flops * 2 * tokens * width * hidden_size, bytes_accessed=moved, transcendentals=0),
-    )(order, *rows, *w_in.arrays, *w_out.arrays)
+    )(order, *[array for array, _ in rows], *w_in.arrays, *w_out.arrays)
 
 
 def weight_grad_kernel(dy_lanes, half_ref, left_ref, right_ref, *refs):
@@ -292,9 +255,360 @@
     )(half, unit, dpre, *extra)
 
 
-def to_lanes(w):
-    rows, columns = w.shape
-    return w.reshape(rows, columns // LANES, LANES).transpose(1, 0, 2)
+class Place:
+    def __init__(self):
+        self.chip = lax.axis_index("local")
+        self.core = lax.axis_index("data")
+        self.chip_x, self.chip_y = lax.rem(self.chip, 2), lax.div(self.chip, 2)
+
+    def chip_at(self, mask):
+        mask_x, mask_y = (mask % 2, mask // 2) if isinstance(mask, int) else (lax.rem(mask, 2), lax.div(mask, 2))
+        return lax.rem(self.chip_x + mask_x, 2) + 2 * lax.rem(self.chip_y + mask_y, 2)
+
+    def across(self, mask):
+        return (self.chip_at(mask), self.core)
+
+    def twin(self):
+        return (self.chip, 1 - self.core)
+
+    def peers(self):
+        return [self.across(1), self.across(2), self.across(3), self.twin()]
+
+
+def meet(place):
+    barrier = pltpu.get_barrier_semaphore()
+    for device in place.peers():
+        pl.semaphore_signal(barrier, inc=1, device_id=device, device_id_type=MESH)
+    pl.semaphore_wait(barrier, 4)
+
+
+def remote(src, dst, send_sem, recv_sem, device):
+    return pltpu.make_async_remote_copy(
+        src_ref=src, dst_ref=dst, send_sem=send_sem, recv_sem=recv_sem, device_id=device, device_id_type=MESH
+    )
+
+
+class Stream:
+    def __init__(self, place, own_in, own_out, kept_in, kept_out, got_in, got_out, twin_in, twin_out, sems):
+        self.place = place
+        self.own_in, self.own_out, self.kept_in, self.kept_out = own_in, own_out, kept_in, kept_out
+        self.got_in, self.got_out, self.twin_in, self.twin_out = got_in, got_out, twin_in, twin_out
+        (self.in_send, self.in_recv, self.out_send, self.out_recv) = sems[:4]
+        (self.twin_in_send, self.twin_in_recv, self.twin_out_send, self.twin_out_recv) = sems[4:]
+        self.blocks = own_in.shape[1] // CHIPS
+
+    def mine_in(self, n, mask, block, count):
+        slot, rows = lax.rem(n, 2), pl.ds(block, count)
+        if mask == 0:
+            return self.own_in.at[n, rows]
+        if mask == 1:
+            return self.kept_in.at[n, rows]
+        return self.got_in.at[slot, mask - 2, rows]
+
+    def mine_out(self, n, mask):
+        slot = lax.rem(n, 2)
+        if mask == 0:
+            return self.own_out.at[n]
+        if mask == 2:
+            return self.kept_out.at[n]
+        return self.got_out.at[slot, (mask - 1) // 2]
+
+    def push_in(self, n, mask, unit, block):
+        src = self.own_in.at[n, pl.ds(block, self.blocks)]
+        dst = self.mine_in(n, mask, block, self.blocks)
+        recv = self.in_recv.at[lax.rem(n, 2), mask - 1, unit]
+        return remote(src, dst, self.in_send.at[mask - 1, unit], recv, self.place.across(mask))
+
+    def push_out(self, n, mask):
+        recv = self.out_recv.at[lax.rem(n, 2), mask - 1]
+        return remote(self.own_out.at[n], self.mine_out(n, mask), self.out_send.at[mask - 1], recv, self.place.across(mask))
+
+    def pushes(self, n):
+        copies = []
+        for unit in range(CHIPS):
+            for mask in (1, 2, 3):
+                copies.append(self.push_in(n, mask, unit, self.place.chip_at(mask ^ unit) * self.blocks))
+            if unit:
+                copies.append(self.push_out(n, unit))
+        return copies
+
+    def push(self, n):
+        for copy in self.pushes(n):
+            copy.start()
+
+    def push_sent(self, n):
+        for copy in self.pushes(n):
+            copy.wait_send()
+
+    def twin_copies(self, n, unit):
+        slot, block = lax.rem(n, 2), self.place.chip_at(unit) * self.blocks
+        return [
+            remote(
+                self.mine_in(n, mask, block, self.blocks),
+                self.twin_in.at[slot, mask, pl.ds(block, self.blocks)],
+                self.twin_in_send.at[mask, unit],
+                self.twin_in_recv.at[slot, mask, unit],
+                self.place.twin(),
+            )
+            for mask in range(CHIPS)
+        ]
+
+    def twin_out_copy(self, n, mask, unit):
+        slot = lax.rem(n, 2)
+        return remote(
+            self.mine_out(n, mask),
+            self.twin_out.at[slot, unit],
+            self.twin_out_send.at[unit],
+            self.twin_out_recv.at[slot, unit],
+            self.place.twin(),
+        )
+
+    def forward(self, n, unit):
+        block = self.place.chip_at(unit) * self.blocks
+        for mask in (1, 2, 3):
+            self.push_in(n, mask, unit, block).wait_recv()
+        for copy in self.twin_copies(n, unit):
+            copy.start()
+        for mask in range(CHIPS):
+
+            @pl.when(unit == mask)
+            def _():
+                if mask:
+                    self.push_out(n, mask).wait_recv()
+                self.twin_out_copy(n, mask, unit).start()
+
+    def forward_sent(self, n, unit):
+        for copy in self.twin_copies(n, unit):
+            copy.wait_send()
+        self.twin_out_copy(n, 0, unit).wait_send()
+
+    def arrive(self, n, unit):
+        for copy in self.twin_copies(n, unit):
+            copy.wait_recv()
+        self.twin_out_copy(n, 0, unit).wait_recv()
+
+    def load_in(self, n, unit, parity, w_in_v, v, sem):
+        count, depth = self.blocks // 2, self.own_in.shape[2]
+        block = self.place.chip_at(unit) * self.blocks + parity * count
+        copies = []
+        for mask in range(CHIPS):
+            for which in range(2):
+                shard = 2 * self.place.chip_at(mask) + (self.place.core if which == 0 else 1 - self.place.core)
+                src = self.mine_in(n, mask, block, count) if which == 0 else self.twin_in.at[lax.rem(n, 2), mask, pl.ds(block, count)]
+                row = pl.ds(pl.multiple_of(shard * depth, depth), depth)
+                copies.append(pltpu.make_async_copy(src, w_in_v.at[v, :, row], sem.at[v, 2 * mask + which]))
+        return copies
+
+    def load(self, n, unit, other, w_in_v, w_out_v, v, sem):
+        parity = self.place.core + other - 2 * self.place.core * other
+        for copy in self.load_in(n, unit, parity, w_in_v, v, sem):
+            copy.start()
+        last = sem.at[v, 2 * CHIPS]
+
+        @pl.when(other == 1)
+        def _():
+            pltpu.make_async_copy(self.twin_out.at[lax.rem(n, 2), unit], w_out_v.at[v], last).start()
+
+        for mask in range(CHIPS):
+
+            @pl.when((other == 0) & (unit == mask))
+            def _():
+                pltpu.make_async_copy(self.mine_out(n, mask), w_out_v.at[v], last).start()
+
+    def loaded(self, w_in_v, w_out_v, v, sem):
+        for copy in self.load_in(0, 0, 0, w_in_v, v, sem):
+            copy.wait()
+        pltpu.make_async_copy(self.own_out.at[0], w_out_v.at[v], sem.at[v, 2 * CHIPS]).wait()
+
+
+def tile_of(ref, rows):
+    return jnp.concatenate([ref[b, rows, :] for b in range(ref.shape[0])], axis=1)
+
+
+def put_tile(ref, rows, value):
+    for b in range(ref.shape[0]):
+        ref[b, rows, :] = value[:, b * LANES : (b + 1) * LANES]
+
+
+def forward_stack_kernel(layers, x_ref, own_in, own_out, *refs):
+    xs_ref, kept_in, kept_out, got_in, got_out, twin_in, twin_out = refs[:7]
+    x_v, unit_v, total_v, w_in_v, w_out_v = refs[7:12]
+    x_sem, load_sem, credit = refs[12:15]
+    sems = refs[15:]
+    place = Place()
+    stream = Stream(place, own_in, own_out, kept_in, kept_out, got_in, got_out, twin_in, twin_out, sems)
+    tokens, width = x_v.shape
+    tiles = tokens // TOK_TILE
+    chunks = 2 * CHIPS
+
+    meet(place)
+    stream.push(0)
+    fetch = pltpu.make_async_copy(x_ref, x_v, x_sem)
+    fetch.start()
+    fetch.wait()
+
+    def first_unit(t, carry):
+        rows = pl.ds(pl.multiple_of(t * TOK_TILE, TOK_TILE), TOK_TILE)
+        x_wide, inv_rms = unit_rows_of(x_v[rows, :])
+        put_tile(unit_v, rows, (x_wide * inv_rms).astype(BF16))
+        total_v[rows, :] = jnp.zeros((TOK_TILE, width), F32)
+        return carry
+
+    lax.fori_loop(0, tiles, first_unit, 0)
+    stream.forward(0, 0)
+    stream.arrive(0, 0)
+    stream.load(0, 0, 0, w_in_v, w_out_v, 0, load_sem)
+    stream.forward_sent(0, 0)
+
+    def save(n):
+        return pltpu.make_async_copy(x_v, xs_ref.at[n], x_sem)
+
+    def compute(v, last):
+        w_in = lane_join(w_in_v.at[v], 0, w_in_v.shape[1])
+        w_out = lane_join(w_out_v.at[v], 0, w_out_v.shape[1])
+        pending = []
+
+        def finish():
+            t, hidden = pending.pop(0)
+            rows = pl.ds(t * TOK_TILE, TOK_TILE)
+            total = total_v[rows, :] + jnp.dot(hidden, w_out, preferred_element_type=F32)
+            if not last:
+                total_v[rows, :] = total
+                return
+            x_next = (x_v[rows, :].astype(F32) + total).astype(BF16)
+            x_v[rows, :] = x_next
+            total_v[rows, :] = jnp.zeros((TOK_TILE, width), F32)
+            x_wide, inv_rms = unit_rows_of(x_next)
+            put_tile(unit_v, rows, (x_wide * inv_rms).astype(BF16))
+
+        for t in range(tiles):
+            unit = tile_of(unit_v, pl.ds(t * TOK_TILE, TOK_TILE))
+            pre = jnp.dot(unit, w_in, preferred_element_type=F32).astype(BF16).astype(F32)
+            tanh = jnp.tanh(pre * (GELU_A + GELU_B * (pre * pre)))
+            pending.append((t, (pre * (0.5 * tanh + 0.5)).astype(BF16)))
+            if len(pending) > 1:
+                finish()
+        while pending:
+            finish()
+
+    def chunk_step(n, step):
+        unit, other, v = lax.div(step, 2), lax.rem(step, 2), lax.rem(step, 2)
+        more = n + 1 < layers
+
+        @pl.when(step == 0)
+        def _():
+            stream.push_sent(n)
+
+            @pl.when(more)
+            def _():
+                for q, device in enumerate(place.peers()):
+                    pl.semaphore_signal(credit.at[q], inc=1, device_id=device, device_id_type=MESH)
+                for q in range(CHIPS):
+                    pl.semaphore_wait(credit.at[q], 1)
+                stream.push(n + 1)
+
+        sends = [
+            ((other == 0) & (unit >= 2) & more, n + 1, unit - 2),
+            ((other == 0) & (unit < 2) & (n > 0), n, unit + 2),
+            ((other == 1) & (unit < 3) & (n == 0), n, unit + 1),
+        ]
+        for condition, layer, which in sends:
+
+            @pl.when(condition)
+            def _():
+                stream.forward(layer, which)
+
+        @pl.when(other == 0)
+        def _():
+            stream.load(n, unit, 1, w_in_v, w_out_v, 1, load_sem)
+
+        @pl.when((other == 1) & (unit < 3))
+        def _():
+            stream.arrive(n, unit + 1)
+            stream.load(n, unit + 1, 0, w_in_v, w_out_v, 0, load_sem)
+
+        @pl.when((step == chunks - 1) & more)
+        def _():
+            stream.arrive(n + 1, 0)
+            stream.load(n + 1, 0, 0, w_in_v, w_out_v, 0, load_sem)
+
+        stream.loaded(w_in_v, w_out_v, v, load_sem)
+
+        @pl.when(step < chunks - 1)
+        def _():
+            compute(v, False)
+
+        @pl.when(step == chunks - 1)
+        def _():
+            @pl.when(n > 0)
+            def _():
+                save(n - 1).wait()
+
+            compute(v, True)
+            save(n).start()
+
+        for condition, layer, which in sends:
+
+            @pl.when(condition)
+            def _():
+                stream.forward_sent(layer, which)
+
+    def layer_step(n, carry):
+        lax.fori_loop(0, chunks, lambda step, c: (chunk_step(n, step), c)[1], 0)
+        return carry
+
+    lax.fori_loop(0, layers, layer_step, 0)
+    save(layers - 1).wait()
+
+
+def stream_semaphores():
+    dma = pltpu.SemaphoreType.DMA
+    return [dma((3, 4)), dma((2, 3, 4)), dma((3,)), dma((2, 3)), dma((4, 4)), dma((2, 4, 4)), dma((4,)), dma((2, 4))]
+
+
+def stream_buffers(own_in, own_out):
+    piece_in, piece_out = own_in.shape[1:], own_out.shape[1:]
+    return [
+        jax.ShapeDtypeStruct((2, 2) + piece_in, BF16),
+        jax.ShapeDtypeStruct((2, 2) + piece_out, BF16),
+        jax.ShapeDtypeStruct((2, CHIPS) + piece_in, BF16),
+        jax.ShapeDtypeStruct((2, CHIPS) + piece_out, BF16),
+    ]
+
+
+def forward_stack(x_rows, own_in, own_out):
+    layers = own_in.shape[0]
+    tokens, width = x_rows.shape
+    blocks_f, blocks_d = own_in.shape[1], own_out.shape[1]
+    chunk_blocks, chunk = blocks_f // SHARDS, own_out.shape[2]
+    anywhere = pl.BlockSpec(memory_space=pl.ANY)
+    shapes = [
+        jax.ShapeDtypeStruct((layers, tokens, width), BF16),
+        jax.ShapeDtypeStruct(own_in.shape, BF16),
+        jax.ShapeDtypeStruct(own_out.shape, BF16),
+    ] + stream_buffers(own_in, own_out)
+    flops = 4 * layers * tokens * width * blocks_f * LANES
+    outs = pl.pallas_call(
+        functools.partial(forward_stack_kernel, layers),
+        in_specs=[anywhere] * 3,
+        out_specs=[anywhere] * len(shapes),
+        out_shape=shapes,
+        scratch_shapes=[
+            pltpu.VMEM((tokens, width), BF16),
+            pltpu.VMEM((blocks_d, tokens, LANES), BF16),
+            pltpu.VMEM((tokens, width), F32),
+            pltpu.VMEM((2, chunk_blocks, width, LANES), BF16),
+            pltpu.VMEM((2, blocks_d, chunk, LANES), BF16),
+            pltpu.SemaphoreType.DMA,
+            pltpu.SemaphoreType.DMA((2, 2 * CHIPS + 1)),
+            pltpu.SemaphoreType.REGULAR((CHIPS,)),
+        ]
+        + stream_semaphores(),
+        compiler_params=pltpu.CompilerParams(vmem_limit_bytes=VMEM_LIMIT, collective_id=0, has_side_effects=True),
+        cost_estimate=pl.CostEstimate(flops=flops, bytes_accessed=100_000_000, transcendentals=0),
+        name="forward_stack",
+    )(x_rows, own_in, own_out)
+    return outs[0], outs[1], outs[2]
 
 
 def solution(mesh):
@@ -311,12 +625,10 @@
         chip_x, chip_y = chip % 2, chip // 2
         mine, other = jnp.reshape(core, (1,)), jnp.reshape(1 - core, (1,))
 
-        seq = [2 * (i // 2) + (core if i % 2 == 0 else 1 - core) for i in range(SHARDS)]
-        order_fwd = jnp.stack([jnp.stack(seq), jnp.stack(seq)]).astype(jnp.int32)
-        fwd_list = [(i % 2, i // 2) for i in range(SHARDS)]
         bwd_list = [(0, 0), (0, 1), (2, 0), (2, 1), (1, 0), (1, 1), (3, 0), (3, 1)]
-        in_chips = [2 * chip_y, 2 * chip_y + 1, 2 - 2 * chip_y, 3 - 2 * chip_y]
-        out_chips = [chip_x, chip_x + 2, 1 - chip_x, 3 - chip_x]
+        across = [chip, chip_y * 2 + 1 - chip_x, 2 - chip_y * 2 + chip_x, 3 - chip]
+        in_chips = [across[0], across[1], across[2], across[3]]
+        out_chips = [across[0], across[2], across[1], across[3]]
 
         def bwd_seq(chips):
             kept, got = chips[:2], chips[2:]
@@ -326,36 +638,14 @@
 
         order_bwd = jnp.stack([bwd_seq(in_chips), bwd_seq(out_chips)]).astype(jnp.int32)
 
-        def gather(n, after):
-            own_in, own_out = to_lanes(w_in_part[n]), to_lanes(w_out_part[n])
-            if after is not None:
-                own_in, own_out, _ = lax.optimization_barrier((own_in, own_out, after))
-            half_in = lax.all_gather(own_in, "local")
-            half_out = lax.all_gather(own_out, "local")
-            return half_in, half_out
-
-        saved_x, kept_in, kept_out = [], [], []
-        x_cur = x_rows
-        halves = gather(0, None)
-        for n in range(layers):
-            half_in, half_out = halves
-            twin_in = lax.ppermute(half_in, "data", swap_cores)
-            twin_out = lax.ppermute(half_out, "data", swap_cores)
-            saved_x.append(x_cur)
-            if n + 1 < layers:
-                halves = gather(n + 1, half_in)
-            keep_in = lax.dynamic_slice_in_dim(half_in, 2 * chip_y, 2, 0)
-            pair_out = half_out.reshape((2, 2) + half_out.shape[1:])
-            keep_out = lax.dynamic_slice_in_dim(pair_out, chip_x, 1, 1)[:, 0]
-            (x_next,) = layer_call(
-                forward_kernel, order_fwd, [x_cur], Pieces([half_in, twin_in], fwd_list), Pieces([half_out, twin_out], fwd_list), ["rows"], 2
+        own_in = w_in_part.reshape(w_in_part.shape[:2] + (-1, LANES)).transpose(0, 2, 1, 3)
+        own_out = w_out_part.reshape(w_out_part.shape[:2] + (-1, LANES)).transpose(0, 2, 1, 3)
+        xs, kept_in, kept_out = forward_stack(x_rows, own_in, own_out)
+
+        def exchange(n, grad_cur):
+            keep_in, keep_out, grad_cur = lax.optimization_barrier(
+                (jnp.stack([own_in[n], kept_in[n]]), jnp.stack([own_out[n], kept_out[n]]), grad_cur)
             )
-            x_cur, keep_in, keep_out = lax.optimization_barrier((x_next, keep_in, keep_out))
-            kept_in.append(keep_in)
-            kept_out.append(keep_out)
-
-        def exchange(n, grad_cur):
-            keep_in, keep_out, grad_cur = lax.optimization_barrier((kept_in[n], kept_out[n], grad_cur))
             got_in = lax.ppermute(keep_in, "local", swap_y)
             got_out = lax.ppermute(keep_out, "local", swap_x)
             twin_in = lax.ppermute(keep_in, "data", swap_cores)
@@ -376,7 +666,7 @@
             unit, hidden, dpre, grad_next = layer_call(
                 backward_kernel,
                 order_bwd,
-                [saved_x[n], grad_cur],
+                [(xs, n - 1) if n else (x_rows[None], 0), (grad_cur[None], 0)],
                 Pieces(in_arrays, bwd_list),
                 Pieces(out_arrays, bwd_list),
                 [x_rows.shape[1], w_out_part.shape[1] * SHARDS, w_out_part.shape[1] * SHARDS, "rows"],
@@ -397,7 +687,7 @@
                 grad_next, grad_out_half, grad_in_half = lax.optimization_barrier((grad_next, grad_out_half, grad_in_half))
             grads_in[n], grads_out[n], grad_cur = grad_in_half, grad_out_half, grad_next
         reduce(grads_in, grads_out, 0)
-        return x_cur, jnp.stack(grads_in), jnp.stack(grads_out), grad_cur
+        return xs[layers - 1], jnp.stack(grads_in), jnp.stack(grads_out), grad_cur
 
     def reduce(grads_in, grads_out, n):
         grads_out[n] = lax.psum_scatter(grads_out[n], "local", scatter_dimension=0, tiled=True)

time: 2770 us -> 2680 us (0.968)
  waiting for transfers between devices: 1120 us -> 897 us
  Pallas kernels: 1490 us -> 1640 us
    pallas_call x0 -> x1, Pallas kernels: none -> 539 us  [forward_stack(): pl.pallas_call(functools.partial(forward_stack_kernel, layers), in_specs=...]
    pallas_call x10 -> x5, Pallas kernels: 1000 us -> 602 us  [layer_call(): pl.pallas_call(functools.partial(kernel, (w_in, w_out)), grid_spec=pltpu....]
    all_gather x10 -> x0, waiting for transfers between devices: 218 us -> none  [the longest x5 130 us: gather(): half_in = lax.all_gather(own_in, 'local')]
  transfers between devices with their start and end apart: 70 -> 50, of which waited for: 30 -> 23; matrix products, arithmetic and copies ran while one was open for 3% -> 2% of each run, Pallas kernels for 24% -> 13%
where the time goes in v3:
time: 2680 us; the launch traced here: 2670 us
  Pallas kernels  1640 us (61%)
  waiting for transfers between devices  897 us (33%)
  local copies, waits for them, and re-layouts  84.1 us (3%)
    pallas_call x5, Pallas kernels, layer_call(): pl.pallas_call(functools.partial(kernel, (w_in, w_out)), grid_spec=pltpu....  602 us
    pallas_call x1, Pallas kernels, forward_stack(): pl.pallas_call(functools.partial(forward_stack_kernel, layers), in_specs=...  539 us
    reduce_scatter x5, waiting for transfers between devices, reduce(): lax.psum_scatter(grads_in[n], 'local', scatter_dimension=0, tiled=True)  404 us
    reduce_scatter x5, waiting for transfers between devices, reduce(): lax.psum_scatter(grads_out[n], 'local', scatter_dimension=0, tiled=True)  324 us
    pallas_call x10, Pallas kernels, grad_w_in_half(): pl.pallas_call(functools.partial(weight_grad_kernel, True), grid_spec=plt...  250 us
    pallas_call x10, Pallas kernels, grad_w_out_half(): pl.pallas_call(functools.partial(weight_grad_kernel, False), grid_spec=pl...  245 us
    ppermute x5, waiting for transfers between devices, exchange(): got_in = lax.ppermute(keep_in, 'local', swap_y)  128 us
  transfers between devices with their start and end apart: 50, of which 23 were waited for; matrix products, arithmetic and copies ran while one was open for 2% of the time, Pallas kernels for 13%

profile of v3, /device:TPU:0, one launch (start us, length us, event | category | flops | bytes accessed | tf_op | source)
XLA Modules:
  0.0 2667.8 jit_solution(18039252578327796911)
XLA Ops:
  38.7 538.6 %forward_stack.1 = (bf16[5,4096,1024]{2,1,0:T(8,128)(2,1)}, bf16[5,32,128,128]{3,2,1,0:T(8,128)(2,1)}, bf16[5,8,512,128]{3,2,1,0:T(8,128)(2,1)}, bf16[2,2,32,128...) custom-call(bf16[4096,1024]{1,0:T(8,128)(2,1)} %x_ref.1, ...), custom_call_target="tpu_custom_call" | custom-call | flops 343597383680 | bytes 100000000 | tf_op jit(solution)/shard_map/forward_stack/pallas_call | solution.py:591
  595.7 44.5 %collective-permute-done.refs_1_ = bf16[2,32,128,128]{3,2,1,0:T(8,128)(2,1)} collective-permute-done((bf16[2,32,128,128]{3,2,1,0:T(8,128)(2,1)}, bf16[2,32,128,128]{3,2,1,0:T(8,128)(2,1)}, u32[]{:S(2)}, u32[]{:S(2)}) %collective-permute-start) | collective-permute-done | bytes 2097184 | tf_op jit(solution)/shard_map/ppermute | solution.py:649
  647.7 120.2 %shard_map.75 = (bf16[8,4096,128]{2,1,0:T(8,128)(2,1)}, bf16[32,4096,128]{2,1,0:T(8,128)(2,1)}, bf16[32,4096,128]{2,1,0:T(8,128)(2,1)}, bf16[4096,1024]{1,0:T(8,128)(2,1)}) custom-call(s32[2,8]{1,0:T(2,128)} %pad_add_fusion.order_ref, bf16[5,4096,1024]{2,1,0:T(8,128)(2,1)} %get-tuple-element.66.x_ref, bf16[1,4096,1024]{2,1,0:T(8,128)(2,1)} %bitcast.62, ...), custom_call_target="tpu_custom_call" | custom-call | flops 103079215104 | bytes 117440512 | tf_op jit(solution)/shard_map/pallas_call | solution.py:166
  792.1 24.2 grad_w_in_half.10
  822.6 24.7 grad_w_out_half.11
  869.5 25.4 grad_w_in_half.11
  895.0 120.6 %shard_map.76 = (bf16[8,4096,128]{2,1,0:T(8,128)(2,1)}, bf16[32,4096,128]{2,1,0:T(8,128)(2,1)}, bf16[32,4096,128]{2,1,0:T(8,128)(2,1)}, bf16[4096,1024]{1,0:T(8,128)(2,1)}) custom-call(s32[2,8]{1,0:T(2,128)} %pad_add_fusion.order_ref, bf16[5,4096,1024]{2,1,0:T(8,128)(2,1)} %get-tuple-element.66.x_ref, bf16[1,4096,1024]{2,1,0:T(8,128)(2,1)} %bitcast.76, ...), custom_call_target="tpu_custom_call" | custom-call | flops 103079215104 | bytes 117440512 | tf_op jit(solution)/shard_map/pallas_call | solution.py:166
  1039.8 24.2 grad_w_in_half.12
  1071.2 24.9 grad_w_out_half.13
  1118.5 25.4 grad_w_in_half.13
  1144.0 120.4 %shard_map.77 = (bf16[8,4096,128]{2,1,0:T(8,128)(2,1)}, bf16[32,4096,128]{2,1,0:T(8,128)(2,1)}, bf16[32,4096,128]{2,1,0:T(8,128)(2,1)}, bf16[4096,1024]{1,0:T(8,128)(2,1)}) custom-call(s32[2,8]{1,0:T(2,128)} %pad_add_fusion.order_ref, bf16[5,4096,1024]{2,1,0:T(8,128)(2,1)} %get-tuple-element.66.x_ref, bf16[1,4096,1024]{2,1,0:T(8,128)(2,1)} %bitcast.75, ...), custom_call_target="tpu_custom_call" | custom-call | flops 103079215104 | bytes 117440512 | tf_op jit(solution)/shard_map/pallas_call | solution.py:166
  1264.4 24.2 grad_w_out_half.14
  1288.6 24.2 grad_w_in_half.14
  1319.1 24.9 grad_w_out_half.15
  1366.0 25.4 grad_w_in_half.15
  1391.5 120.6 %shard_map.78 = (bf16[8,4096,128]{2,1,0:T(8,128)(2,1)}, bf16[32,4096,128]{2,1,0:T(8,128)(2,1)}, bf16[32,4096,128]{2,1,0:T(8,128)(2,1)}, bf16[4096,1024]{1,0:T(8,128)(2,1)}) custom-call(s32[2,8]{1,0:T(2,128)} %pad_add_fusion.order_ref, bf16[5,4096,1024]{2,1,0:T(8,128)(2,1)} %get-tuple-element.66.x_ref, bf16[1,4096,1024]{2,1,0:T(8,128)(2,1)} %bitcast.74, ...), custom_call_target="tpu_custom_call" | custom-call | flops 103079215104 | bytes 117440512 | tf_op jit(solution)/shard_map/pallas_call | solution.py:166
  1536.2 24.2 grad_w_in_half.16
  1567.7 24.7 grad_w_out_half.17
  1615.0 25.4 grad_w_in_half.17
  1640.4 120.5 %shard_map.79 = (bf16[8,4096,128]{2,1,0:T(8,128)(2,1)}, bf16[32,4096,128]{2,1,0:T(8,128)(2,1)}, bf16[32,4096,128]{2,1,0:T(8,128)(2,1)}, bf16[4096,1024]{1,0:T(8,128)(2,1)}) custom-call(s32[2,8]{1,0:T(2,128)} %pad_add_fusion.order_ref, bf16[1,4096,1024]{2,1,0:T(8,128)(2,1)} %bitcast.63, bf16[1,4096,1024]{2,1,0:T(8,128)(2,1)} %bitcast.77, ...), custom_call_target="tpu_custom_call" | custom-call | flops 103079215104 | bytes 117440512 | tf_op jit(solution)/shard_map/pallas_call | solution.py:166
  1798.5 24.7 grad_w_out_half.19
  1825.4 25.4 grad_w_in_half.18
  1864.3 26.4 grad_w_in_half.19
  1906.3 80.6 %reduce-scatter.23.cloned.1.call-done = f32[512,1024]{1,0:T(8,128)} async-done(((f32[2048,1024]{1,0:T(8,128)}), f32[512,1024]{1,0:T(8,128)}) %reduce-scatter.23.cloned.1.call-update) | async-done | bytes 2097168 | tf_op jit(solution)/shard_map/reduce_scatter | solution.py:693
  1990.1 80.7 %reduce-scatter.25.cloned.1.call-done = f32[512,1024]{1,0:T(8,128)} async-done(((f32[2048,1024]{1,0:T(8,128)}), f32[512,1024]{1,0:T(8,128)}) %reduce-scatter.25.cloned.1.call-update) | async-done | bytes 2097168 | tf_op jit(solution)/shard_map/reduce_scatter | solution.py:693
  2073.9 80.5 %reduce-scatter.27.cloned.1.call-done = f32[512,1024]{1,0:T(8,128)} async-done(((f32[2048,1024]{1,0:T(8,128)}), f32[512,1024]{1,0:T(8,128)}) %reduce-scatter.27.cloned.1.call-update) | async-done | bytes 2097168 | tf_op jit(solution)/shard_map/reduce_scatter | solution.py:693
  2157.6 81.1 %reduce-scatter.11.cloned.1.call-done = f32[128,4096]{1,0:T(8,128)} async-done(((f32[512,4096]{1,0:T(8,128)}), f32[128,4096]{1,0:T(8,128)}) %reduce-scatter.11.cloned.1.call-update) | async-done | bytes 2097168 | tf_op jit(solution)/shard_map/reduce_scatter | solution.py:694
  2241.7 80.5 %reduce-scatter.13.cloned.1.call-done = f32[128,4096]{1,0:T(8,128)} async-done(((f32[512,4096]{1,0:T(8,128)}), f32[128,4096]{1,0:T(8,128)}) %reduce-scatter.13.cloned.1.call-update) | async-done | bytes 2097168 | tf_op jit(solution)/shard_map/reduce_scatter | solution.py:694
  2325.4 80.7 %reduce-scatter.15.cloned.1.call-done = f32[128,4096]{1,0:T(8,128)} async-done(((f32[512,4096]{1,0:T(8,128)}), f32[128,4096]{1,0:T(8,128)}) %reduce-scatter.15.cloned.1.call-update) | async-done | bytes 2097168 | tf_op jit(solution)/shard_map/reduce_scatter | solution.py:694
  2409.2 80.7 %reduce-scatter.17.cloned.1.call-done = f32[128,4096]{1,0:T(8,128)} async-done(((f32[512,4096]{1,0:T(8,128)}), f32[128,4096]{1,0:T(8,128)}) %reduce-scatter.17.cloned.1.call-update) | async-done | bytes 2097168 | tf_op jit(solution)/shard_map/reduce_scatter | solution.py:694
  2493.0 80.7 %reduce-scatter.19.cloned.1.call-done = f32[128,4096]{1,0:T(8,128)} async-done(((f32[512,4096]{1,0:T(8,128)}), f32[128,4096]{1,0:T(8,128)}) %reduce-scatter.19.cloned.1.call-update) | async-done | bytes 2097168 | tf_op jit(solution)/shard_map/reduce_scatter | solution.py:694
  2576.8 80.5 %reduce-scatter.29.cloned.1.call-done = f32[512,1024]{1,0:T(8,128)} async-done(((f32[2048,1024]{1,0:T(8,128)}), f32[512,1024]{1,0:T(8,128)}) %reduce-scatter.29.cloned.1.call-update) | async-done | bytes 2097168 | tf_op jit(solution)/shard_map/reduce_scatter | solution.py:693
  (168 shorter events, 343.2 us)
Async XLA Ops:
  7.2 1896.0 %reduce-scatter.21.cloned.1.call-start = ((), (), s32[]{:S(2)}) async-start(), calls=%async_computation.15 | async-start | bytes 10485760 | tf_op jit(solution)/shard_map/reduce_scatter | solution.py:693
  593.5 46.7 %collective-permute-start = (bf16[2,32,128,128]{3,2,1,0:T(8,128)(2,1)}, bf16[2,32,128,128]{3,2,1,0:T(8,128)(2,1)}, u32[]{:S(2)}, u32[]{:S(2)}) collective-permute-start(bf16[2,32,128,128]{3,2,1,0:T(8,128)(2,1)} %pad_maximum_fusion.8.refs_0_), channel_id=1, source_target_pairs={{0,4},{2,6},{4,0},{6,2},{1,5},{3,7},{5,1},{7,3}} | collective-permute-start | bytes 6291464 | tf_op jit(solution)/shard_map/ppermute | solution.py:649
  595.2 46.2 %collective-permute-start.1 = (bf16[2,32,128,128]{3,2,1,0:T(8,128)(2,1)}, bf16[2,32,128,128]{3,2,1,0:T(8,128)(2,1)}, u32[]{:S(2)}, u32[]{:S(2)}) collective-permute-start(bf16[2,32,128,128]{3,2,1,0:T(8,128)(2,1)} %pad_maximum_fusion.8.refs_0_), channel_id=1, source_target_pairs={{0,1},{1,0},{2,3},{3,2},{4,5},{5,4},{6,7},{7,6}} | collective-permute-start | bytes 6291464 | tf_op jit(solution)/shard_map/ppermute | solution.py:651
  816.3 53.2 %collective-permute-start.9 = (f32[512,4096]{1,0:T(8,128)}, f32[512,4096]{1,0:T(8,128)}, u32[]{:S(2)}, u32[]{:S(2)}) collective-permute-start(f32[512,4096]{1,0:T(8,128)} %grad_w_in_half.10), channel_id=1, source_target_pairs={{0,1},{1,0},{2,3},{3,2},{4,5},{5,4},{6,7},{7,6}} | collective-permute-start | bytes 25165832 | tf_op jit(solution)/shard_map/ppermute | solution.py:680
  821.0 47.9 %collective-permute-start.6 = (bf16[2,32,128,128]{3,2,1,0:T(8,128)(2,1)}, bf16[2,32,128,128]{3,2,1,0:T(8,128)(2,1)S(1)}, u32[]{:S(2)}, u32[]{:S(2)}) collective-permute-start(bf16[2,32,128,128]{3,2,1,0:T(8,128)(2,1)} %pad_maximum_fusion.6.refs_0_), channel_id=1, source_target_pairs={{0,4},{2,6},{4,0},{6,2},{1,5},{3,7},{5,1},{7,3}} | collective-permute-start | bytes 6291464 | tf_op jit(solution)/shard_map/ppermute | solution.py:649
  821.3 47.7 %collective-permute-start.7 = (bf16[2,8,512,128]{3,2,1,0:T(8,128)(2,1)}, bf16[2,8,512,128]{3,2,1,0:T(8,128)(2,1)}, u32[]{:S(2)}, u32[]{:S(2)}) collective-permute-start(bf16[2,8,512,128]{3,2,1,0:T(8,128)(2,1)} %pad_maximum_fusion.7.refs_4_), channel_id=1, source_target_pairs={{0,2},{2,0},{4,6},{6,4},{1,3},{3,1},{5,7},{7,5}} | collective-permute-start | bytes 6291464 | tf_op jit(solution)/shard_map/ppermute | solution.py:650
  822.1 72.9 %collective-permute-start.10 = (bf16[2,32,128,128]{3,2,1,0:T(8,128)(2,1)}, bf16[2,32,128,128]{3,2,1,0:T(8,128)(2,1)}, u32[]{:S(2)}, u32[]{:S(2)}) collective-permute-start(bf16[2,32,128,128]{3,2,1,0:T(8,128)(2,1)} %pad_maximum_fusion.6.refs_0_), channel_id=1, source_target_pairs={{0,1},{1,0},{2,3},{3,2},{4,5},{5,4},{6,7},{7,6}} | collective-permute-start | bytes 6291464 | tf_op jit(solution)/shard_map/ppermute | solution.py:651
  822.1 72.9 %collective-permute-start.12 = (bf16[2,8,512,128]{3,2,1,0:T(8,128)(2,1)}, bf16[2,8,512,128]{3,2,1,0:T(8,128)(2,1)}, u32[]{:S(2)}, u32[]{:S(2)}) collective-permute-start(bf16[2,8,512,128]{3,2,1,0:T(8,128)(2,1)} %pad_maximum_fusion.7.refs_4_), channel_id=1, source_target_pairs={{0,1},{1,0},{2,3},{3,2},{4,5},{5,4},{6,7},{7,6}} | collective-permute-start | bytes 6291464 | tf_op jit(solution)/shard_map/ppermute | solution.py:652
  1064.0 54.5 %collective-permute-start.17 = (f32[512,4096]{1,0:T(8,128)}, f32[512,4096]{1,0:T(8,128)}, u32[]{:S(2)}, u32[]{:S(2)}) collective-permute-start(f32[512,4096]{1,0:T(8,128)} %grad_w_in_half.12), channel_id=1, source_target_pairs={{0,1},{1,0},{2,3},{3,2},{4,5},{5,4},{6,7},{7,6}} | collective-permute-start | bytes 25165832 | tf_op jit(solution)/shard_map/ppermute | solution.py:680
  1068.8 47.8 %collective-permute-start.14 = (bf16[2,32,128,128]{3,2,1,0:T(8,128)(2,1)}, bf16[2,32,128,128]{3,2,1,0:T(8,128)(2,1)S(1)}, u32[]{:S(2)}, u32[]{:S(2)}) collective-permute-start(bf16[2,32,128,128]{3,2,1,0:T(8,128)(2,1)} %pad_maximum_fusion.4.refs_0_), channel_id=1, source_target_pairs={{0,4},{2,6},{4,0},{6,2},{1,5},{3,7},{5,1},{7,3}} | collective-permute-start | bytes 6291464 | tf_op jit(solution)/shard_map/ppermute | solution.py:649
  1070.4 47.6 %collective-permute-start.15 = (bf16[2,8,512,128]{3,2,1,0:T(8,128)(2,1)}, bf16[2,8,512,128]{3,2,1,0:T(8,128)(2,1)}, u32[]{:S(2)}, u32[]{:S(2)}) collective-permute-start(bf16[2,8,512,128]{3,2,1,0:T(8,128)(2,1)} %pad_maximum_fusion.5.refs_4_), channel_id=1, source_target_pairs={{0,2},{2,0},{4,6},{6,4},{1,3},{3,1},{5,7},{7,5}} | collective-permute-start | bytes 6291464 | tf_op jit(solution)/shard_map/ppermute | solution.py:650
  1070.7 73.3 %collective-permute-start.18 = (bf16[2,32,128,128]{3,2,1,0:T(8,128)(2,1)}, bf16[2,32,128,128]{3,2,1,0:T(8,128)(2,1)}, u32[]{:S(2)}, u32[]{:S(2)}) collective-permute-start(bf16[2,32,128,128]{3,2,1,0:T(8,128)(2,1)} %pad_maximum_fusion.4.refs_0_), channel_id=1, source_target_pairs={{0,1},{1,0},{2,3},{3,2},{4,5},{5,4},{6,7},{7,6}} | collective-permute-start | bytes 6291464 | tf_op jit(solution)/shard_map/ppermute | solution.py:651
  1070.7 73.3 %collective-permute-start.20 = (bf16[2,8,512,128]{3,2,1,0:T(8,128)(2,1)}, bf16[2,8,512,128]{3,2,1,0:T(8,128)(2,1)}, u32[]{:S(2)}, u32[]{:S(2)}) collective-permute-start(bf16[2,8,512,128]{3,2,1,0:T(8,128)(2,1)} %pad_maximum_fusion.5.refs_4_), channel_id=1, source_target_pairs={{0,1},{1,0},{2,3},{3,2},{4,5},{5,4},{6,7},{7,6}} | collective-permute-start | bytes 6291464 | tf_op jit(solution)/shard_map/ppermute | solution.py:652
  1312.8 53.2 %collective-permute-start.25 = (f32[512,4096]{1,0:T(8,128)}, f32[512,4096]{1,0:T(8,128)}, u32[]{:S(2)}, u32[]{:S(2)}) collective-permute-start(f32[512,4096]{1,0:T(8,128)} %grad_w_in_half.14), channel_id=1, source_target_pairs={{0,1},{1,0},{2,3},{3,2},{4,5},{5,4},{6,7},{7,6}} | collective-permute-start | bytes 25165832 | tf_op jit(solution)/shard_map/ppermute | solution.py:680
  1317.6 47.8 %collective-permute-start.22 = (bf16[2,32,128,128]{3,2,1,0:T(8,128)(2,1)}, bf16[2,32,128,128]{3,2,1,0:T(8,128)(2,1)S(1)}, u32[]{:S(2)}, u32[]{:S(2)}) collective-permute-start(bf16[2,32,128,128]{3,2,1,0:T(8,128)(2,1)} %pad_maximum_fusion.2.refs_0_), channel_id=1, source_target_pairs={{0,4},{2,6},{4,0},{6,2},{1,5},{3,7},{5,1},{7,3}} | collective-permute-start | bytes 6291464 | tf_op jit(solution)/shard_map/ppermute | solution.py:649
  1317.9 47.6 %collective-permute-start.23 = (bf16[2,8,512,128]{3,2,1,0:T(8,128)(2,1)}, bf16[2,8,512,128]{3,2,1,0:T(8,128)(2,1)}, u32[]{:S(2)}, u32[]{:S(2)}) collective-permute-start(bf16[2,8,512,128]{3,2,1,0:T(8,128)(2,1)} %pad_maximum_fusion.3.refs_4_), channel_id=1, source_target_pairs={{0,2},{2,0},{4,6},{6,4},{1,3},{3,1},{5,7},{7,5}} | collective-permute-start | bytes 6291464 | tf_op jit(solution)/shard_map/ppermute | solution.py:650
  1318.6 72.9 %collective-permute-start.26 = (bf16[2,32,128,128]{3,2,1,0:T(8,128)(2,1)}, bf16[2,32,128,128]{3,2,1,0:T(8,128)(2,1)}, u32[]{:S(2)}, u32[]{:S(2)}) collective-permute-start(bf16[2,32,128,128]{3,2,1,0:T(8,128)(2,1)} %pad_maximum_fusion.2.refs_0_), channel_id=1, source_target_pairs={{0,1},{1,0},{2,3},{3,2},{4,5},{5,4},{6,7},{7,6}} | collective-permute-start | bytes 6291464 | tf_op jit(solution)/shard_map/ppermute | solution.py:651
  1318.6 72.9 %collective-permute-start.28 = (bf16[2,8,512,128]{3,2,1,0:T(8,128)(2,1)}, bf16[2,8,512,128]{3,2,1,0:T(8,128)(2,1)}, u32[]{:S(2)}, u32[]{:S(2)}) collective-permute-start(bf16[2,8,512,128]{3,2,1,0:T(8,128)(2,1)} %pad_maximum_fusion.3.refs_4_), channel_id=1, source_target_pairs={{0,1},{1,0},{2,3},{3,2},{4,5},{5,4},{6,7},{7,6}} | collective-permute-start | bytes 6291464 | tf_op jit(solution)/shard_map/ppermute | solution.py:652
  1560.4 54.5 %collective-permute-start.33 = (f32[512,4096]{1,0:T(8,128)}, f32[512,4096]{1,0:T(8,128)}, u32[]{:S(2)}, u32[]{:S(2)}) collective-permute-start(f32[512,4096]{1,0:T(8,128)} %grad_w_in_half.16), channel_id=1, source_target_pairs={{0,1},{1,0},{2,3},{3,2},{4,5},{5,4},{6,7},{7,6}} | collective-permute-start | bytes 25165832 | tf_op jit(solution)/shard_map/ppermute | solution.py:680
  1565.2 47.8 %collective-permute-start.30 = (bf16[2,32,128,128]{3,2,1,0:T(8,128)(2,1)}, bf16[2,32,128,128]{3,2,1,0:T(8,128)(2,1)S(1)}, u32[]{:S(2)}, u32[]{:S(2)}) collective-permute-start(bf16[2,32,128,128]{3,2,1,0:T(8,128)(2,1)} %pad_maximum_fusion.refs_0_), channel_id=1, source_target_pairs={{0,4},{2,6},{4,0},{6,2},{1,5},{3,7},{5,1},{7,3}} | collective-permute-start | bytes 6291464 | tf_op jit(solution)/shard_map/ppermute | solution.py:649
  1566.9 47.6 %collective-permute-start.31 = (bf16[2,8,512,128]{3,2,1,0:T(8,128)(2,1)}, bf16[2,8,512,128]{3,2,1,0:T(8,128)(2,1)}, u32[]{:S(2)}, u32[]{:S(2)}) collective-permute-start(bf16[2,8,512,128]{3,2,1,0:T(8,128)(2,1)} %pad_maximum_fusion.1.refs_4_), channel_id=1, source_target_pairs={{0,2},{2,0},{4,6},{6,4},{1,3},{3,1},{5,7},{7,5}} | collective-permute-start | bytes 6291464 | tf_op jit(solution)/shard_map/ppermute | solution.py:650
  1567.2 73.2 %collective-permute-start.34 = (bf16[2,32,128,128]{3,2,1,0:T(8,128)(2,1)}, bf16[2,32,128,128]{3,2,1,0:T(8,128)(2,1)}, u32[]{:S(2)}, u32[]{:S(2)}) collective-permute-start(bf16[2,32,128,128]{3,2,1,0:T(8,128)(2,1)} %pad_maximum_fusion.refs_0_), channel_id=1, source_target_pairs={{0,1},{1,0},{2,3},{3,2},{4,5},{5,4},{6,7},{7,6}} | collective-permute-start | bytes 6291464 | tf_op jit(solution)/shard_map/ppermute | solution.py:651
  1567.2 73.2 %collective-permute-start.36 = (bf16[2,8,512,128]{3,2,1,0:T(8,128)(2,1)}, bf16[2,8,512,128]{3,2,1,0:T(8,128)(2,1)}, u32[]{:S(2)}, u32[]{:S(2)}) collective-permute-start(bf16[2,8,512,128]{3,2,1,0:T(8,128)(2,1)} %pad_maximum_fusion.1.refs_4_), channel_id=1, source_target_pairs={{0,1},{1,0},{2,3},{3,2},{4,5},{5,4},{6,7},{7,6}} | collective-permute-start | bytes 6291464 | tf_op jit(solution)/shard_map/ppermute | solution.py:652
  1823.2 163.7 %reduce-scatter.23.cloned.1.call-start = ((), (), s32[]{:S(2)}) async-start(), calls=%async_computation.16 | async-start | bytes 10485760 | tf_op jit(solution)/shard_map/reduce_scatter | solution.py:693
  1824.0 246.8 %reduce-scatter.25.cloned.1.call-start = ((), (), s32[]{:S(2)}) async-start(), calls=%async_computation.17 | async-start | bytes 10485760 | tf_op jit(solution)/shard_map/reduce_scatter | solution.py:693
  1824.7 329.7 %reduce-scatter.27.cloned.1.call-start = ((), (), s32[]{:S(2)}) async-start(), calls=%async_computation.18 | async-start | bytes 10485760 | tf_op jit(solution)/shard_map/reduce_scatter | solution.py:693
  1825.3 413.3 %reduce-scatter.11.cloned.1.call-start = ((), (), s32[]{:S(2)}) async-start(), calls=%async_computation.10 | async-start | bytes 10485760 | tf_op jit(solution)/shard_map/reduce_scatter | solution.py:694
  1890.7 431.6 %reduce-scatter.13.cloned.1.call-start = ((), (), s32[]{:S(2)}) async-start(), calls=%async_computation.11 | async-start | bytes 10485760 | tf_op jit(solution)/shard_map/reduce_scatter | solution.py:694
  1891.3 514.8 %reduce-scatter.15.cloned.1.call-start = ((), (), s32[]{:S(2)}) async-start(), calls=%async_computation.12 | async-start | bytes 10485760 | tf_op jit(solution)/shard_map/reduce_scatter | solution.py:694
  1892.0 597.8 %reduce-scatter.17.cloned.1.call-start = ((), (), s32[]{:S(2)}) async-start(), calls=%async_computation.13 | async-start | bytes 10485760 | tf_op jit(solution)/shard_map/reduce_scatter | solution.py:694
  1892.8 680.9 %reduce-scatter.19.cloned.1.call-start = ((), (), s32[]{:S(2)}) async-start(), calls=%async_computation.14 | async-start | bytes 10485760 | tf_op jit(solution)/shard_map/reduce_scatter | solution.py:694
  1893.5 763.8 %reduce-scatter.29.cloned.1.call-start = ((), (), s32[]{:S(2)}) async-start(), calls=%async_computation.19 | async-start | bytes 10485760 | tf_op jit(solution)/shard_map/reduce_scatter | solution.py:693
  (35 other events, 863.0 us)
Sparse Core Ops, SparseCore 0:
  1823.4 79.7 reduce-scatter.20
  1906.2 80.7 reduce-scatter.22
  1990.0 80.7 reduce-scatter.24
  2073.6 80.7 reduce-scatter.26
  2157.8 80.7 reduce-scatter.10
  2241.5 80.7 reduce-scatter.12
  2325.3 80.7 reduce-scatter.14
  2409.1 80.7 reduce-scatter.16
  2492.9 80.7 reduce-scatter.18
  2576.5 80.7 reduce-scatter.28

commit v4 on v0

v4 whole, which is shorter than its diff:
```python
import functools

import jax
import jax.numpy as jnp
from jax import lax
from jax.experimental import pallas as pl
from jax.experimental.pallas import tpu as pltpu
from jax.sharding import PartitionSpec as P

NORM_EPS = 1e-6
GELU_A = 0.7978845608028654
GELU_B = GELU_A * 0.044715
LAST_LAST = (((1,), (1,)), ((), ()))
FIRST_FIRST = (((0,), (0,)), ((), ()))
BF16 = jnp.bfloat16
F32 = jnp.float32
MESH = pl.DeviceIdType.MESH

CHIPS = 4
SHARDS = 8
LANES = 128
TOK_TILE = 256
VMEM_LIMIT = 67_000_000


def unit_rows_of(x_tile):
    x_wide = x_tile.astype(F32)
    inv_rms = lax.rsqrt(jnp.mean(x_wide * x_wide, axis=-1, keepdims=True) + NORM_EPS)
    return x_wide, inv_rms


def lane_join(ref):
    return jnp.concatenate([ref[b] for b in range(ref.shape[0])], axis=1)


def tile_of(ref, rows):
    return jnp.concatenate([ref[b, rows, :] for b in range(ref.shape[0])], axis=1)


def put_tile(ref, rows, value):
    for b in range(ref.shape[0]):
        ref[b, rows, :] = value[:, b * LANES : (b + 1) * LANES]


def tile_rows(t):
    return pl.ds(pl.multiple_of(t * TOK_TILE, TOK_TILE), TOK_TILE)


class Place:
    def __init__(self):
        self.chip = lax.axis_index("local")
        self.core = lax.axis_index("data")
        self.chip_x, self.chip_y = lax.rem(self.chip, 2), lax.div(self.chip, 2)

    def chip_at(self, mask):
        mask_x, mask_y = (mask % 2, mask // 2) if isinstance(mask, int) else (lax.rem(mask, 2), lax.div(mask, 2))
        return lax.rem(self.chip_x + mask_x, 2) + 2 * lax.rem(self.chip_y + mask_y, 2)

    def across(self, mask):
        return (self.chip_at(mask), self.core)

    def twin(self):
        return (self.chip, 1 - self.core)

    def peers(self):
        return [self.across(1), self.across(2), self.twin()]


def meet(place):
    barrier = pltpu.get_barrier_semaphore()
    for device in place.peers():
        pl.semaphore_signal(barrier, inc=1, device_id=device, device_id_type=MESH)
    pl.semaphore_wait(barrier, 3)


def remote(src, dst, send_sem, recv_sem, device):
    return pltpu.make_async_remote_copy(
        src_ref=src, dst_ref=dst, send_sem=send_sem, recv_sem=recv_sem, device_id=device, device_id_type=MESH
    )


class Stream:
    def __init__(self, place, order, own_in, own_out, kept_in, kept_out, got_in, got_out, twin_in, twin_out, sems):
        self.place, self.order = place, order
        self.own_in, self.own_out, self.kept_in, self.kept_out = own_in, own_out, kept_in, kept_out
        self.got_in, self.got_out, self.twin_in, self.twin_out = got_in, got_out, twin_in, twin_out
        (self.in_send, self.in_recv, self.out_send, self.out_recv) = sems[:4]
        (self.twin_in_send, self.twin_in_recv, self.twin_out_send, self.twin_out_recv) = sems[4:]
        self.blocks = own_in.shape[1] // CHIPS

    def mine_in(self, n, mask, block, count):
        rows = pl.ds(block, count)
        if mask == 0:
            return self.own_in.at[n, rows]
        if mask == 1:
            return self.kept_in.at[n, rows]
        return self.got_in.at[lax.rem(n, 2), mask - 2, rows]

    def mine_out(self, n, mask):
        if mask == 0:
            return self.own_out.at[n]
        if mask == 2:
            return self.kept_out.at[n]
        return self.got_out.at[lax.rem(n, 2), (mask - 1) // 2]

    def send_in(self, n, mask, unit):
        there = 1 if mask == 1 else 2
        block = self.place.chip_at(there ^ unit) * self.blocks
        src = self.mine_in(n, 1 if mask == 3 else 0, block, self.blocks)
        dst = self.mine_in(n, mask, block, self.blocks)
        recv = self.in_recv.at[lax.rem(n, 2), mask - 1, unit]
        return remote(src, dst, self.in_send.at[lax.rem(n, 2), mask - 1, unit], recv, self.place.across(there))

    def got_slice(self, n, mask, unit):
        dst = self.mine_in(n, mask, self.place.chip_at(unit) * self.blocks, self.blocks)
        recv = self.in_recv.at[lax.rem(n, 2), mask - 1, unit]
        return remote(dst, dst, self.in_send.at[lax.rem(n, 2), mask - 1, unit], recv, self.place.across(1))

    def send_out(self, n, mask):
        src, dst = self.mine_out(n, 2 if mask == 3 else 0), self.mine_out(n, mask)
        recv = self.out_recv.at[lax.rem(n, 2), mask - 1]
        return remote(src, dst, self.out_send.at[lax.rem(n, 2), mask - 1], recv, self.place.across(2 if mask == 2 else 1))

    def push(self, n, keep):
        for unit in self.order:
            for mask in (1, 2) if keep else (2, 3):
                self.send_in(n, mask, unit).start()
        for mask in (1, 2) if keep else (1, 3):
            self.send_out(n, mask).start()

    def relay_in(self, n):
        for unit in self.order:
            self.got_slice(n, 1, 2 ^ unit).wait_recv()
            self.send_in(n, 3, unit).start()

    def relay_out(self, n):
        self.send_out(n, 2).wait_recv()
        self.send_out(n, 3).start()

    def pushed(self, n, keep):
        for mask in (1, 2, 3) if keep else (2, 3):
            for unit in self.order:
                self.send_in(n, mask, unit).wait_send()
        for mask in (1, 2, 3) if keep else (1, 3):
            self.send_out(n, mask).wait_send()

    def twin_copies(self, n, unit):
        slot, block = lax.rem(n, 2), self.place.chip_at(unit) * self.blocks
        return [
            remote(
                self.mine_in(n, mask, block, self.blocks),
                self.twin_in.at[slot, mask, pl.ds(block, self.blocks)],
                self.twin_in_send.at[mask, unit],
                self.twin_in_recv.at[slot, mask, unit],
                self.place.twin(),
            )
            for mask in range(CHIPS)
        ]

    def twin_out_copy(self, n, mask, unit):
        slot = lax.rem(n, 2)
        recv = self.twin_out_recv.at[slot, unit]
        return remote(self.mine_out(n, mask), self.twin_out.at[slot, unit], self.twin_out_send.at[unit], recv, self.place.twin())

    def forward(self, n, unit):
        for mask in (2, 3):
            self.got_slice(n, mask, unit).wait_recv()
        for copy in self.twin_copies(n, unit):
            copy.start()
        for mask in range(CHIPS):

            @pl.when(unit == mask)
            def _():
                if mask in (1, 3):
                    self.send_out(n, mask).wait_recv()
                self.twin_out_copy(n, mask, unit).start()

    def forwarded(self, n, unit):
        for copy in self.twin_copies(n, unit):
            copy.wait_send()
        self.twin_out_copy(n, 0, unit).wait_send()

    def arrive(self, n, unit):
        for copy in self.twin_copies(n, unit):
            copy.wait_recv()
        self.twin_out_copy(n, 0, unit).wait_recv()

    def load_in(self, n, unit, parity, w_in_v, v, sem):
        count, depth = self.blocks // 2, self.own_in.shape[2]
        block = self.place.chip_at(unit) * self.blocks + parity * count
        copies = []
        for mask in range(CHIPS):
            for which in range(2):
                shard = 2 * self.place.chip_at(mask) + (self.place.core if which == 0 else 1 - self.place.core)
                src = self.mine_in(n, mask, block, count) if which == 0 else self.twin_in.at[lax.rem(n, 2), mask, pl.ds(block, count)]
                row = pl.ds(pl.multiple_of(shard * depth, depth), depth)
                copies.append(pltpu.make_async_copy(src, w_in_v.at[v, :, row], sem.at[v, 2 * mask + which]))
        return copies

    def load(self, n, unit, mine, w_in_v, w_out_v, v, sem):
        parity = 1 - self.place.core - mine + 2 * self.place.core * mine
        for copy in self.load_in(n, unit, parity, w_in_v, v, sem):
            copy.start()
        last = sem.at[v, 2 * CHIPS]

        @pl.when(mine == 0)
        def _():
            pltpu.make_async_copy(self.twin_out.at[lax.rem(n, 2), unit], w_out_v.at[v], last).start()

        for mask in range(CHIPS):

            @pl.when((mine == 1) & (unit == mask))
            def _():
                pltpu.make_async_copy(self.mine_out(n, mask), w_out_v.at[v], last).start()

    def loaded(self, w_in_v, w_out_v, v, sem):
        for copy in self.load_in(0, 0, 0, w_in_v, v, sem):
            copy.wait()
        pltpu.make_async_copy(self.own_out.at[0], w_out_v.at[v], sem.at[v, 2 * CHIPS]).wait()


class Pace:
    def __init__(self, place, stream, layers, layer_at, unit_at, keep, bufs, credit):
        self.place, self.stream, self.layers, self.layer_at, self.unit_at = place, stream, layers, layer_at, unit_at
        self.keep, self.credit = keep, credit
        self.w_in_v, self.w_out_v, self.load_sem = bufs

    def load(self, q, i, b):
        self.stream.load(self.layer_at(q), self.unit_at(i), b, self.w_in_v, self.w_out_v, b, self.load_sem)

    def head(self):
        self.stream.push(self.layer_at(0), self.keep)

    def head_end(self):
        if self.keep:
            self.stream.relay_in(self.layer_at(0))
        self.stream.forward(self.layer_at(0), self.unit_at(0))
        self.stream.arrive(self.layer_at(0), self.unit_at(0))
        self.load(0, 0, 0)
        self.stream.forwarded(self.layer_at(0), self.unit_at(0))

    def sends(self, q, s):
        i, b = lax.div(s, 2), lax.rem(s, 2)
        return [
            ((b == 0) & (i == 3) & (q + 1 < self.layers), q + 1, 0),
            ((b == 0) & (i < 3) & (q > 0), q, i + 1),
            ((b == 1) & (i < 3) & (q == 0), q, i + 1),
        ]

    def before(self, q, s):
        i, b = lax.div(s, 2), lax.rem(s, 2)
        more = q + 1 < self.layers

        @pl.when((s == 0) & (q > 0))
        def _():
            self.stream.pushed(self.layer_at(q - 1), self.keep)

        @pl.when((s == 0) & more)
        def _():
            for at, device in enumerate(self.place.peers()):
                pl.semaphore_signal(self.credit.at[at], inc=1, device_id=device, device_id_type=MESH)
            for at in range(3):
                pl.semaphore_wait(self.credit.at[at], 1)
            self.stream.push(self.layer_at(q + 1), self.keep)

        if self.keep:

            @pl.when((s == 2) & (q == 0))
            def _():
                self.stream.relay_out(self.layer_at(0))

            @pl.when(((s == 3) & (q > 0) | (s == 4) & (q == 0)) & more)
            def _():
                self.stream.relay_in(self.layer_at(q + 1))

            @pl.when(((s == 5) & (q > 0) | (s == 7) & (q == 0)) & more)
            def _():
                self.stream.relay_out(self.layer_at(q + 1))

        for condition, count, unit in self.sends(q, s):

            @pl.when(condition)
            def _():
                self.stream.forward(self.layer_at(count), self.unit_at(unit))

        @pl.when(b == 0)
        def _():
            self.load(q, i, 1)

        for condition, count, unit in (((b == 1) & (i < 3), q, i + 1), ((s == 7) & more, q + 1, 0)):

            @pl.when(condition)
            def _():
                self.stream.arrive(self.layer_at(count), self.unit_at(unit))
                self.load(count, unit, 0)

        self.stream.loaded(self.w_in_v, self.w_out_v, b, self.load_sem)

    def after(self, q, s):
        for condition, count, unit in self.sends(q, s):

            @pl.when(condition)
            def _():
                self.stream.forwarded(self.layer_at(count), self.unit_at(unit))


def when(condition):
    if isinstance(condition, bool):
        return lambda body: body() if condition else None
    return pl.when(condition)


def both(*conditions):
    kept = [c for c in conditions if not (isinstance(c, bool) and c)]
    if any(isinstance(c, bool) for c in kept):
        return False
    if not kept:
        return True
    return functools.reduce(lambda a, b: a & b, kept)


BACKWARD_UNITS = (1, 3, 2, 0)


def backward_mask(unit):
    if isinstance(unit, int):
        return BACKWARD_UNITS[unit]
    return (1 - lax.div(unit, 2)) + 2 * lax.rem(lax.div(unit + 1, 2), 2)


class Reduce:
    def __init__(self, place, layers, hbm, vmem, sems, outs):
        self.place, self.layers = place, layers
        self.p_out, self.o_a, self.o_b, self.u_out, self.q_in, self.i_a, self.s_in, self.i_b = hbm
        self.r_v, self.gt_v, self.gm_v, self.o_v, self.it_v, self.out_a, self.out_b, self.in_a, self.in_b = vmem
        (
            self.to_send,
            self.to_recv,
            self.ti_send,
            self.ti_recv,
            self.oa_send,
            self.oa_recv,
            self.ob_send,
            self.ob_recv,
            self.ia_send,
            self.ia_recv,
            self.ib_send,
            self.ib_recv,
            self.p_sem,
            self.q_sem,
            self.out_sem,
            self.in_sem,
            self.out_save,
            self.in_save,
            self.credit_o,
            self.credit_i,
        ) = sems
        self.gw_in, self.gw_out = outs
        self.half_out = self.out_a.shape[1]
        self.side = self.in_a.shape[0] // 2
        self.row = self.side // 2
        self.chunk = self.in_a.shape[1]

    def slot(self, q):
        return q % 2 if isinstance(q, int) else lax.rem(q, 2)

    def twin_out(self):
        return remote(self.r_v, self.o_v, self.to_send, self.to_recv, self.place.twin())

    def twin_in(self, b):
        return remote(self.gt_v, self.it_v.at[b], self.ti_send.at[b], self.ti_recv.at[b], self.place.twin())

    def across_x_out(self, q, i, h):
        s = self.slot(q)
        return remote(self.p_out.at[s, i, h], self.o_a.at[s, i, h], self.oa_send.at[i, h], self.oa_recv.at[s, i, h], self.place.across(1))

    def across_y_out(self, q, h):
        s = self.slot(q)
        return remote(self.u_out.at[s, h], self.o_b.at[s, h], self.ob_send.at[h], self.ob_recv.at[s, h], self.place.across(2))

    def across_y_in(self, q, i, b):
        s, far = self.slot(q), pl.ds(pl.multiple_of((1 - self.place.chip_y) * self.side, self.side), self.side)
        there = i + 1 - 2 * (i % 2)
        return remote(
            self.q_in.at[s, i, b, far], self.i_a.at[s, there, b], self.ia_send.at[i, b], self.ia_recv.at[s, there, b], self.place.across(2)
        )

    def across_x_in(self, q, i, b):
        s, far = self.slot(q), pl.ds(pl.multiple_of((1 - self.place.chip_x) * self.row, self.row), self.row)
        there = 3 - i
        return remote(
            self.s_in.at[s, i, b, far], self.i_b.at[s, there, b], self.ib_send.at[i, b], self.ib_recv.at[s, there, b], self.place.across(1)
        )

    def resend(self, q, copy_of):
        @when(q > 0)
        def _():
            copy_of(q).wait_send()

        copy_of(q).start()

    def save_p(self, q, i):
        s = self.slot(q)
        return [
            pltpu.make_async_copy(self.r_v.at[:, pl.ds(h * self.half_out, self.half_out)], self.p_out.at[s, i, h], self.p_sem.at[h])
            for h in range(2)
        ]

    def save_q(self, q, i, b, gm):
        return pltpu.make_async_copy(self.gm_v.at[gm], self.q_in.at[self.slot(q), i, b], self.q_sem.at[b])

    def out_loads(self, a, b):
        return [pltpu.make_async_copy(a, self.out_a, self.out_sem.at[0]), pltpu.make_async_copy(b, self.out_b, self.out_sem.at[1])]

    def out_first(self, q):
        return self.out_loads(self.o_a.at[self.slot(q), 0, 0], self.o_a.at[self.slot(q), 0, 1])

    def out_second(self, q, h):
        s = self.slot(q)
        return self.out_loads(self.p_out.at[s, 2, h], self.o_a.at[s, 1, h])

    def out_third(self, q, h):
        s = self.slot(q)
        return self.out_loads(self.p_out.at[s, 3, h], self.o_b.at[s, h])

    def out_second_save(self, q, h):
        return pltpu.make_async_copy(self.out_a, self.u_out.at[self.slot(q), h], self.out_save)

    def out_third_save(self, q, h):
        n = self.layers - 1 - q
        return pltpu.make_async_copy(self.out_a, self.gw_out.at[n, :, pl.ds(h * self.half_out, self.half_out)], self.out_save)

    def in_second(self, q, pair, b):
        s, near = self.slot(q), pl.ds(pl.multiple_of(self.place.chip_y * self.side, self.side), self.side)
        copies = []
        for at in range(2):
            i, rows = 2 * pair + at, pl.ds(at * self.side, self.side)
            copies.append(pltpu.make_async_copy(self.q_in.at[s, i, b, near], self.in_a.at[rows], self.in_sem.at[0, at]))
            copies.append(pltpu.make_async_copy(self.i_a.at[s, i, b], self.in_b.at[rows], self.in_sem.at[1, at]))
        return copies

    def in_third(self, q, b):
        s, near = self.slot(q), pl.ds(pl.multiple_of(self.place.chip_x * self.row, self.row), self.row)
        copies = []
        for i in range(CHIPS):
            rows = pl.ds(i * self.row, self.row)
            copies.append(pltpu.make_async_copy(self.s_in.at[s, i, b, near], self.in_a.at[rows], self.in_sem.at[0, i]))
            copies.append(pltpu.make_async_copy(self.i_b.at[s, i, b], self.in_b.at[rows], self.in_sem.at[1, i]))
        return copies

    def in_second_save(self, q, pair, b):
        s = self.slot(q)
        return [
            pltpu.make_async_copy(self.in_a.at[pl.ds(at * self.side, self.side)], self.s_in.at[s, 2 * pair + at, b], self.in_save.at[at])
            for at in range(2)
        ]

    def in_third_save(self, q, b):
        n = self.layers - 1 - q
        core = self.place.core
        copies = []
        for i in range(CHIPS):
            shard = 2 * self.place.chip_at(BACKWARD_UNITS[i]) + (core if b else 1 - core)
            columns = pl.ds(pl.multiple_of(shard * self.chunk, self.chunk), self.chunk)
            copies.append(pltpu.make_async_copy(self.in_a.at[pl.ds(i * self.row, self.row)], self.gw_in.at[n, :, columns], self.in_save.at[i]))
        return copies

    def add(self, a, b):
        for start in range(0, a.shape[0], 64):
            rows = pl.ds(start, 64)
            a[rows, :] = a[rows, :] + b[rows, :]

    def free(self, semaphore):
        pl.semaphore_signal(semaphore, inc=1, device_id=self.place.twin(), device_id_type=MESH)

    def start(self):
        for semaphore in (self.credit_o, self.credit_i.at[0], self.credit_i.at[1]):
            self.free(semaphore)

    def mid(self, q, s):
        here = q < self.layers
        older = q > 0

        for t in range(8):
            i, b = t // 2, t % 2
            layer = q if t < 7 else q - 1

            @when(both(s == (t + 1) % 8, here if t < 7 else older))
            def _():
                self.twin_in(b).wait_send()
                if b == 0:
                    self.twin_out().wait_send()
                else:
                    for copy in self.save_p(layer, i):
                        copy.wait()
                    self.save_q(layer, i, 1, 0).wait()
                    if i < 2:
                        for h in range(2):
                            self.resend(layer, lambda q, h=h: self.across_x_out(q, i, h))
                    self.resend(layer, lambda q: self.across_y_in(q, i, 1))

            layer = q if t < 5 else q - 1
            if b == 0:

                @when(both(s == (t + 3) % 8, here if t < 5 else older))
                def _():
                    self.save_q(layer, i, 0, 0).wait()
                    self.resend(layer, lambda q: self.across_y_in(q, i, 0))

        for step, pair, b, late in ((6, 0, 1, 0), (7, 0, 0, 0), (2, 1, 1, 1), (3, 1, 0, 1)):
            layer = q - late

            @when(both(s == step, older if late else here))
            def _():
                for copy in self.in_second_save(layer, pair, b):
                    copy.wait()
                for at in range(2):
                    self.resend(layer, lambda q, at=at: self.across_x_in(q, 2 * pair + at, b))

        for step, b in ((4, 1), (5, 0)):

            @when(both(s == step, older))
            def _():
                for copy in self.in_third_save(q - 1, b):
                    copy.wait()

        for step, pair, b, late in ((5, 0, 1, 0), (6, 0, 0, 0), (1, 1, 1, 1), (2, 1, 0, 1)):
            layer = q - late

            @when(both(s == step, older if late else here))
            def _():
                for at in range(2):
                    there = 2 * pair + 1 - at
                    self.across_y_in(layer, there, b).wait_recv()
                for copy in self.in_second(layer, pair, b):
                    copy.start()

        for step, b in ((3, 1), (4, 0)):

            @when(both(s == step, older))
            def _():
                for i in range(CHIPS):
                    self.across_x_in(q - 1, 3 - i, b).wait_recv()
                for copy in self.in_third(q - 1, b):
                    copy.start()

        for step, h in ((1, 0), (2, 1)):

            @when(both(s == step, older))
            def _():
                self.out_second_save(q - 1, h).wait()
                self.resend(q - 1, lambda q: self.across_y_out(q, h))

        for step, h in ((5, 0), (6, 1)):

            @when(both(s == step, older))
            def _():
                self.out_third_save(q - 1, h).wait()

        @when(both(s == 7, here))
        def _():
            for h in range(2):
                self.across_x_out(q, 0, h).wait_recv()
            for copy in self.out_first(q):
                copy.start()

        for step, h in ((0, 0), (1, 1)):

            @when(both(s == step, older))
            def _():
                self.across_x_out(q - 1, 1, h).wait_recv()
                for copy in self.out_second(q - 1, h):
                    copy.start()

        for step, h in ((4, 0), (5, 1)):

            @when(both(s == step, older))
            def _():
                self.across_y_out(q - 1, h).wait_recv()
                for copy in self.out_third(q - 1, h):
                    copy.start()

    def end(self, q, s, gm):
        here = q < self.layers
        older = q > 0
        final = q == self.layers - 1

        for t in range(8):
            i, b = t // 2, t % 2

            @when(both(s == t, here))
            def _():
                pl.semaphore_wait(self.credit_i.at[b], 1)
                self.twin_in(b).start()
                if b == 0:
                    pl.semaphore_wait(self.credit_o, 1)
                    self.twin_out().start()
                    return
                self.twin_out().wait_recv()
                self.add(self.r_v, self.o_v)

                @when(True if i < 3 else q < self.layers - 1)
                def _():
                    self.free(self.credit_o)

                if i == 3:
                    for copy in self.out_first(q):
                        copy.wait()
                    for start in range(0, self.r_v.shape[0], 64):
                        rows = pl.ds(start, 64)
                        for h, part in enumerate((self.out_a, self.out_b)):
                            columns = pl.ds(h * self.half_out, self.half_out)
                            self.r_v[rows, columns] = self.r_v[rows, columns] + part[rows, :]
                for copy in self.save_p(q, i):
                    copy.start()
                self.twin_in(0).wait_recv()
                self.add(self.gm_v.at[gm], self.it_v.at[0])

                @when(True if i < 3 else q < self.layers - 1)
                def _():
                    self.free(self.credit_i.at[0])

                self.save_q(q, i, 1, gm).start()

            if b == 0:
                layer = q if t < 6 else q - 1
                old = (gm + 1) % 3 if isinstance(gm, int) else lax.rem(gm + 1, 3)

                @when(both(s == (t + 2) % 8, here if t < 6 else older))
                def _():
                    self.twin_in(1).wait_recv()
                    self.add(self.gm_v.at[old], self.it_v.at[1])

                    @when(True if i < 3 else layer < self.layers - 1)
                    def _():
                        self.free(self.credit_i.at[1])

                    self.save_q(layer, i, 0, old).start()

        for step, pair, b, late in ((5, 0, 1, 0), (6, 0, 0, 0), (1, 1, 1, 1), (2, 1, 0, 1)):
            layer = q - late

            @when(both(s == step, older if late else here))
            def _():
                for copy in self.in_second(layer, pair, b):
                    copy.wait()
                self.add(self.in_a, self.in_b)
                for copy in self.in_second_save(layer, pair, b):
                    copy.start()

        for step, b in ((3, 1), (4, 0)):

            @when(both(s == step, older))
            def _():
                for copy in self.in_third(q - 1, b):
                    copy.wait()
                self.add(self.in_a, self.in_b)
                for copy in self.in_third_save(q - 1, b):
                    copy.start()

        for step, h in ((0, 0), (1, 1)):

            @when(both(s == step, older))
            def _():
                for copy in self.out_second(q - 1, h):
                    copy.wait()
                self.add(self.out_a, self.out_b)
                self.out_second_save(q - 1, h).start()

        for step, h in ((4, 0), (5, 1)):

            @when(both(s == step, older))
            def _():
                for copy in self.out_third(q - 1, h):
                    copy.wait()
                self.add(self.out_a, self.out_b)
                self.out_third_save(q - 1, h).start()

    def finish(self):
        q = self.layers
        for s in range(7):
            self.mid(q, s)
            if s < 6:
                self.end(q, s, (8 * q + s) % 3)
        last = q - 1
        for h in range(2):
            for i in range(2):
                self.across_x_out(last, i, h).wait_send()
            self.across_y_out(last, h).wait_send()
        for b in range(2):
            for i in range(CHIPS):
                self.across_y_in(last, i, b).wait_send()
                self.across_x_in(last, i, b).wait_send()


def forward_stack_kernel(layers, x_ref, w_in_ref, w_out_ref, *refs):
    xs_ref, own_in, own_out, kept_in, kept_out, got_in, got_out, twin_in, twin_out = refs[:9]
    x_v, unit_v, total_v, w_in_v, w_out_v, stage_in, stage_out = refs[9:16]
    x_sem, load_sem, stage_sem, credit = refs[16:20]
    place = Place()
    stream = Stream(place, (0, 1, 2, 3), own_in, own_out, kept_in, kept_out, got_in, got_out, twin_in, twin_out, refs[20:])
    pace = Pace(place, stream, layers, lambda q: q, lambda i: i, True, (w_in_v, w_out_v, load_sem), credit)
    tokens, width = x_v.shape
    tiles = tokens // TOK_TILE

    def to_lanes(n):
        pairs = ((w_in_ref, stage_in, own_in, 0), (w_out_ref, stage_out, own_out, 1))
        for src, stage, _, at in pairs:
            for b in range(stage.shape[0]):
                pltpu.make_async_copy(src.at[n, :, pl.ds(b * LANES, LANES)], stage.at[b], stage_sem.at[at]).start()
        for _, stage, own, at in pairs:
            pltpu.make_async_copy(own.at[n], stage, stage_sem.at[at]).wait()
            pltpu.make_async_copy(stage, own.at[n], stage_sem.at[at]).start()
        for _, stage, own, at in pairs:
            pltpu.make_async_copy(stage, own.at[n], stage_sem.at[at]).wait()

    fetch = pltpu.make_async_copy(x_ref, x_v, x_sem)
    fetch.start()
    to_lanes(0)
    meet(place)
    pace.head()

    def other_lanes(n, carry):
        to_lanes(n)
        return carry

    lax.fori_loop(1, layers, other_lanes, 0)
    fetch.wait()

    def first_unit(t, carry):
        rows = tile_rows(t)
        x_wide, inv_rms = unit_rows_of(x_v[rows, :])
        put_tile(unit_v, rows, (x_wide * inv_rms).astype(BF16))
        total_v[rows, :] = jnp.zeros((TOK_TILE, width), F32)
        return carry

    lax.fori_loop(0, tiles, first_unit, 0)
    pace.head_end()

    def save(n):
        return pltpu.make_async_copy(x_v, xs_ref.at[n], x_sem)

    def compute(v, last):
        w_in, w_out = lane_join(w_in_v.at[v]), lane_join(w_out_v.at[v])
        pending = []

        def finish():
            t, hidden = pending.pop(0)
            rows = pl.ds(t * TOK_TILE, TOK_TILE)
            total = total_v[rows, :] + jnp.dot(hidden, w_out, preferred_element_type=F32)
            if not last:
                total_v[rows, :] = total
                return
            x_next = (x_v[rows, :].astype(F32) + total).astype(BF16)
            x_v[rows, :] = x_next
            total_v[rows, :] = jnp.zeros((TOK_TILE, width), F32)
            x_wide, inv_rms = unit_rows_of(x_next)
            put_tile(unit_v, rows, (x_wide * inv_rms).astype(BF16))

        for t in range(tiles):
            unit = tile_of(unit_v, pl.ds(t * TOK_TILE, TOK_TILE))
            pre = jnp.dot(unit, w_in, preferred_element_type=F32).astype(BF16).astype(F32)
            tanh = jnp.tanh(pre * (GELU_A + GELU_B * (pre * pre)))
            pending.append((t, (pre * (0.5 * tanh + 0.5)).astype(BF16)))
            if len(pending) > 1:
                finish()
        while pending:
            finish()

    def step(n, s):
        v = lax.rem(s, 2)
        pace.before(n, s)

        @pl.when(s < 7)
        def _():
            compute(v, False)

        @pl.when(s == 7)
        def _():
            @pl.when(n > 0)
            def _():
                save(n - 1).wait()

            compute(v, True)
            save(n).start()

        pace.after(n, s)

    def layer_step(n, carry):
        lax.fori_loop(0, 8, lambda s, c: (step(n, s), c)[1], 0)
        return carry

    lax.fori_loop(0, layers, layer_step, 0)
    stream.pushed(layers - 1, True)
    save(layers - 1).wait()


def backward_stack_kernel(layers, x_ref, xs_ref, dy_ref, own_in, own_out, kept_in, kept_out, *refs):
    gw_in, gw_out, dx_ref, got_in, got_out, twin_in, twin_out = refs[:7]
    sums_hbm = refs[7:15]
    unit_v, dy_v, du_v, hidden_v, dpre_v, w_in_v, w_out_v, x_v = refs[15:23]
    sums_v = refs[23:32]
    row_sem, x_sem, load_sem, credit = refs[32:36]
    stream_sems, sum_sems = refs[36:44], refs[44:]
    place = Place()
    stream = Stream(place, BACKWARD_UNITS, own_in, own_out, kept_in, kept_out, got_in, got_out, twin_in, twin_out, stream_sems)
    pace = Pace(place, stream, layers, lambda q: layers - 1 - q, backward_mask, False, (w_in_v, w_out_v, load_sem), credit)
    sums = Reduce(place, layers, sums_hbm, sums_v, sum_sems, (gw_in, gw_out))
    r_v, gt_v, gm_v = sums_v[:3]
    blocks_d, tokens, _ = unit_v.shape
    width = blocks_d * LANES
    tiles = tokens // TOK_TILE

    meet(place)
    pace.head()
    sums.start()

    def rows_copies(to_vmem, ref):
        copies = []
        for b in range(blocks_d):
            pair = (ref.at[:, pl.ds(b * LANES, LANES)], dy_v.at[b])
            copies.append(pltpu.make_async_copy(*(pair if to_vmem else pair[::-1]), row_sem.at[b]))
        return copies

    dy_copies = rows_copies(True, dy_ref)
    for copy in dy_copies:
        copy.start()

    def fetch(n, which, t):
        dst, sem = x_v.at[which, lax.rem(t, 2)], x_sem.at[which, lax.rem(t, 2)]

        @pl.when(n > 0)
        def _():
            pltpu.make_async_copy(xs_ref.at[n - 1, tile_rows(t)], dst, sem).start()

        @pl.when(n == 0)
        def _():
            pltpu.make_async_copy(x_ref.at[tile_rows(t)], dst, sem).start()

    def fetched(which, t):
        at = lax.rem(t, 2)
        pltpu.make_async_copy(x_ref.at[tile_rows(0)], x_v.at[which, at], x_sem.at[which, at]).wait()
        return x_v[which, at]

    def first_unit(t, carry):
        @pl.when(t + 1 < tiles)
        def _():
            fetch(layers - 1, 1, t + 1)

        rows = tile_rows(t)
        x_wide, inv_rms = unit_rows_of(fetched(1, t))
        put_tile(unit_v, rows, (x_wide * inv_rms).astype(BF16))
        du_v[rows, :] = jnp.zeros((TOK_TILE, width), F32)
        return carry

    fetch(layers - 1, 1, 0)
    lax.fori_loop(0, tiles, first_unit, 0)
    for copy in dy_copies:
        copy.wait()
    pace.head_end()

    def hidden_part(v):
        w_in, w_out = lane_join(w_in_v.at[v]), lane_join(w_out_v.at[v])
        pending = []

        def finish():
            t, dpre = pending.pop(0)
            rows = pl.ds(t * TOK_TILE, TOK_TILE)
            du_v[rows, :] = du_v[rows, :] + lax.dot_general(dpre, w_in, LAST_LAST, preferred_element_type=F32)

        for t in range(tiles):
            rows = pl.ds(t * TOK_TILE, TOK_TILE)
            pre = jnp.dot(tile_of(unit_v, rows), w_in, preferred_element_type=F32).astype(BF16).astype(F32)
            dhidden = lax.dot_general(tile_of(dy_v, rows), w_out, LAST_LAST, preferred_element_type=F32)
            poly = GELU_A + GELU_B * (pre * pre)
            cdf = 0.5 * jnp.tanh(pre * poly) + 0.5
            hidden = pre * cdf
            slope = cdf + (hidden * (6.0 * poly - 4.0 * GELU_A)) * (1.0 - cdf)
            dpre = (slope * dhidden).astype(BF16)
            put_tile(hidden_v, rows, hidden.astype(BF16))
            put_tile(dpre_v, rows, dpre)
            pending.append((t, dpre))
            if len(pending) > 1:
                finish()
        while pending:
            finish()

    def gradient_part(gm):
        r_v[...] = lax.dot_general(lane_join(hidden_v), lane_join(dy_v), FIRST_FIRST, preferred_element_type=F32)
        dpre = lane_join(dpre_v)

        def unit_of(parity):
            per = blocks_d // SHARDS
            parts = [unit_v[(2 * c + parity) * per + b] for c in range(CHIPS) for b in range(per)]
            return jnp.concatenate(parts, axis=1)

        gt_v[...] = lax.dot_general(unit_of(1 - place.core), dpre, FIRST_FIRST, preferred_element_type=F32)
        gm_v[gm] = lax.dot_general(unit_of(place.core), dpre, FIRST_FIRST, preferred_element_type=F32)

    def step(q, s):
        gm = lax.rem(8 * q + s, 3)
        pace.before(q, s)
        hidden_part(lax.rem(s, 2))
        sums.mid(q, s)
        gradient_part(gm)
        sums.end(q, s, gm)
        pace.after(q, s)

    def layer_step(q, carry):
        n = layers - 1 - q
        lax.fori_loop(0, 8, lambda s, c: (step(q, s), c)[1], 0)
        fetch(n, 0, 0)

        @pl.when(n > 0)
        def _():
            fetch(n - 1, 1, 0)

        def close(t, carry):
            @pl.when(t + 1 < tiles)
            def _():
                fetch(n, 0, t + 1)

                @pl.when(n > 0)
                def _():
                    fetch(n - 1, 1, t + 1)

            rows = tile_rows(t)
            x_wide, inv_rms = unit_rows_of(fetched(0, t))
            value, du = x_wide * inv_rms, du_v[rows, :]
            row_mean = jnp.mean(du * value, axis=-1, keepdims=True)
            put_tile(dy_v, rows, (tile_of(dy_v, rows).astype(F32) + inv_rms * (du - value * row_mean)).astype(BF16))
            du_v[rows, :] = jnp.zeros((TOK_TILE, width), F32)

            @pl.when(n > 0)
            def _():
                x_wide, inv_rms = unit_rows_of(fetched(1, t))
                put_tile(unit_v, rows, (x_wide * inv_rms).astype(BF16))

            return carry

        lax.fori_loop(0, tiles, close, 0)
        return carry

    lax.fori_loop(0, layers, layer_step, 0)
    dx_copies = rows_copies(False, dx_ref)
    for copy in dx_copies:
        copy.start()
    sums.finish()
    stream.pushed(0, False)
    for copy in dx_copies:
        copy.wait()


def stream_semaphores():
    dma = pltpu.SemaphoreType.DMA
    return [dma((2, 3, 4)), dma((2, 3, 4)), dma((2, 3)), dma((2, 3)), dma((4, 4)), dma((2, 4, 4)), dma((4,)), dma((2, 4))]


def sum_semaphores():
    dma, regular = pltpu.SemaphoreType.DMA, pltpu.SemaphoreType.REGULAR
    return [
        dma,
        dma,
        dma((2,)),
        dma((2,)),
        dma((2, 2)),
        dma((2, 2, 2)),
        dma((2,)),
        dma((2, 2)),
        dma((4, 2)),
        dma((2, 4, 2)),
        dma((4, 2)),
        dma((2, 4, 2)),
        dma((2,)),
        dma((2,)),
        dma((2,)),
        dma((2, 4)),
        dma,
        dma((4,)),
        regular,
        regular((2,)),
    ]


def stream_buffers(piece_in, piece_out):
    return [
        jax.ShapeDtypeStruct((2, 2) + piece_in, BF16),
        jax.ShapeDtypeStruct((2, 2) + piece_out, BF16),
        jax.ShapeDtypeStruct((2, CHIPS) + piece_in, BF16),
        jax.ShapeDtypeStruct((2, CHIPS) + piece_out, BF16),
    ]


ANYWHERE = pl.BlockSpec(memory_space=pl.ANY)


def forward_stack(x_rows, w_in, w_out):
    layers, depth, hidden_size = w_in.shape
    tokens, width = x_rows.shape
    chunk = w_out.shape[1]
    piece_in, piece_out = (hidden_size // LANES, depth, LANES), (width // LANES, chunk, LANES)
    pieces = [jax.ShapeDtypeStruct((layers,) + piece, BF16) for piece in (piece_in, piece_out)]
    shapes = [jax.ShapeDtypeStruct((layers, tokens, width), BF16)] + pieces * 2 + stream_buffers(piece_in, piece_out)
    outs = pl.pallas_call(
        functools.partial(forward_stack_kernel, layers),
        in_specs=[ANYWHERE] * 3,
        out_specs=[ANYWHERE] * len(shapes),
        out_shape=shapes,
        scratch_shapes=[
            pltpu.VMEM((tokens, width), BF16),
            pltpu.VMEM((width // LANES, tokens, LANES), BF16),
            pltpu.VMEM((tokens, width), F32),
            pltpu.VMEM((2, chunk // LANES, width, LANES), BF16),
            pltpu.VMEM((2, width // LANES, chunk, LANES), BF16),
            pltpu.VMEM(piece_in, BF16),
            pltpu.VMEM(piece_out, BF16),
            pltpu.SemaphoreType.DMA,
            pltpu.SemaphoreType.DMA((2, 2 * CHIPS + 1)),
            pltpu.SemaphoreType.DMA((2,)),
            pltpu.SemaphoreType.REGULAR((3,)),
        ]
        + stream_semaphores(),
        compiler_params=pltpu.CompilerParams(vmem_limit_bytes=VMEM_LIMIT, collective_id=0, has_side_effects=True),
        cost_estimate=pl.CostEstimate(flops=4 * layers * tokens * width * hidden_size, bytes_accessed=100_000_000, transcendentals=0),
        name="forward_stack",
    )(x_rows, w_in, w_out)
    return outs[:5]


def backward_stack(x_rows, xs, grad_rows, own_in, own_out, kept_in, kept_out):
    layers, blocks_f, depth, _ = own_in.shape
    blocks_d, chunk = own_out.shape[1], own_out.shape[2]
    tokens, width = x_rows.shape
    half, quarter = width // 2, width // 4
    hidden_size = blocks_f * LANES

    def sums(*shape):
        return jax.ShapeDtypeStruct(shape, F32)

    shapes = (
        [sums(layers, depth, hidden_size), sums(layers, chunk, width), jax.ShapeDtypeStruct((tokens, width), BF16)]
        + stream_buffers(own_in.shape[1:], own_out.shape[1:])
        + [
            sums(2, 4, 2, chunk, half),
            sums(2, 2, 2, chunk, half),
            sums(2, 2, chunk, half),
            sums(2, 2, chunk, half),
            sums(2, 4, 2, half, chunk),
            sums(2, 4, 2, quarter, chunk),
            sums(2, 4, 2, quarter, chunk),
            sums(2, 4, 2, depth, chunk),
        ]
    )
    outs = pl.pallas_call(
        functools.partial(backward_stack_kernel, layers),
        in_specs=[ANYWHERE] * 7,
        out_specs=[ANYWHERE] * len(shapes),
        out_shape=shapes,
        scratch_shapes=[
            pltpu.VMEM((blocks_d, tokens, LANES), BF16),
            pltpu.VMEM((blocks_d, tokens, LANES), BF16),
            pltpu.VMEM((tokens, width), F32),
            pltpu.VMEM((chunk // LANES, tokens, LANES), BF16),
            pltpu.VMEM((chunk // LANES, tokens, LANES), BF16),
            pltpu.VMEM((2, chunk // LANES, width, LANES), BF16),
            pltpu.VMEM((2, blocks_d, chunk, LANES), BF16),
            pltpu.VMEM((2, 2, TOK_TILE, width), BF16),
            pltpu.VMEM((chunk, width), F32),
            pltpu.VMEM((half, chunk), F32),
            pltpu.VMEM((3, half, chunk), F32),
            pltpu.VMEM((chunk, width), F32),
            pltpu.VMEM((2, half, chunk), F32),
            pltpu.VMEM((chunk, half), F32),
            pltpu.VMEM((chunk, half), F32),
            pltpu.VMEM((half, chunk), F32),
            pltpu.VMEM((half, chunk), F32),
            pltpu.SemaphoreType.DMA((blocks_d,)),
            pltpu.SemaphoreType.DMA((2, 2)),
            pltpu.SemaphoreType.DMA((2, 2 * CHIPS + 1)),
            pltpu.SemaphoreType.REGULAR((3,)),
        ]
        + stream_semaphores()
        + sum_semaphores(),
        compiler_params=pltpu.CompilerParams(vmem_limit_bytes=VMEM_LIMIT, collective_id=1, has_side_effects=True),
        cost_estimate=pl.CostEstimate(flops=10 * layers * tokens * width * hidden_size, bytes_accessed=300_000_000, transcendentals=0),
        name="backward_stack",
    )(x_rows, xs, grad_rows, own_in, own_out, kept_in, kept_out)
    return outs[:3]


def solution(mesh):
    row_spec = P(("local", "data"), None)
    weight_spec = P(None, ("local", "data"), None)

    def device_step(x_rows, grad_rows, w_in, w_out):
        xs, own_in, own_out, kept_in, kept_out = forward_stack(x_rows, w_in, w_out)
        gw_in, gw_out, dx = backward_stack(x_rows, xs, grad_rows, own_in, own_out, kept_in, kept_out)
        return xs[w_in.shape[0] - 1], gw_in, gw_out, dx

    return jax.shard_map(
        device_step,
        mesh=mesh,
        in_specs=(row_spec, row_spec, weight_spec, weight_spec),
        out_specs=(row_spec, weight_spec, weight_spec, row_spec),
        check_vma=False,
    )
```

time: 3480 us -> 1910 us (0.55)
  matrix products: 1870 us -> 0 us
  Pallas kernels: 0 us -> 1870 us
  waiting for transfers between devices: 1430 us -> 0 us
  other arithmetic: 72.7 us -> 0.01 us
  local copies, waits for them, and re-layouts: 91.4 us -> 29.3 us
    dot_general x35 -> x0, matrix products: 1870 us -> none  [the longest x5 437 us: layer_backward(): lax.dot_general(grad_rows, w_out, LAST_LAST, preferred_element_type=jnp.f...]
    pallas_call x0 -> x2, Pallas kernels: none -> 1870 us  [the longest x1 1380 us: backward_stack(): pl.pallas_call(functools.partial(backward_stack_kernel, layers), in_specs...]
    all_gather x30 -> x0, waiting for transfers between devices: 897 us -> none  [the longest x10 541 us: device_step(): full_in = lax.all_gather(sub_in, 'local', axis=0, tiled=True)]
    reduce_scatter x10 -> x0, waiting for transfers between devices: 521 us -> none  [the longest x5 521 us: device_step(): lax.psum_scatter(part_in, ('local', 'data'), scatter_dimension=0, tiled=T...]
    convert_element_type x5 -> x0, other arithmetic: 67.5 us -> none  [layer_backward(): return (grad_x.astype(jnp.bfloat16), grad_w_in, grad_w_out)]
    unnamed x49 -> x9, local copies, waits for them, and re-layouts: 63.5 us -> 21.3 us
  transfers between devices with their start and end apart: 40 -> 0, of which waited for: 32 -> 0; matrix products, arithmetic and copies ran while one was open for 42% -> 0% of each run, Pallas kernels for 0% -> 0%
where the time goes in v4:
time: 1910 us; the launch traced here: 1900 us
  Pallas kernels  1870 us (98%)
  local copies, waits for them, and re-layouts  29.3 us (2%)
    pallas_call x1, Pallas kernels, backward_stack(): pl.pallas_call(functools.partial(backward_stack_kernel, layers), in_specs...  1380 us
    pallas_call x1, Pallas kernels, forward_stack(): pl.pallas_call(functools.partial(forward_stack_kernel, layers), in_specs=...  488 us

profile of v4, /device:TPU:0, one launch (start us, length us, event | category | flops | bytes accessed | tf_op | source)
XLA Modules:
  0.0 1896.3 jit_solution(9762759856866150169)
XLA Ops:
  0.6 488.0 %forward_stack.1 = (bf16[5,4096,1024]{2,1,0:T(8,128)(2,1)}, bf16[5,32,128,128]{3,2,1,0:T(8,128)(2,1)}, bf16[5,8,512,128]{3,2,1,0:T(8,128)(2,1)}, bf16[5,32,128,1...) custom-call(bf16[4096,1024]{1,0:T(8,128)(2,1)} %x_ref.3, ...), custom_call_target="tpu_custom_call" | custom-call | flops 343597383680 | bytes 100000000 | tf_op jit(solution)/shard_map/forward_stack/pallas_call | solution.py:1004
  488.7 1377.9 %backward_stack.1 = (f32[5,128,4096]{2,1,0:T(8,128)}, f32[5,512,1024]{2,1,0:T(8,128)}, bf16[4096,1024]{1,0:T(8,128)(2,1)}, bf16[2,2,32,128,128]{4,3,2,1,0:T(8,12...) custom-call(bf16[4096,1024]{1,0:T(8,128)(2,1)} %x_ref.3, ...), custom_call_target="tpu_custom_call" | custom-call | flops 858993459200 | bytes 300000000 | tf_op jit(solution)/shard_map/backward_stack/pallas_call | solution.py:1054
  1866.5 0.0 slice-start
  1866.6 0.0 slice-start.1
  1866.6 8.0 slice_bitcast_fusion
  1874.5 0.0 slice-start.2
  1874.5 9.5 copy.11
  1884.0 0.0 slice-done
  1884.0 0.0 slice-done.1
  1884.0 0.0 slice-done.2
  1884.0 4.1 copy.12
  1888.1 7.8 copy.13
  (1 shorter events, 0.0 us)
Async XLA Ops:
  1866.5 17.5 slice-start
  1866.6 17.5 slice-start.1
  1874.5 9.5 slice-start.2

commit v5 on v4

--- a/solution.py
+++ b/solution.py
@@ -16,11 +16,14 @@
 F32 = jnp.float32
 MESH = pl.DeviceIdType.MESH
 
+TWO = 2
 CHIPS = 4
+STEPS = 8
 SHARDS = 8
 LANES = 128
 TOK_TILE = 256
 VMEM_LIMIT = 67_000_000
+ADD_ROWS = 64
 
 
 def unit_rows_of(x_tile):
@@ -46,15 +49,31 @@
     return pl.ds(pl.multiple_of(t * TOK_TILE, TOK_TILE), TOK_TILE)
 
 
+def odd(x):
+    return lax.rem(x, TWO)
+
+
+def half(x):
+    return lax.div(x, TWO)
+
+
+def notify(semaphore, device):
+    pl.semaphore_signal(semaphore, inc=1, device_id=device, device_id_type=MESH)
+
+
+def await_one(semaphore):
+    pl.semaphore_wait(semaphore, 1)
+
+
 class Place:
     def __init__(self):
         self.chip = lax.axis_index("local")
         self.core = lax.axis_index("data")
-        self.chip_x, self.chip_y = lax.rem(self.chip, 2), lax.div(self.chip, 2)
+        self.chip_x, self.chip_y = odd(self.chip), half(self.chip)
 
     def chip_at(self, mask):
-        mask_x, mask_y = (mask % 2, mask // 2) if isinstance(mask, int) else (lax.rem(mask, 2), lax.div(mask, 2))
-        return lax.rem(self.chip_x + mask_x, 2) + 2 * lax.rem(self.chip_y + mask_y, 2)
+        mask_x, mask_y = (mask % 2, mask // 2) if isinstance(mask, int) else (odd(mask), half(mask))
+        return odd(self.chip_x + mask_x) + 2 * odd(self.chip_y + mask_y)
 
     def across(self, mask):
         return (self.chip_at(mask), self.core)
@@ -69,7 +88,7 @@
 def meet(place):
     barrier = pltpu.get_barrier_semaphore()
     for device in place.peers():
-        pl.semaphore_signal(barrier, inc=1, device_id=device, device_id_type=MESH)
+        notify(barrier, device)
     pl.semaphore_wait(barrier, 3)
 
 
@@ -94,44 +113,45 @@
             return self.own_in.at[n, rows]
         if mask == 1:
             return self.kept_in.at[n, rows]
-        return self.got_in.at[lax.rem(n, 2), mask - 2, rows]
+        return self.got_in.at[odd(n), mask - 2, rows]
 
     def mine_out(self, n, mask):
         if mask == 0:
             return self.own_out.at[n]
         if mask == 2:
             return self.kept_out.at[n]
-        return self.got_out.at[lax.rem(n, 2), (mask - 1) // 2]
+        return self.got_out.at[odd(n), (mask - 1) // 2]
 
     def send_in(self, n, mask, unit):
         there = 1 if mask == 1 else 2
         block = self.place.chip_at(there ^ unit) * self.blocks
         src = self.mine_in(n, 1 if mask == 3 else 0, block, self.blocks)
         dst = self.mine_in(n, mask, block, self.blocks)
-        recv = self.in_recv.at[lax.rem(n, 2), mask - 1, unit]
-        return remote(src, dst, self.in_send.at[lax.rem(n, 2), mask - 1, unit], recv, self.place.across(there))
+        recv = self.in_recv.at[odd(n), mask - 1, unit]
+        return remote(src, dst, self.in_send.at[odd(n), mask - 1, unit], recv, self.place.across(there))
 
     def got_slice(self, n, mask, unit):
         dst = self.mine_in(n, mask, self.place.chip_at(unit) * self.blocks, self.blocks)
-        recv = self.in_recv.at[lax.rem(n, 2), mask - 1, unit]
-        return remote(dst, dst, self.in_send.at[lax.rem(n, 2), mask - 1, unit], recv, self.place.across(1))
+        recv = self.in_recv.at[odd(n), mask - 1, unit]
+        return remote(dst, dst, self.in_send.at[odd(n), mask - 1, unit], recv, self.place.across(1))
 
     def send_out(self, n, mask):
         src, dst = self.mine_out(n, 2 if mask == 3 else 0), self.mine_out(n, mask)
-        recv = self.out_recv.at[lax.rem(n, 2), mask - 1]
-        return remote(src, dst, self.out_send.at[lax.rem(n, 2), mask - 1], recv, self.place.across(2 if mask == 2 else 1))
-
-    def push(self, n, keep):
-        for unit in self.order:
-            for mask in (1, 2) if keep else (2, 3):
+        recv = self.out_recv.at[odd(n), mask - 1]
+        return remote(src, dst, self.out_send.at[odd(n), mask - 1], recv, self.place.across(2 if mask == 2 else 1))
+
+    def push_in(self, n, masks, units):
+        for unit in units:
+            for mask in masks:
                 self.send_in(n, mask, unit).start()
-        for mask in (1, 2) if keep else (1, 3):
+
+    def push_out(self, n, masks):
+        for mask in masks:
             self.send_out(n, mask).start()
 
-    def relay_in(self, n):
-        for unit in self.order:
-            self.got_slice(n, 1, 2 ^ unit).wait_recv()
-            self.send_in(n, 3, unit).start()
+    def relay_in(self, n, unit):
+        self.got_slice(n, 1, 2 ^ unit).wait_recv()
+        self.send_in(n, 3, unit).start()
 
     def relay_out(self, n):
         self.send_out(n, 2).wait_recv()
@@ -145,7 +165,7 @@
             self.send_out(n, mask).wait_send()
 
     def twin_copies(self, n, unit):
-        slot, block = lax.rem(n, 2), self.place.chip_at(unit) * self.blocks
+        slot, block = odd(n), self.place.chip_at(unit) * self.blocks
         return [
             remote(
                 self.mine_in(n, mask, block, self.blocks),
@@ -158,7 +178,7 @@
         ]
 
     def twin_out_copy(self, n, mask, unit):
-        slot = lax.rem(n, 2)
+        slot = odd(n)
         recv = self.twin_out_recv.at[slot, unit]
         return remote(self.mine_out(n, mask), self.twin_out.at[slot, unit], self.twin_out_send.at[unit], recv, self.place.twin())
 
@@ -190,9 +210,9 @@
         block = self.place.chip_at(unit) * self.blocks + parity * count
         copies = []
         for mask in range(CHIPS):
-            for which in range(2):
+            for which in range(TWO):
                 shard = 2 * self.place.chip_at(mask) + (self.place.core if which == 0 else 1 - self.place.core)
-                src = self.mine_in(n, mask, block, count) if which == 0 else self.twin_in.at[lax.rem(n, 2), mask, pl.ds(block, count)]
+                src = self.mine_in(n, mask, block, count) if which == 0 else self.twin_in.at[odd(n), mask, pl.ds(block, count)]
                 row = pl.ds(pl.multiple_of(shard * depth, depth), depth)
                 copies.append(pltpu.make_async_copy(src, w_in_v.at[v, :, row], sem.at[v, 2 * mask + which]))
         return copies
@@ -201,11 +221,11 @@
         parity = 1 - self.place.core - mine + 2 * self.place.core * mine
         for copy in self.load_in(n, unit, parity, w_in_v, v, sem):
             copy.start()
-        last = sem.at[v, 2 * CHIPS]
+        last = sem.at[v, SHARDS]
 
         @pl.when(mine == 0)
         def _():
-            pltpu.make_async_copy(self.twin_out.at[lax.rem(n, 2), unit], w_out_v.at[v], last).start()
+            pltpu.make_async_copy(self.twin_out.at[odd(n), unit], w_out_v.at[v], last).start()
 
         for mask in range(CHIPS):
 
@@ -216,7 +236,7 @@
     def loaded(self, w_in_v, w_out_v, v, sem):
         for copy in self.load_in(0, 0, 0, w_in_v, v, sem):
             copy.wait()
-        pltpu.make_async_copy(self.own_out.at[0], w_out_v.at[v], sem.at[v, 2 * CHIPS]).wait()
+        pltpu.make_async_copy(self.own_out.at[0], w_out_v.at[v], sem.at[v, SHARDS]).wait()
 
 
 class Pace:
@@ -229,26 +249,81 @@
         self.stream.load(self.layer_at(q), self.unit_at(i), b, self.w_in_v, self.w_out_v, b, self.load_sem)
 
     def head(self):
-        self.stream.push(self.layer_at(0), self.keep)
+        n, units = self.layer_at(0), self.stream.order
+        if not self.keep:
+            self.stream.push_in(n, (2, 3), units)
+            self.stream.push_out(n, (1, 3))
+            return
+        self.stream.push_in(n, (1,), [units[at] for at in (0, 2, 1, 3)])
+        self.stream.push_in(n, (2,), units[:1])
+        self.stream.push_out(n, (1,))
 
     def head_end(self):
+        n, units = self.layer_at(0), self.stream.order
         if self.keep:
-            self.stream.relay_in(self.layer_at(0))
-        self.stream.forward(self.layer_at(0), self.unit_at(0))
-        self.stream.arrive(self.layer_at(0), self.unit_at(0))
-        self.load(0, 0, 0)
-        self.stream.forwarded(self.layer_at(0), self.unit_at(0))
+            for at, unit in enumerate(units):
+                if at:
+                    self.stream.push_in(n, (2,), (unit,))
+                self.stream.relay_in(n, unit)
+                if at == 1:
+                    self.stream.push_out(n, (2,))
+        self.first_chunk(0)
+
+    def first_chunk(self, q):
+        n, unit = self.layer_at(q), self.unit_at(0)
+        self.stream.forward(n, unit)
+        self.stream.arrive(n, unit)
+        self.load(q, 0, 0)
+        self.stream.forwarded(n, unit)
 
     def sends(self, q, s):
-        i, b = lax.div(s, 2), lax.rem(s, 2)
+        i, b = half(s), odd(s)
+        early = (q + 1 < self.layers) & (q > 0) if self.keep else q + 1 < self.layers
         return [
-            ((b == 0) & (i == 3) & (q + 1 < self.layers), q + 1, 0),
+            ((b == 0) & (i == 3) & early, q + 1, 0),
             ((b == 0) & (i < 3) & (q > 0), q, i + 1),
             ((b == 1) & (i < 3) & (q == 0), q, i + 1),
         ]
 
+    def push_parts(self, q, s):
+        stream, units = self.stream, self.stream.order
+        there, more = self.layer_at(q + 1), q + 1 < self.layers
+        if not self.keep:
+
+            @pl.when((s == 0) & more)
+            def _():
+                stream.push_in(there, (2, 3), units[:2])
+                stream.push_out(there, (1,))
+
+            @pl.when((s == 1) & more)
+            def _():
+                stream.push_out(there, (3,))
+
+            @pl.when((s == 6) & more)
+            def _():
+                stream.push_in(there, (2, 3), units[2:])
+
+            return
+
+        @pl.when((s == 0) & (q > 0) | (s == 3) & (q == 0))
+        def _():
+            stream.relay_out(self.layer_at(q))
+
+        @pl.when((s == 0) & more)
+        def _():
+            stream.push_in(there, (1, 2), units)
+
+        @pl.when(((s == 0) & (q > 0) | (s == 3) & (q == 0)) & more)
+        def _():
+            stream.push_out(there, (1, 2))
+
+        @pl.when((s == 5) & more)
+        def _():
+            for unit in units:
+                stream.relay_in(there, unit)
+
     def before(self, q, s):
-        i, b = lax.div(s, 2), lax.rem(s, 2)
+        i, b = half(s), odd(s)
         more = q + 1 < self.layers
 
         @pl.when((s == 0) & (q > 0))
@@ -258,25 +333,11 @@
         @pl.when((s == 0) & more)
         def _():
             for at, device in enumerate(self.place.peers()):
-                pl.semaphore_signal(self.credit.at[at], inc=1, device_id=device, device_id_type=MESH)
+                notify(self.credit.at[at], device)
             for at in range(3):
-                pl.semaphore_wait(self.credit.at[at], 1)
-            self.stream.push(self.layer_at(q + 1), self.keep)
-
-        if self.keep:
-
-            @pl.when((s == 2) & (q == 0))
-            def _():
-                self.stream.relay_out(self.layer_at(0))
-
-            @pl.when(((s == 3) & (q > 0) | (s == 4) & (q == 0)) & more)
-            def _():
-                self.stream.relay_in(self.layer_at(q + 1))
-
-            @pl.when(((s == 5) & (q > 0) | (s == 7) & (q == 0)) & more)
-            def _():
-                self.stream.relay_out(self.layer_at(q + 1))
-
+                await_one(self.credit.at[at])
+
+        self.push_parts(q, s)
         for condition, count, unit in self.sends(q, s):
 
             @pl.when(condition)
@@ -287,7 +348,8 @@
         def _():
             self.load(q, i, 1)
 
-        for condition, count, unit in (((b == 1) & (i < 3), q, i + 1), ((s == 7) & more, q + 1, 0)):
+        early = more & (q > 0) if self.keep else more
+        for condition, count, unit in (((b == 1) & (i < 3), q, i + 1), ((s == 7) & early, q + 1, 0)):
 
             @pl.when(condition)
             def _():
@@ -302,6 +364,12 @@
             @pl.when(condition)
             def _():
                 self.stream.forwarded(self.layer_at(count), self.unit_at(unit))
+
+        if self.keep:
+
+            @pl.when((s == 7) & (q == 0) & (q + 1 < self.layers))
+            def _():
+                self.first_chunk(q + 1)
 
 
 def when(condition):
@@ -325,10 +393,13 @@
 def backward_mask(unit):
     if isinstance(unit, int):
         return BACKWARD_UNITS[unit]
-    return (1 - lax.div(unit, 2)) + 2 * lax.rem(lax.div(unit + 1, 2), 2)
+    return (1 - half(unit)) + 2 * lax.rem(half(unit + 1), 2)
 
 
 class Reduce:
+    PARTS = ((0, 1), (0, 0), (1, 1), (1, 0))
+    SECOND = (0, 1, 3, 4)
+
     def __init__(self, place, layers, hbm, vmem, sems, outs):
         self.place, self.layers = place, layers
         self.p_out, self.o_a, self.o_b, self.u_out, self.q_in, self.i_a, self.s_in, self.i_b = hbm
@@ -362,7 +433,7 @@
         self.chunk = self.in_a.shape[1]
 
     def slot(self, q):
-        return q % 2 if isinstance(q, int) else lax.rem(q, 2)
+        return q % 2 if isinstance(q, int) else odd(q)
 
     def twin_out(self):
         return remote(self.r_v, self.o_v, self.to_send, self.to_recv, self.place.twin())
@@ -403,7 +474,7 @@
         s = self.slot(q)
         return [
             pltpu.make_async_copy(self.r_v.at[:, pl.ds(h * self.half_out, self.half_out)], self.p_out.at[s, i, h], self.p_sem.at[h])
-            for h in range(2)
+            for h in range(TWO)
         ]
 
     def save_q(self, q, i, b, gm):
@@ -433,8 +504,8 @@
     def in_second(self, q, pair, b):
         s, near = self.slot(q), pl.ds(pl.multiple_of(self.place.chip_y * self.side, self.side), self.side)
         copies = []
-        for at in range(2):
-            i, rows = 2 * pair + at, pl.ds(at * self.side, self.side)
+        for at in range(TWO):
+            i, rows = TWO * pair + at, pl.ds(at * self.side, self.side)
             copies.append(pltpu.make_async_copy(self.q_in.at[s, i, b, near], self.in_a.at[rows], self.in_sem.at[0, at]))
             copies.append(pltpu.make_async_copy(self.i_a.at[s, i, b], self.in_b.at[rows], self.in_sem.at[1, at]))
         return copies
@@ -451,8 +522,8 @@
     def in_second_save(self, q, pair, b):
         s = self.slot(q)
         return [
-            pltpu.make_async_copy(self.in_a.at[pl.ds(at * self.side, self.side)], self.s_in.at[s, 2 * pair + at, b], self.in_save.at[at])
-            for at in range(2)
+            pltpu.make_async_copy(self.in_a.at[pl.ds(at * self.side, self.side)], self.s_in.at[s, TWO * pair + at, b], self.in_save.at[at])
+            for at in range(TWO)
         ]
 
     def in_third_save(self, q, b):
@@ -466,148 +537,156 @@
         return copies
 
     def add(self, a, b):
-        for start in range(0, a.shape[0], 64):
-            rows = pl.ds(start, 64)
+        for start in range(0, a.shape[0], ADD_ROWS):
+            rows = pl.ds(start, ADD_ROWS)
             a[rows, :] = a[rows, :] + b[rows, :]
 
     def free(self, semaphore):
-        pl.semaphore_signal(semaphore, inc=1, device_id=self.place.twin(), device_id_type=MESH)
+        notify(semaphore, self.place.twin())
 
     def start(self):
         for semaphore in (self.credit_o, self.credit_i.at[0], self.credit_i.at[1]):
             self.free(semaphore)
 
     def mid(self, q, s):
-        here = q < self.layers
-        older = q > 0
-
-        for t in range(8):
-            i, b = t // 2, t % 2
-            layer = q if t < 7 else q - 1
-
-            @when(both(s == (t + 1) % 8, here if t < 7 else older))
+        here, older, prev = q < self.layers, q > 0, q - 1
+
+        for t in range(STEPS):
+            i, b = divmod(t, TWO)
+            layer, real = (q, here) if t < 7 else (prev, older)
+
+            @when(both(s == (t + 1) % STEPS, real))
             def _():
                 self.twin_in(b).wait_send()
                 if b == 0:
                     self.twin_out().wait_send()
-                else:
-                    for copy in self.save_p(layer, i):
-                        copy.wait()
-                    self.save_q(layer, i, 1, 0).wait()
-                    if i < 2:
-                        for h in range(2):
-                            self.resend(layer, lambda q, h=h: self.across_x_out(q, i, h))
-                    self.resend(layer, lambda q: self.across_y_in(q, i, 1))
-
-            layer = q if t < 5 else q - 1
+                    return
+                for copy in self.save_p(layer, i):
+                    copy.wait()
+                self.save_q(layer, i, 1, 0).wait()
+
+            layer, real = (q, here) if t < 5 else (prev, older)
             if b == 0:
 
-                @when(both(s == (t + 3) % 8, here if t < 5 else older))
+                @when(both(s == (t + 3) % STEPS, real))
                 def _():
                     self.save_q(layer, i, 0, 0).wait()
-                    self.resend(layer, lambda q: self.across_y_in(q, i, 0))
-
-        for step, pair, b, late in ((6, 0, 1, 0), (7, 0, 0, 0), (2, 1, 1, 1), (3, 1, 0, 1)):
-            layer = q - late
-
-            @when(both(s == step, older if late else here))
-            def _():
-                for copy in self.in_second_save(layer, pair, b):
+
+        for (pair, b), step in zip(self.PARTS, self.SECOND):
+
+            @when(both(s == step + 1, older))
+            def _():
+                for copy in self.in_second_save(prev, pair, b):
                     copy.wait()
-                for at in range(2):
-                    self.resend(layer, lambda q, at=at: self.across_x_in(q, 2 * pair + at, b))
-
-        for step, b in ((4, 1), (5, 0)):
+                for at in range(TWO):
+                    self.resend(prev, lambda q, at=at: self.across_x_in(q, TWO * pair + at, b))
+
+        for i in range(CHIPS):
+            layer, real = (q, here) if i < 3 else (prev, older)
+
+            @when(both(s == (2 * i + 3) % STEPS, real))
+            def _():
+                for b in (1, 0):
+                    self.resend(layer, lambda q, b=b: self.across_y_in(q, i, b))
+
+        for at in range(CHIPS):
+
+            @when(both(s == 3 + at, here))
+            def _():
+                i, h = divmod(at, TWO)
+                self.resend(q, lambda q: self.across_x_out(q, i, h))
+
+        for h in range(TWO):
+
+            @when(both(s == 1 + h, older))
+            def _():
+                self.out_second_save(prev, h).wait()
+
+            @when(both(s == 2 + 2 * h, older))
+            def _():
+                self.resend(prev, lambda q: self.across_y_out(q, h))
+
+            @when(both(s == 5 + 2 * h, older))
+            def _():
+                self.out_third_save(prev, h).wait()
+
+        @when(both(s == 7, older))
+        def _():
+            for copy in self.in_third_save(prev, 1):
+                copy.wait()
+
+        @when(both(s == 0, q > 1))
+        def _():
+            for copy in self.in_third_save(q - 2, 0):
+                copy.wait()
+
+        for (pair, b), step in zip(self.PARTS, self.SECOND):
 
             @when(both(s == step, older))
             def _():
-                for copy in self.in_third_save(q - 1, b):
-                    copy.wait()
-
-        for step, pair, b, late in ((5, 0, 1, 0), (6, 0, 0, 0), (1, 1, 1, 1), (2, 1, 0, 1)):
-            layer = q - late
-
-            @when(both(s == step, older if late else here))
-            def _():
-                for at in range(2):
-                    there = 2 * pair + 1 - at
-                    self.across_y_in(layer, there, b).wait_recv()
-                for copy in self.in_second(layer, pair, b):
+                for at in range(TWO):
+                    self.across_y_in(prev, TWO * pair + 1 - at, b).wait_recv()
+                for copy in self.in_second(prev, pair, b):
                     copy.start()
 
-        for step, b in ((3, 1), (4, 0)):
-
-            @when(both(s == step, older))
+        for b in range(TWO):
+
+            @when(both(s == 7 - b, older))
             def _():
                 for i in range(CHIPS):
-                    self.across_x_in(q - 1, 3 - i, b).wait_recv()
-                for copy in self.in_third(q - 1, b):
+                    self.across_x_in(prev, 3 - i, b).wait_recv()
+                for copy in self.in_third(prev, b):
                     copy.start()
 
-        for step, h in ((1, 0), (2, 1)):
-
-            @when(both(s == step, older))
-            def _():
-                self.out_second_save(q - 1, h).wait()
-                self.resend(q - 1, lambda q: self.across_y_out(q, h))
-
-        for step, h in ((5, 0), (6, 1)):
-
-            @when(both(s == step, older))
-            def _():
-                self.out_third_save(q - 1, h).wait()
-
         @when(both(s == 7, here))
         def _():
-            for h in range(2):
+            for h in range(TWO):
                 self.across_x_out(q, 0, h).wait_recv()
             for copy in self.out_first(q):
                 copy.start()
 
-        for step, h in ((0, 0), (1, 1)):
-
-            @when(both(s == step, older))
-            def _():
-                self.across_x_out(q - 1, 1, h).wait_recv()
-                for copy in self.out_second(q - 1, h):
+        for h in range(TWO):
+
+            @when(both(s == h, older))
+            def _():
+                self.across_x_out(prev, 1, h).wait_recv()
+                for copy in self.out_second(prev, h):
                     copy.start()
 
-        for step, h in ((4, 0), (5, 1)):
-
-            @when(both(s == step, older))
-            def _():
-                self.across_y_out(q - 1, h).wait_recv()
-                for copy in self.out_third(q - 1, h):
+            @when(both(s == 4 + 2 * h, older))
+            def _():
+                self.across_y_out(prev, h).wait_recv()
+                for copy in self.out_third(prev, h):
                     copy.start()
 
     def end(self, q, s, gm):
-        here = q < self.layers
-        older = q > 0
-        final = q == self.layers - 1
-
-        for t in range(8):
-            i, b = t // 2, t % 2
+        here, older, prev = q < self.layers, q > 0, q - 1
+        old = (gm + 1) % 3 if isinstance(gm, int) else lax.rem(gm + 1, 3)
+
+        for t in range(STEPS):
+            i, b = divmod(t, TWO)
 
             @when(both(s == t, here))
             def _():
-                pl.semaphore_wait(self.credit_i.at[b], 1)
+                more = True if i < 3 else q < self.layers - 1
+                await_one(self.credit_i.at[b])
                 self.twin_in(b).start()
                 if b == 0:
-                    pl.semaphore_wait(self.credit_o, 1)
+                    await_one(self.credit_o)
                     self.twin_out().start()
                     return
                 self.twin_out().wait_recv()
                 self.add(self.r_v, self.o_v)
 
-                @when(True if i < 3 else q < self.layers - 1)
+                @when(more)
                 def _():
                     self.free(self.credit_o)
 
                 if i == 3:
                     for copy in self.out_first(q):
                         copy.wait()
-                    for start in range(0, self.r_v.shape[0], 64):
-                        rows = pl.ds(start, 64)
+                    for start in range(0, self.r_v.shape[0], ADD_ROWS):
+                        rows = pl.ds(start, ADD_ROWS)
                         for h, part in enumerate((self.out_a, self.out_b)):
                             columns = pl.ds(h * self.half_out, self.half_out)
                             self.r_v[rows, columns] = self.r_v[rows, columns] + part[rows, :]
@@ -616,17 +695,16 @@
                 self.twin_in(0).wait_recv()
                 self.add(self.gm_v.at[gm], self.it_v.at[0])
 
-                @when(True if i < 3 else q < self.layers - 1)
+                @when(more)
                 def _():
                     self.free(self.credit_i.at[0])
 
                 self.save_q(q, i, 1, gm).start()
 
             if b == 0:
-                layer = q if t < 6 else q - 1
-                old = (gm + 1) % 3 if isinstance(gm, int) else lax.rem(gm + 1, 3)
-
-                @when(both(s == (t + 2) % 8, here if t < 6 else older))
+                layer, real = (q, here) if t < 6 else (prev, older)
+
+                @when(both(s == (t + 2) % STEPS, real))
                 def _():
                     self.twin_in(1).wait_recv()
                     self.add(self.gm_v.at[old], self.it_v.at[1])
@@ -637,57 +715,47 @@
 
                     self.save_q(layer, i, 0, old).start()
 
-        for step, pair, b, late in ((5, 0, 1, 0), (6, 0, 0, 0), (1, 1, 1, 1), (2, 1, 0, 1)):
-            layer = q - late
-
-            @when(both(s == step, older if late else here))
-            def _():
-                for copy in self.in_second(layer, pair, b):
-                    copy.wait()
-                self.add(self.in_a, self.in_b)
-                for copy in self.in_second_save(layer, pair, b):
-                    copy.start()
-
-        for step, b in ((3, 1), (4, 0)):
+        def summed(parts, loads, saves):
+            for copy in loads:
+                copy.wait()
+            self.add(*parts)
+            for copy in saves:
+                copy.start()
+
+        ins, outs = (self.in_a, self.in_b), (self.out_a, self.out_b)
+        for (pair, b), step in zip(self.PARTS, self.SECOND):
 
             @when(both(s == step, older))
             def _():
-                for copy in self.in_third(q - 1, b):
-                    copy.wait()
-                self.add(self.in_a, self.in_b)
-                for copy in self.in_third_save(q - 1, b):
-                    copy.start()
-
-        for step, h in ((0, 0), (1, 1)):
-
-            @when(both(s == step, older))
-            def _():
-                for copy in self.out_second(q - 1, h):
-                    copy.wait()
-                self.add(self.out_a, self.out_b)
-                self.out_second_save(q - 1, h).start()
-
-        for step, h in ((4, 0), (5, 1)):
-
-            @when(both(s == step, older))
-            def _():
-                for copy in self.out_third(q - 1, h):
-                    copy.wait()
-                self.add(self.out_a, self.out_b)
-                self.out_third_save(q - 1, h).start()
+                summed(ins, self.in_second(prev, pair, b), self.in_second_save(prev, pair, b))
+
+        for b in range(TWO):
+
+            @when(both(s == 7 - b, older))
+            def _():
+                summed(ins, self.in_third(prev, b), self.in_third_save(prev, b))
+
+            @when(both(s == b, older))
+            def _():
+                summed(outs, self.out_second(prev, b), [self.out_second_save(prev, b)])
+
+            @when(both(s == 4 + 2 * b, older))
+            def _():
+                summed(outs, self.out_third(prev, b), [self.out_third_save(prev, b)])
 
     def finish(self):
         q = self.layers
-        for s in range(7):
+        last = q - 1
+        for s in range(STEPS):
             self.mid(q, s)
-            if s < 6:
-                self.end(q, s, (8 * q + s) % 3)
-        last = q - 1
-        for h in range(2):
-            for i in range(2):
+            self.end(q, s, (STEPS * q + s) % 3)
+        for copy in self.in_third_save(last, 0):
+            copy.wait()
+        for h in range(TWO):
+            for i in range(TWO):
                 self.across_x_out(last, i, h).wait_send()
             self.across_y_out(last, h).wait_send()
-        for b in range(2):
+        for b in range(TWO):
             for i in range(CHIPS):
                 self.across_y_in(last, i, b).wait_send()
                 self.across_x_in(last, i, b).wait_send()
@@ -703,28 +771,27 @@
     tokens, width = x_v.shape
     tiles = tokens // TOK_TILE
 
-    def to_lanes(n):
-        pairs = ((w_in_ref, stage_in, own_in, 0), (w_out_ref, stage_out, own_out, 1))
-        for src, stage, _, at in pairs:
-            for b in range(stage.shape[0]):
-                pltpu.make_async_copy(src.at[n, :, pl.ds(b * LANES, LANES)], stage.at[b], stage_sem.at[at]).start()
-        for _, stage, own, at in pairs:
-            pltpu.make_async_copy(own.at[n], stage, stage_sem.at[at]).wait()
-            pltpu.make_async_copy(stage, own.at[n], stage_sem.at[at]).start()
-        for _, stage, own, at in pairs:
-            pltpu.make_async_copy(stage, own.at[n], stage_sem.at[at]).wait()
+    pairs = ((w_in_ref, stage_in, own_in, 0), (w_out_ref, stage_out, own_out, 1))
+
+    def to_lanes(n, phase):
+        for src, stage, own, at in pairs:
+            if phase == 0:
+                for b in range(stage.shape[0]):
+                    pltpu.make_async_copy(src.at[n, :, pl.ds(b * LANES, LANES)], stage.at[b], stage_sem.at[at]).start()
+            elif phase == 1:
+                pltpu.make_async_copy(own.at[n], stage, stage_sem.at[at]).wait()
+                pltpu.make_async_copy(stage, own.at[n], stage_sem.at[at]).start()
+            else:
+                pltpu.make_async_copy(stage, own.at[n], stage_sem.at[at]).wait()
 
     fetch = pltpu.make_async_copy(x_ref, x_v, x_sem)
+    for phase in range(3):
+        to_lanes(0, phase)
     fetch.start()
-    to_lanes(0)
     meet(place)
     pace.head()
-
-    def other_lanes(n, carry):
-        to_lanes(n)
-        return carry
-
-    lax.fori_loop(1, layers, other_lanes, 0)
+    for phase in range(3):
+        to_lanes(1, phase)
     fetch.wait()
 
     def first_unit(t, carry):
@@ -768,8 +835,13 @@
             finish()
 
     def step(n, s):
-        v = lax.rem(s, 2)
+        v = odd(s)
         pace.before(n, s)
+        for phase in range(3):
+
+            @pl.when((s == 1 + phase) & (n + 2 < layers))
+            def _():
+                to_lanes(n + 2, phase)
 
         @pl.when(s < 7)
         def _():
@@ -787,7 +859,7 @@
         pace.after(n, s)
 
     def layer_step(n, carry):
-        lax.fori_loop(0, 8, lambda s, c: (step(n, s), c)[1], 0)
+        lax.fori_loop(0, STEPS, lambda s, c: (step(n, s), c)[1], 0)
         return carry
 
     lax.fori_loop(0, layers, layer_step, 0)
@@ -827,7 +899,7 @@
         copy.start()
 
     def fetch(n, which, t):
-        dst, sem = x_v.at[which, lax.rem(t, 2)], x_sem.at[which, lax.rem(t, 2)]
+        dst, sem = x_v.at[which, odd(t)], x_sem.at[which, odd(t)]
 
         @pl.when(n > 0)
         def _():
@@ -838,7 +910,7 @@
             pltpu.make_async_copy(x_ref.at[tile_rows(t)], dst, sem).start()
 
     def fetched(which, t):
-        at = lax.rem(t, 2)
+        at = odd(t)
         pltpu.make_async_copy(x_ref.at[tile_rows(0)], x_v.at[which, at], x_sem.at[which, at]).wait()
         return x_v[which, at]
 
@@ -898,9 +970,9 @@
         gm_v[gm] = lax.dot_general(unit_of(place.core), dpre, FIRST_FIRST, preferred_element_type=F32)
 
     def step(q, s):
-        gm = lax.rem(8 * q + s, 3)
+        gm = lax.rem(STEPS * q + s, 3)
         pace.before(q, s)
-        hidden_part(lax.rem(s, 2))
+        hidden_part(odd(s))
         sums.mid(q, s)
         gradient_part(gm)
         sums.end(q, s, gm)
@@ -908,7 +980,7 @@
 
     def layer_step(q, carry):
         n = layers - 1 - q
-        lax.fori_loop(0, 8, lambda s, c: (step(q, s), c)[1], 0)
+        lax.fori_loop(0, STEPS, lambda s, c: (step(q, s), c)[1], 0)
         fetch(n, 0, 0)
 
         @pl.when(n > 0)
@@ -953,7 +1025,7 @@
 
 def stream_semaphores():
     dma = pltpu.SemaphoreType.DMA
-    return [dma((2, 3, 4)), dma((2, 3, 4)), dma((2, 3)), dma((2, 3)), dma((4, 4)), dma((2, 4, 4)), dma((4,)), dma((2, 4))]
+    return [dma((TWO, 3, CHIPS))] * TWO + [dma((TWO, 3))] * TWO + [dma((CHIPS, CHIPS)), dma((TWO, CHIPS, CHIPS)), dma((CHIPS,)), dma((TWO, CHIPS))]
 
 
 def sum_semaphores():
@@ -961,33 +1033,33 @@
     return [
         dma,
         dma,
-        dma((2,)),
-        dma((2,)),
-        dma((2, 2)),
-        dma((2, 2, 2)),
-        dma((2,)),
-        dma((2, 2)),
-        dma((4, 2)),
-        dma((2, 4, 2)),
-        dma((4, 2)),
-        dma((2, 4, 2)),
-        dma((2,)),
-        dma((2,)),
-        dma((2,)),
-        dma((2, 4)),
+        dma((TWO,)),
+        dma((TWO,)),
+        dma((TWO, TWO)),
+        dma((TWO, TWO, TWO)),
+        dma((TWO,)),
+        dma((TWO, TWO)),
+        dma((CHIPS, TWO)),
+        dma((TWO, CHIPS, TWO)),
+        dma((CHIPS, TWO)),
+        dma((TWO, CHIPS, TWO)),
+        dma((TWO,)),
+        dma((TWO,)),
+        dma((TWO,)),
+        dma((TWO, CHIPS)),
         dma,
-        dma((4,)),
+        dma((CHIPS,)),
         regular,
-        regular((2,)),
+        regular((TWO,)),
     ]
 
 
 def stream_buffers(piece_in, piece_out):
     return [
-        jax.ShapeDtypeStruct((2, 2) + piece_in, BF16),
-        jax.ShapeDtypeStruct((2, 2) + piece_out, BF16),
-        jax.ShapeDtypeStruct((2, CHIPS) + piece_in, BF16),
-        jax.ShapeDtypeStruct((2, CHIPS) + piece_out, BF16),
+        jax.ShapeDtypeStruct((TWO, TWO) + piece_in, BF16),
+        jax.ShapeDtypeStruct((TWO, TWO) + piece_out, BF16),
+        jax.ShapeDtypeStruct((TWO, CHIPS) + piece_in, BF16),
+        jax.ShapeDtypeStruct((TWO, CHIPS) + piece_out, BF16),
     ]
 
 
@@ -1010,13 +1082,13 @@
             pltpu.VMEM((tokens, width), BF16),
             pltpu.VMEM((width // LANES, tokens, LANES), BF16),
             pltpu.VMEM((tokens, width), F32),
-            pltpu.VMEM((2, chunk // LANES, width, LANES), BF16),
-            pltpu.VMEM((2, width // LANES, chunk, LANES), BF16),
+            pltpu.VMEM((TWO, chunk // LANES, width, LANES), BF16),
+            pltpu.VMEM((TWO, width // LANES, chunk, LANES), BF16),
             pltpu.VMEM(piece_in, BF16),
             pltpu.VMEM(piece_out, BF16),
             pltpu.SemaphoreType.DMA,
-            pltpu.SemaphoreType.DMA((2, 2 * CHIPS + 1)),
-            pltpu.SemaphoreType.DMA((2,)),
+            pltpu.SemaphoreType.DMA((TWO, SHARDS + 1)),
+            pltpu.SemaphoreType.DMA((TWO,)),
             pltpu.SemaphoreType.REGULAR((3,)),
         ]
         + stream_semaphores(),
@@ -1041,14 +1113,14 @@
         [sums(layers, depth, hidden_size), sums(layers, chunk, width), jax.ShapeDtypeStruct((tokens, width), BF16)]
         + stream_buffers(own_in.shape[1:], own_out.shape[1:])
         + [
-            sums(2, 4, 2, chunk, half),
-            sums(2, 2, 2, chunk, half),
-            sums(2, 2, chunk, half),
-            sums(2, 2, chunk, half),
-            sums(2, 4, 2, half, chunk),
-            sums(2, 4, 2, quarter, chunk),
-            sums(2, 4, 2, quarter, chunk),
-            sums(2, 4, 2, depth, chunk),
+            sums(TWO, CHIPS, TWO, chunk, half),
+            sums(TWO, TWO, TWO, chunk, half),
+            sums(TWO, TWO, chunk, half),
+            sums(TWO, TWO, chunk, half),
+            sums(TWO, CHIPS, TWO, half, chunk),
+            sums(TWO, CHIPS, TWO, quarter, chunk),
+            sums(TWO, CHIPS, TWO, quarter, chunk),
+            sums(TWO, CHIPS, TWO, depth, chunk),
         ]
     )
     outs = pl.pallas_call(
@@ -1062,21 +1134,21 @@
             pltpu.VMEM((tokens, width), F32),
             pltpu.VMEM((chunk // LANES, tokens, LANES), BF16),
             pltpu.VMEM((chunk // LANES, tokens, LANES), BF16),
-            pltpu.VMEM((2, chunk // LANES, width, LANES), BF16),
-            pltpu.VMEM((2, blocks_d, chunk, LANES), BF16),
-            pltpu.VMEM((2, 2, TOK_TILE, width), BF16),
+            pltpu.VMEM((TWO, chunk // LANES, width, LANES), BF16),
+            pltpu.VMEM((TWO, blocks_d, chunk, LANES), BF16),
+            pltpu.VMEM((TWO, TWO, TOK_TILE, width), BF16),
             pltpu.VMEM((chunk, width), F32),
             pltpu.VMEM((half, chunk), F32),
             pltpu.VMEM((3, half, chunk), F32),
             pltpu.VMEM((chunk, width), F32),
-            pltpu.VMEM((2, half, chunk), F32),
+            pltpu.VMEM((TWO, half, chunk), F32),
             pltpu.VMEM((chunk, half), F32),
             pltpu.VMEM((chunk, half), F32),
             pltpu.VMEM((half, chunk), F32),
             pltpu.VMEM((half, chunk), F32),
             pltpu.SemaphoreType.DMA((blocks_d,)),
-            pltpu.SemaphoreType.DMA((2, 2)),
-            pltpu.SemaphoreType.DMA((2, 2 * CHIPS + 1)),
+            pltpu.SemaphoreType.DMA((TWO, TWO)),
+            pltpu.SemaphoreType.DMA((TWO, SHARDS + 1)),
             pltpu.SemaphoreType.REGULAR((3,)),
         ]
         + stream_semaphores()

time: 1910 us -> 1710 us (0.90)
  Pallas kernels: 1870 us -> 1660 us
    pallas_call x1, Pallas kernels: 1380 us -> 1200 us  [backward_stack(): pl.pallas_call(functools.partial(backward_stack_kernel, layers), in_specs...]
    pallas_call x1, Pallas kernels: 488 us -> 461 us  [forward_stack(): pl.pallas_call(functools.partial(forward_stack_kernel, layers), in_specs=...]
where the time goes in v5:
time: 1710 us; the launch traced here: 1690 us
  Pallas kernels  1660 us (97%)
  local copies, waits for them, and re-layouts  29.3 us (2%)
    pallas_call x1, Pallas kernels, backward_stack(): pl.pallas_call(functools.partial(backward_stack_kernel, layers), in_specs...  1200 us
    pallas_call x1, Pallas kernels, forward_stack(): pl.pallas_call(functools.partial(forward_stack_kernel, layers), in_specs=...  461 us

profile of v5, /device:TPU:0, one launch (start us, length us, event | category | flops | bytes accessed | tf_op | source)
XLA Modules:
  0.0 1693.0 jit_solution(13685093350054471122)
XLA Ops:
  0.6 461.1 %forward_stack.1 = (bf16[5,4096,1024]{2,1,0:T(8,128)(2,1)}, bf16[5,32,128,128]{3,2,1,0:T(8,128)(2,1)}, bf16[5,8,512,128]{3,2,1,0:T(8,128)(2,1)}, bf16[5,32,128,1...) custom-call(bf16[4096,1024]{1,0:T(8,128)(2,1)} %x_ref.3, ...), custom_call_target="tpu_custom_call" | custom-call | flops 343597383680 | bytes 100000000 | tf_op jit(solution)/shard_map/forward_stack/pallas_call | solution.py:1076
  461.7 1201.6 %backward_stack.1 = (f32[5,128,4096]{2,1,0:T(8,128)}, f32[5,512,1024]{2,1,0:T(8,128)}, bf16[4096,1024]{1,0:T(8,128)(2,1)}, bf16[2,2,32,128,128]{4,3,2,1,0:T(8,12...) custom-call(bf16[4096,1024]{1,0:T(8,128)(2,1)} %x_ref.3, ...), custom_call_target="tpu_custom_call" | custom-call | flops 858993459200 | bytes 300000000 | tf_op jit(solution)/shard_map/backward_stack/pallas_call | solution.py:1126
  1663.3 0.0 slice-start
  1663.3 0.0 slice-start.1
  1663.3 8.0 slice_bitcast_fusion
  1671.3 0.0 slice-start.2
  1671.3 9.5 copy.11
  1680.8 0.0 slice-done
  1680.8 0.0 slice-done.1
  1680.8 0.0 slice-done.2
  1680.8 4.1 copy.12
  1684.9 7.8 copy.13
  (1 shorter events, 0.0 us)
Async XLA Ops:
  1663.3 17.5 %slice-start = ((s8[10485760]{0:T(1024)(128)(4,1)}), s8[4194304]{0:T(1024)(128)(4,1)S(1)}, s32[]{:S(2)}) async-start(s8[10485760]{0:T(1024)(128)(4,1)} %bitcast.2), calls=%async_computation | async-start | bytes 8388608
  1663.3 17.5 %slice-start.1 = ((s8[10485760]{0:T(1024)(128)(4,1)}), s8[2097152]{0:T(1024)(128)(4,1)S(1)}, s32[]{:S(2)}) async-start(s8[10485760]{0:T(1024)(128)(4,1)} %bitcast.2), calls=%async_computation.1 | async-start | bytes 4194304
  1671.3 9.5 slice-start.2

commit v6 on v5

--- a/solution.py
+++ b/solution.py
@@ -50,11 +50,34 @@
 
 
 def odd(x):
-    return lax.rem(x, TWO)
+    return x % TWO if isinstance(x, int) else lax.rem(x, TWO)
 
 
 def half(x):
-    return lax.div(x, TWO)
+    return x // TWO if isinstance(x, int) else lax.div(x, TWO)
+
+
+def when(condition):
+    if isinstance(condition, bool):
+        return lambda body: body() if condition else None
+    return pl.when(condition)
+
+
+def both(*conditions):
+    kept = [c for c in conditions if not (isinstance(c, bool) and c)]
+    if any(isinstance(c, bool) for c in kept):
+        return False
+    if not kept:
+        return True
+    return functools.reduce(lambda a, b: a & b, kept)
+
+
+def by_step(s, body):
+    for k in range(STEPS):
+
+        @pl.when(s == k)
+        def _():
+            body(k)
 
 
 def notify(semaphore, device):
@@ -189,7 +212,7 @@
             copy.start()
         for mask in range(CHIPS):
 
-            @pl.when(unit == mask)
+            @when(unit == mask)
             def _():
                 if mask in (1, 3):
                     self.send_out(n, mask).wait_recv()
@@ -223,13 +246,13 @@
             copy.start()
         last = sem.at[v, SHARDS]
 
-        @pl.when(mine == 0)
+        @when(mine == 0)
         def _():
             pltpu.make_async_copy(self.twin_out.at[odd(n), unit], w_out_v.at[v], last).start()
 
         for mask in range(CHIPS):
 
-            @pl.when((mine == 1) & (unit == mask))
+            @when(both(mine == 1, unit == mask))
             def _():
                 pltpu.make_async_copy(self.mine_out(n, mask), w_out_v.at[v], last).start()
 
@@ -252,22 +275,25 @@
         n, units = self.layer_at(0), self.stream.order
         if not self.keep:
             self.stream.push_in(n, (2, 3), units)
-            self.stream.push_out(n, (1, 3))
+            self.stream.push_out(n, (3, 1))
             return
-        self.stream.push_in(n, (1,), [units[at] for at in (0, 2, 1, 3)])
+        self.stream.push_in(n, (1,), [units[at] for at in (0, 2, 3, 1)])
         self.stream.push_in(n, (2,), units[:1])
         self.stream.push_out(n, (1,))
 
     def head_end(self):
         n, units = self.layer_at(0), self.stream.order
-        if self.keep:
-            for at, unit in enumerate(units):
-                if at:
-                    self.stream.push_in(n, (2,), (unit,))
-                self.stream.relay_in(n, unit)
-                if at == 1:
-                    self.stream.push_out(n, (2,))
-        self.first_chunk(0)
+        if not self.keep:
+            self.first_chunk(0)
+            return
+        for at, unit in enumerate(units):
+            if at:
+                self.stream.push_in(n, (2,), (unit,))
+            if at == 3:
+                self.first_chunk(0)
+            self.stream.relay_in(n, unit)
+            if at == 1:
+                self.stream.push_out(n, (2,))
 
     def first_chunk(self, q):
         n, unit = self.layer_at(q), self.unit_at(0)
@@ -280,9 +306,9 @@
         i, b = half(s), odd(s)
         early = (q + 1 < self.layers) & (q > 0) if self.keep else q + 1 < self.layers
         return [
-            ((b == 0) & (i == 3) & early, q + 1, 0),
-            ((b == 0) & (i < 3) & (q > 0), q, i + 1),
-            ((b == 1) & (i < 3) & (q == 0), q, i + 1),
+            (both(s == 6, early), q + 1, 0),
+            (both(b == 0 and i < 3, q > 0), q, i + 1),
+            (both(b == 1 and i < 3, q == 0), q, i + 1),
         ]
 
     def push_parts(self, q, s):
@@ -290,34 +316,33 @@
         there, more = self.layer_at(q + 1), q + 1 < self.layers
         if not self.keep:
 
-            @pl.when((s == 0) & more)
-            def _():
-                stream.push_in(there, (2, 3), units[:2])
-                stream.push_out(there, (1,))
-
-            @pl.when((s == 1) & more)
-            def _():
-                stream.push_out(there, (3,))
-
-            @pl.when((s == 6) & more)
-            def _():
-                stream.push_in(there, (2, 3), units[2:])
+            for at, (step, mask) in enumerate(((1, 3), (4, 1))):
+
+                @when(both(s == 3 * at, more))
+                def _():
+                    stream.push_in(there, (2, 3), units[TWO * at : TWO * at + TWO])
+
+                @when(both(s == step, more))
+                def _():
+                    stream.push_out(there, (mask,))
 
             return
 
-        @pl.when((s == 0) & (q > 0) | (s == 3) & (q == 0))
+        turn = q > 0 if s == 0 else q == 0
+
+        @when(both(s in (0, 3), turn))
         def _():
             stream.relay_out(self.layer_at(q))
 
-        @pl.when((s == 0) & more)
+        @when(both(s == 0, more))
         def _():
             stream.push_in(there, (1, 2), units)
 
-        @pl.when(((s == 0) & (q > 0) | (s == 3) & (q == 0)) & more)
+        @when(both(s in (0, 3), turn, more))
         def _():
             stream.push_out(there, (1, 2))
 
-        @pl.when((s == 5) & more)
+        @when(both(s == 5, more))
         def _():
             for unit in units:
                 stream.relay_in(there, unit)
@@ -326,11 +351,11 @@
         i, b = half(s), odd(s)
         more = q + 1 < self.layers
 
-        @pl.when((s == 0) & (q > 0))
+        @when(both(s == 0, q > 0))
         def _():
             self.stream.pushed(self.layer_at(q - 1), self.keep)
 
-        @pl.when((s == 0) & more)
+        @when(both(s == 0, more))
         def _():
             for at, device in enumerate(self.place.peers()):
                 notify(self.credit.at[at], device)
@@ -340,65 +365,57 @@
         self.push_parts(q, s)
         for condition, count, unit in self.sends(q, s):
 
-            @pl.when(condition)
+            @when(condition)
             def _():
                 self.stream.forward(self.layer_at(count), self.unit_at(unit))
 
-        @pl.when(b == 0)
+        @when(b == 0)
         def _():
             self.load(q, i, 1)
 
         early = more & (q > 0) if self.keep else more
-        for condition, count, unit in (((b == 1) & (i < 3), q, i + 1), ((s == 7) & early, q + 1, 0)):
-
-            @pl.when(condition)
+        for condition, count, unit in ((both(b == 1 and i < 3, q > 0), q, i + 1), (both(s == 7, early), q + 1, 0)):
+
+            @when(condition)
             def _():
                 self.stream.arrive(self.layer_at(count), self.unit_at(unit))
                 self.load(count, unit, 0)
 
         self.stream.loaded(self.w_in_v, self.w_out_v, b, self.load_sem)
 
+    def late(self, q, s):
+        i, b = half(s), odd(s)
+
+        @when(both(b == 1 and i < 3, q == 0))
+        def _():
+            self.stream.arrive(self.layer_at(q), self.unit_at(i + 1))
+            self.load(q, i + 1, 0)
+
     def after(self, q, s):
         for condition, count, unit in self.sends(q, s):
 
-            @pl.when(condition)
+            @when(condition)
             def _():
                 self.stream.forwarded(self.layer_at(count), self.unit_at(unit))
 
         if self.keep:
 
-            @pl.when((s == 7) & (q == 0) & (q + 1 < self.layers))
+            @when(both(s == 7, (q == 0) & (q + 1 < self.layers)))
             def _():
                 self.first_chunk(q + 1)
 
 
-def when(condition):
-    if isinstance(condition, bool):
-        return lambda body: body() if condition else None
-    return pl.when(condition)
-
-
-def both(*conditions):
-    kept = [c for c in conditions if not (isinstance(c, bool) and c)]
-    if any(isinstance(c, bool) for c in kept):
-        return False
-    if not kept:
-        return True
-    return functools.reduce(lambda a, b: a & b, kept)
-
-
-BACKWARD_UNITS = (1, 3, 2, 0)
-
-
-def backward_mask(unit):
-    if isinstance(unit, int):
-        return BACKWARD_UNITS[unit]
-    return (1 - half(unit)) + 2 * lax.rem(half(unit + 1), 2)
+BACKWARD_UNITS = (3, 2, 1, 0)
 
 
 class Reduce:
     PARTS = ((0, 1), (0, 0), (1, 1), (1, 0))
-    SECOND = (0, 1, 3, 4)
+    SECOND = (0, 1, 2, 4)
+    THIRD = (7, 5)
+    OUT = (4, 7)
+    SENT = ((5, 5), (0, 1))
+    NEXT = (1, 5)
+    LAST = (3, 6)
 
     def __init__(self, place, layers, hbm, vmem, sems, outs):
         self.place, self.layers = place, layers
@@ -443,7 +460,10 @@
 
     def across_x_out(self, q, i, h):
         s = self.slot(q)
-        return remote(self.p_out.at[s, i, h], self.o_a.at[s, i, h], self.oa_send.at[i, h], self.oa_recv.at[s, i, h], self.place.across(1))
+        at = i // TWO
+        return remote(
+            self.p_out.at[s, i, h], self.o_a.at[s, at, h], self.oa_send.at[at, h], self.oa_recv.at[s, at, h], self.place.across(1)
+        )
 
     def across_y_out(self, q, h):
         s = self.slot(q)
@@ -451,14 +471,14 @@
 
     def across_y_in(self, q, i, b):
         s, far = self.slot(q), pl.ds(pl.multiple_of((1 - self.place.chip_y) * self.side, self.side), self.side)
-        there = i + 1 - 2 * (i % 2)
+        there = (i + TWO) % CHIPS
         return remote(
             self.q_in.at[s, i, b, far], self.i_a.at[s, there, b], self.ia_send.at[i, b], self.ia_recv.at[s, there, b], self.place.across(2)
         )
 
     def across_x_in(self, q, i, b):
         s, far = self.slot(q), pl.ds(pl.multiple_of((1 - self.place.chip_x) * self.row, self.row), self.row)
-        there = 3 - i
+        there = i ^ 1
         return remote(
             self.s_in.at[s, i, b, far], self.i_b.at[s, there, b], self.ib_send.at[i, b], self.ib_recv.at[s, there, b], self.place.across(1)
         )
@@ -483,16 +503,16 @@
     def out_loads(self, a, b):
         return [pltpu.make_async_copy(a, self.out_a, self.out_sem.at[0]), pltpu.make_async_copy(b, self.out_b, self.out_sem.at[1])]
 
-    def out_first(self, q):
-        return self.out_loads(self.o_a.at[self.slot(q), 0, 0], self.o_a.at[self.slot(q), 0, 1])
-
     def out_second(self, q, h):
         s = self.slot(q)
-        return self.out_loads(self.p_out.at[s, 2, h], self.o_a.at[s, 1, h])
+        return self.out_loads(self.p_out.at[s, 1, h], self.o_a.at[s, 0, h])
 
     def out_third(self, q, h):
         s = self.slot(q)
-        return self.out_loads(self.p_out.at[s, 3, h], self.o_b.at[s, h])
+        return self.out_loads(self.p_out.at[s, 3, h], self.o_a.at[s, 1, h])
+
+    def out_last(self, q, h):
+        return [pltpu.make_async_copy(self.o_b.at[self.slot(q), h], self.out_b, self.out_sem.at[1])]
 
     def out_second_save(self, q, h):
         return pltpu.make_async_copy(self.out_a, self.u_out.at[self.slot(q), h], self.out_save)
@@ -505,7 +525,7 @@
         s, near = self.slot(q), pl.ds(pl.multiple_of(self.place.chip_y * self.side, self.side), self.side)
         copies = []
         for at in range(TWO):
-            i, rows = TWO * pair + at, pl.ds(at * self.side, self.side)
+            i, rows = pair + TWO * at, pl.ds(at * self.side, self.side)
             copies.append(pltpu.make_async_copy(self.q_in.at[s, i, b, near], self.in_a.at[rows], self.in_sem.at[0, at]))
             copies.append(pltpu.make_async_copy(self.i_a.at[s, i, b], self.in_b.at[rows], self.in_sem.at[1, at]))
         return copies
@@ -522,7 +542,7 @@
     def in_second_save(self, q, pair, b):
         s = self.slot(q)
         return [
-            pltpu.make_async_copy(self.in_a.at[pl.ds(at * self.side, self.side)], self.s_in.at[s, TWO * pair + at, b], self.in_save.at[at])
+            pltpu.make_async_copy(self.in_a.at[pl.ds(at * self.side, self.side)], self.s_in.at[s, pair + TWO * at, b], self.in_save.at[at])
             for at in range(TWO)
         ]
 
@@ -551,6 +571,15 @@
     def mid(self, q, s):
         here, older, prev = q < self.layers, q > 0, q - 1
 
+        for (pair, b), step in zip(self.PARTS, self.SECOND):
+
+            @when(both(s == step + 1, older))
+            def _():
+                for copy in self.in_second_save(prev, pair, b):
+                    copy.wait()
+                for at in range(TWO):
+                    self.resend(prev, lambda q, at=at: self.across_x_in(q, pair + TWO * at, b))
+
         for t in range(STEPS):
             i, b = divmod(t, TWO)
             layer, real = (q, here) if t < 7 else (prev, older)
@@ -564,6 +593,7 @@
                 for copy in self.save_p(layer, i):
                     copy.wait()
                 self.save_q(layer, i, 1, 0).wait()
+                self.resend(layer, lambda q: self.across_y_in(q, i, 1))
 
             layer, real = (q, here) if t < 5 else (prev, older)
             if b == 0:
@@ -571,46 +601,34 @@
                 @when(both(s == (t + 3) % STEPS, real))
                 def _():
                     self.save_q(layer, i, 0, 0).wait()
-
-        for (pair, b), step in zip(self.PARTS, self.SECOND):
-
-            @when(both(s == step + 1, older))
-            def _():
-                for copy in self.in_second_save(prev, pair, b):
-                    copy.wait()
-                for at in range(TWO):
-                    self.resend(prev, lambda q, at=at: self.across_x_in(q, TWO * pair + at, b))
-
-        for i in range(CHIPS):
-            layer, real = (q, here) if i < 3 else (prev, older)
-
-            @when(both(s == (2 * i + 3) % STEPS, real))
-            def _():
-                for b in (1, 0):
-                    self.resend(layer, lambda q, b=b: self.across_y_in(q, i, b))
-
-        for at in range(CHIPS):
-
-            @when(both(s == 3 + at, here))
-            def _():
-                i, h = divmod(at, TWO)
-                self.resend(q, lambda q: self.across_x_out(q, i, h))
+                    self.resend(layer, lambda q: self.across_y_in(q, i, 0))
 
         for h in range(TWO):
 
-            @when(both(s == 1 + h, older))
-            def _():
-                self.out_second_save(prev, h).wait()
-
-            @when(both(s == 2 + 2 * h, older))
-            def _():
-                self.resend(prev, lambda q: self.across_y_out(q, h))
-
-            @when(both(s == 5 + 2 * h, older))
+            @when(both(s == TWO + h, here))
+            def _():
+                self.resend(q, lambda q: self.across_x_out(q, 0, h))
+
+            @when(both(s == 6, here))
+            def _():
+                self.resend(q, lambda q: self.across_x_out(q, 2, h))
+
+            layer, real = (prev, older) if h else (q, here)
+            saved, sent = self.SENT[h]
+
+            @when(both(s == saved, real))
+            def _():
+                self.out_second_save(layer, h).wait()
+
+            @when(both(s == sent, real))
+            def _():
+                self.resend(layer, lambda q: self.across_y_out(q, h))
+
+            @when(both(s == self.LAST[h] + 1, older))
             def _():
                 self.out_third_save(prev, h).wait()
 
-        @when(both(s == 7, older))
+        @when(both(s == 6, older))
         def _():
             for copy in self.in_third_save(prev, 1):
                 copy.wait()
@@ -625,38 +643,37 @@
             @when(both(s == step, older))
             def _():
                 for at in range(TWO):
-                    self.across_y_in(prev, TWO * pair + 1 - at, b).wait_recv()
+                    self.across_y_in(prev, (pair + TWO * at + TWO) % CHIPS, b).wait_recv()
                 for copy in self.in_second(prev, pair, b):
                     copy.start()
 
-        for b in range(TWO):
-
-            @when(both(s == 7 - b, older))
+        for b, step in enumerate(self.THIRD):
+
+            @when(both(s == step, older))
             def _():
                 for i in range(CHIPS):
-                    self.across_x_in(prev, 3 - i, b).wait_recv()
+                    self.across_x_in(prev, i ^ 1, b).wait_recv()
                 for copy in self.in_third(prev, b):
                     copy.start()
 
-        @when(both(s == 7, here))
-        def _():
-            for h in range(TWO):
+        for h in range(TWO):
+
+            @when(both(s == self.OUT[h], here))
+            def _():
                 self.across_x_out(q, 0, h).wait_recv()
-            for copy in self.out_first(q):
-                copy.start()
-
-        for h in range(TWO):
-
-            @when(both(s == h, older))
-            def _():
-                self.across_x_out(prev, 1, h).wait_recv()
-                for copy in self.out_second(prev, h):
+                for copy in self.out_second(q, h):
                     copy.start()
 
-            @when(both(s == 4 + 2 * h, older))
+            @when(both(s == self.NEXT[h], older))
+            def _():
+                self.across_x_out(prev, 2, h).wait_recv()
+                for copy in self.out_third(prev, h):
+                    copy.start()
+
+            @when(both(s == self.LAST[h], older))
             def _():
                 self.across_y_out(prev, h).wait_recv()
-                for copy in self.out_third(prev, h):
+                for copy in self.out_last(prev, h):
                     copy.start()
 
     def end(self, q, s, gm):
@@ -682,14 +699,6 @@
                 def _():
                     self.free(self.credit_o)
 
-                if i == 3:
-                    for copy in self.out_first(q):
-                        copy.wait()
-                    for start in range(0, self.r_v.shape[0], ADD_ROWS):
-                        rows = pl.ds(start, ADD_ROWS)
-                        for h, part in enumerate((self.out_a, self.out_b)):
-                            columns = pl.ds(h * self.half_out, self.half_out)
-                            self.r_v[rows, columns] = self.r_v[rows, columns] + part[rows, :]
                 for copy in self.save_p(q, i):
                     copy.start()
                 self.twin_in(0).wait_recv()
@@ -731,17 +740,21 @@
 
         for b in range(TWO):
 
-            @when(both(s == 7 - b, older))
+            @when(both(s == self.THIRD[b], older))
             def _():
                 summed(ins, self.in_third(prev, b), self.in_third_save(prev, b))
 
-            @when(both(s == b, older))
-            def _():
-                summed(outs, self.out_second(prev, b), [self.out_second_save(prev, b)])
-
-            @when(both(s == 4 + 2 * b, older))
-            def _():
-                summed(outs, self.out_third(prev, b), [self.out_third_save(prev, b)])
+            @when(both(s == self.OUT[b], here))
+            def _():
+                summed(outs, self.out_second(q, b), [self.out_second_save(q, b)])
+
+            @when(both(s == self.NEXT[b], older))
+            def _():
+                summed(outs, self.out_third(prev, b), [])
+
+            @when(both(s == self.LAST[b], older))
+            def _():
+                summed(outs, self.out_last(prev, b), [self.out_third_save(prev, b)])
 
     def finish(self):
         q = self.layers
@@ -752,7 +765,7 @@
         for copy in self.in_third_save(last, 0):
             copy.wait()
         for h in range(TWO):
-            for i in range(TWO):
+            for i in (0, 2):
                 self.across_x_out(last, i, h).wait_send()
             self.across_y_out(last, h).wait_send()
         for b in range(TWO):
@@ -835,17 +848,23 @@
             finish()
 
     def step(n, s):
-        v = odd(s)
-        pace.before(n, s)
-        for phase in range(3):
-
-            @pl.when((s == 1 + phase) & (n + 2 < layers))
-            def _():
-                to_lanes(n + 2, phase)
+        def before(k):
+            pace.before(n, k)
+            if 0 < k < 4:
+
+                @pl.when(n + 2 < layers)
+                def _():
+                    to_lanes(n + 2, k - 1)
+
+        def after(k):
+            pace.late(n, k)
+            pace.after(n, k)
+
+        by_step(s, before)
 
         @pl.when(s < 7)
         def _():
-            compute(v, False)
+            compute(odd(s), False)
 
         @pl.when(s == 7)
         def _():
@@ -853,10 +872,10 @@
             def _():
                 save(n - 1).wait()
 
-            compute(v, True)
+            compute(1, True)
             save(n).start()
 
-        pace.after(n, s)
+        by_step(s, after)
 
     def layer_step(n, carry):
         lax.fori_loop(0, STEPS, lambda s, c: (step(n, s), c)[1], 0)
@@ -876,7 +895,7 @@
     stream_sems, sum_sems = refs[36:44], refs[44:]
     place = Place()
     stream = Stream(place, BACKWARD_UNITS, own_in, own_out, kept_in, kept_out, got_in, got_out, twin_in, twin_out, stream_sems)
-    pace = Pace(place, stream, layers, lambda q: layers - 1 - q, backward_mask, False, (w_in_v, w_out_v, load_sem), credit)
+    pace = Pace(place, stream, layers, lambda q: layers - 1 - q, lambda i: CHIPS - 1 - i, False, (w_in_v, w_out_v, load_sem), credit)
     sums = Reduce(place, layers, sums_hbm, sums_v, sum_sems, (gw_in, gw_out))
     r_v, gt_v, gm_v = sums_v[:3]
     blocks_d, tokens, _ = unit_v.shape
@@ -971,12 +990,20 @@
 
     def step(q, s):
         gm = lax.rem(STEPS * q + s, 3)
-        pace.before(q, s)
+
+        def middle(k):
+            pace.late(q, k)
+            sums.mid(q, k)
+
+        def after(k):
+            sums.end(q, k, gm)
+            pace.after(q, k)
+
+        by_step(s, lambda k: pace.before(q, k))
         hidden_part(odd(s))
-        sums.mid(q, s)
+        by_step(s, middle)
         gradient_part(gm)
-        sums.end(q, s, gm)
-        pace.after(q, s)
+        by_step(s, after)
 
     def layer_step(q, carry):
         n = layers - 1 - q

time: 1710 us -> 1650 us (0.965)
  Pallas kernels: 1660 us -> 1600 us
    pallas_call x1, Pallas kernels: 1200 us -> 1140 us  [backward_stack(): pl.pallas_call(functools.partial(backward_stack_kernel, layers), in_specs...]
where the time goes in v6:
time: 1650 us; the launch traced here: 1630 us
  Pallas kernels  1600 us (97%)
  local copies, waits for them, and re-layouts  29.3 us (2%)
    pallas_call x1, Pallas kernels, backward_stack(): pl.pallas_call(functools.partial(backward_stack_kernel, layers), in_specs...  1140 us
    pallas_call x1, Pallas kernels, forward_stack(): pl.pallas_call(functools.partial(forward_stack_kernel, layers), in_specs=...  459 us

profile of v6, /device:TPU:0, one launch (start us, length us, event | category | flops | bytes accessed | tf_op | source)
XLA Modules:
  0.0 1633.3 jit_solution(2916076137101289865)
XLA Ops:
  0.6 459.2 %forward_stack.1 = (bf16[5,4096,1024]{2,1,0:T(8,128)(2,1)}, bf16[5,32,128,128]{3,2,1,0:T(8,128)(2,1)}, bf16[5,8,512,128]{3,2,1,0:T(8,128)(2,1)}, bf16[5,32,128,1...) custom-call(bf16[4096,1024]{1,0:T(8,128)(2,1)} %x_ref.3, ...), custom_call_target="tpu_custom_call" | custom-call | flops 343597383680 | bytes 100000000 | tf_op jit(solution)/shard_map/forward_stack/pallas_call | solution.py:1103
  459.9 1143.6 %backward_stack.1 = (f32[5,128,4096]{2,1,0:T(8,128)}, f32[5,512,1024]{2,1,0:T(8,128)}, bf16[4096,1024]{1,0:T(8,128)(2,1)}, bf16[2,2,32,128,128]{4,3,2,1,0:T(8,12...) custom-call(bf16[4096,1024]{1,0:T(8,128)(2,1)} %x_ref.3, ...), custom_call_target="tpu_custom_call" | custom-call | flops 858993459200 | bytes 300000000 | tf_op jit(solution)/shard_map/backward_stack/pallas_call | solution.py:1153
  1603.5 0.0 slice-start
  1603.5 0.0 slice-start.1
  1603.6 8.0 slice_bitcast_fusion
  1611.5 0.0 slice-start.2
  1611.5 9.5 copy.11
  1621.0 0.0 slice-done
  1621.0 0.0 slice-done.1
  1621.0 0.0 slice-done.2
  1621.0 4.1 copy.12
  1625.1 7.8 copy.13
  (1 shorter events, 0.0 us)
Async XLA Ops:
  1603.5 17.5 %slice-start = ((s8[10485760]{0:T(1024)(128)(4,1)}), s8[4194304]{0:T(1024)(128)(4,1)S(1)}, s32[]{:S(2)}) async-start(s8[10485760]{0:T(1024)(128)(4,1)} %bitcast.2), calls=%async_computation | async-start | bytes 8388608
  1603.5 17.5 %slice-start.1 = ((s8[10485760]{0:T(1024)(128)(4,1)}), s8[2097152]{0:T(1024)(128)(4,1)S(1)}, s32[]{:S(2)}) async-start(s8[10485760]{0:T(1024)(128)(4,1)} %bitcast.2), calls=%async_computation.1 | async-start | bytes 4194304
  1611.5 9.5 slice-start.2

commit v7 on v6

--- a/solution.py
+++ b/solution.py
@@ -172,9 +172,10 @@
         for mask in masks:
             self.send_out(n, mask).start()
 
-    def relay_in(self, n, unit):
-        self.got_slice(n, 1, 2 ^ unit).wait_recv()
-        self.send_in(n, 3, unit).start()
+    def relay_in(self, n, units):
+        for unit in units:
+            self.got_slice(n, 1, 2 ^ unit).wait_recv()
+            self.send_in(n, 3, unit).start()
 
     def relay_out(self, n):
         self.send_out(n, 2).wait_recv()
@@ -263,6 +264,9 @@
 
 
 class Pace:
+    LATE = ((1, 0, 0, 1), (1, 0, 1, 1), (0, 0, 0, 0))
+    PUSH = ((1, 1, 0, 1, 5, 6, 7), (2, 0, 4, 2, 3, 1, 7), (0, 1, 1, 3, 4, 5, 6))
+
     def __init__(self, place, stream, layers, layer_at, unit_at, keep, bufs, credit):
         self.place, self.stream, self.layers, self.layer_at, self.unit_at = place, stream, layers, layer_at, unit_at
         self.keep, self.credit = keep, credit
@@ -272,28 +276,26 @@
         self.stream.load(self.layer_at(q), self.unit_at(i), b, self.w_in_v, self.w_out_v, b, self.load_sem)
 
     def head(self):
-        n, units = self.layer_at(0), self.stream.order
+        n, stream = self.layer_at(0), self.stream
         if not self.keep:
-            self.stream.push_in(n, (2, 3), units)
-            self.stream.push_out(n, (3, 1))
+            stream.push_in(n, (2, 3), stream.order)
+            stream.push_out(n, (3, 1))
             return
-        self.stream.push_in(n, (1,), [units[at] for at in (0, 2, 3, 1)])
-        self.stream.push_in(n, (2,), units[:1])
-        self.stream.push_out(n, (1,))
+        stream.push_in(n, (1,), (2, 3, 1, 0))
+        stream.push_out(n, (1,))
+        stream.push_in(n, (2,), (0, 1))
 
     def head_end(self):
-        n, units = self.layer_at(0), self.stream.order
+        n, stream = self.layer_at(0), self.stream
         if not self.keep:
             self.first_chunk(0)
             return
-        for at, unit in enumerate(units):
-            if at:
-                self.stream.push_in(n, (2,), (unit,))
-            if at == 3:
-                self.first_chunk(0)
-            self.stream.relay_in(n, unit)
-            if at == 1:
-                self.stream.push_out(n, (2,))
+        stream.relay_in(n, (0, 1))
+        stream.push_out(n, (2,))
+        stream.relay_in(n, (2,))
+        self.first_chunk(0)
+        stream.push_in(n, (2,), (2, 3))
+        stream.relay_in(n, (3,))
 
     def first_chunk(self, q):
         n, unit = self.layer_at(q), self.unit_at(0)
@@ -302,20 +304,25 @@
         self.load(q, 0, 0)
         self.stream.forwarded(n, unit)
 
+    def turns(self, q):
+        return [q == 0, q == 1, q > 1] if self.keep else [q == 0, q > 0]
+
+    def units(self, q, late):
+        units = []
+        for turn, flags in zip(self.turns(q), self.LATE if self.keep else ((1, 1, 1, 0), (0, 0, 0, 0))):
+            for i, flag in enumerate(flags):
+                if flag == late:
+                    count, real = (q, True) if i < 3 else (q + 1, q + 1 < self.layers)
+                    units.append((2 * i, both(turn, real), count, (i + 1) % CHIPS))
+        return units
+
     def sends(self, q, s):
-        i, b = half(s), odd(s)
-        early = (q + 1 < self.layers) & (q > 0) if self.keep else q + 1 < self.layers
-        return [
-            (both(s == 6, early), q + 1, 0),
-            (both(b == 0 and i < 3, q > 0), q, i + 1),
-            (both(b == 1 and i < 3, q == 0), q, i + 1),
-        ]
+        return [(both(s == step + late, turn), count, unit) for late in range(TWO) for step, turn, count, unit in self.units(q, late)]
 
     def push_parts(self, q, s):
         stream, units = self.stream, self.stream.order
         there, more = self.layer_at(q + 1), q + 1 < self.layers
         if not self.keep:
-
             for at, (step, mask) in enumerate(((1, 3), (4, 1))):
 
                 @when(both(s == 3 * at, more))
@@ -328,24 +335,21 @@
 
             return
 
-        turn = q > 0 if s == 0 else q == 0
-
-        @when(both(s in (0, 3), turn))
-        def _():
-            stream.relay_out(self.layer_at(q))
-
-        @when(both(s == 0, more))
-        def _():
-            stream.push_in(there, (1, 2), units)
-
-        @when(both(s in (0, 3), turn, more))
-        def _():
-            stream.push_out(there, (1, 2))
-
-        @when(both(s == 5, more))
-        def _():
-            for unit in units:
-                stream.relay_in(there, unit)
+        parts = (
+            (True, lambda: stream.relay_out(self.layer_at(q))),
+            (more, lambda: stream.push_in(there, (1,), (2, 3, 0, 1))),
+            (more, lambda: stream.push_in(there, (2,), units)),
+            (more, lambda: stream.push_out(there, (1,))),
+            (more, lambda: stream.relay_in(there, (0, 1))),
+            (more, lambda: stream.push_out(there, (2,))),
+            (more, lambda: stream.relay_in(there, (2, 3))),
+        )
+        for at, (real, part) in enumerate(parts):
+            for turn, steps in zip(self.turns(q), self.PUSH):
+
+                @when(both(s == steps[at], turn, real))
+                def _():
+                    part()
 
     def before(self, q, s):
         i, b = half(s), odd(s)
@@ -373,23 +377,19 @@
         def _():
             self.load(q, i, 1)
 
-        early = more & (q > 0) if self.keep else more
-        for condition, count, unit in ((both(b == 1 and i < 3, q > 0), q, i + 1), (both(s == 7, early), q + 1, 0)):
-
-            @when(condition)
+        self.fetch_unit(q, s, 0)
+        self.stream.loaded(self.w_in_v, self.w_out_v, b, self.load_sem)
+
+    def fetch_unit(self, q, s, late):
+        for step, turn, count, unit in self.units(q, late):
+
+            @when(both(s == step + 1, turn))
             def _():
                 self.stream.arrive(self.layer_at(count), self.unit_at(unit))
                 self.load(count, unit, 0)
 
-        self.stream.loaded(self.w_in_v, self.w_out_v, b, self.load_sem)
-
     def late(self, q, s):
-        i, b = half(s), odd(s)
-
-        @when(both(b == 1 and i < 3, q == 0))
-        def _():
-            self.stream.arrive(self.layer_at(q), self.unit_at(i + 1))
-            self.load(q, i + 1, 0)
+        self.fetch_unit(q, s, 1)
 
     def after(self, q, s):
         for condition, count, unit in self.sends(q, s):
@@ -397,12 +397,6 @@
             @when(condition)
             def _():
                 self.stream.forwarded(self.layer_at(count), self.unit_at(unit))
-
-        if self.keep:
-
-            @when(both(s == 7, (q == 0) & (q + 1 < self.layers)))
-            def _():
-                self.first_chunk(q + 1)
 
 
 BACKWARD_UNITS = (3, 2, 1, 0)

time: 1650 us -> 1630 us (0.988)
    pallas_call x1, Pallas kernels: 459 us -> 442 us  [forward_stack(): pl.pallas_call(functools.partial(forward_stack_kernel, layers), in_specs=...]
where the time goes in v7:
time: 1630 us; the launch traced here: 1620 us
  Pallas kernels  1590 us (98%)
  local copies, waits for them, and re-layouts  29.3 us (2%)
    pallas_call x1, Pallas kernels, backward_stack(): pl.pallas_call(functools.partial(backward_stack_kernel, layers), in_specs...  1140 us
    pallas_call x1, Pallas kernels, forward_stack(): pl.pallas_call(functools.partial(forward_stack_kernel, layers), in_specs=...  442 us

profile of v7, /device:TPU:0, one launch (start us, length us, event | category | flops | bytes accessed | tf_op | source)
XLA Modules:
  0.0 1616.4 jit_solution(10580142662406976980)
XLA Ops:
  0.6 441.9 %forward_stack.1 = (bf16[5,4096,1024]{2,1,0:T(8,128)(2,1)}, bf16[5,32,128,128]{3,2,1,0:T(8,128)(2,1)}, bf16[5,8,512,128]{3,2,1,0:T(8,128)(2,1)}, bf16[5,32,128,1...) custom-call(bf16[4096,1024]{1,0:T(8,128)(2,1)} %x_ref.3, ...), custom_call_target="tpu_custom_call" | custom-call | flops 343597383680 | bytes 100000000 | tf_op jit(solution)/shard_map/forward_stack/pallas_call | solution.py:1097
  442.5 1144.2 %backward_stack.1 = (f32[5,128,4096]{2,1,0:T(8,128)}, f32[5,512,1024]{2,1,0:T(8,128)}, bf16[4096,1024]{1,0:T(8,128)(2,1)}, bf16[2,2,32,128,128]{4,3,2,1,0:T(8,12...) custom-call(bf16[4096,1024]{1,0:T(8,128)(2,1)} %x_ref.3, ...), custom_call_target="tpu_custom_call" | custom-call | flops 858993459200 | bytes 300000000 | tf_op jit(solution)/shard_map/backward_stack/pallas_call | solution.py:1147
  1586.6 0.0 slice-start
  1586.7 0.0 slice-start.1
  1586.7 8.0 slice_bitcast_fusion
  1594.6 0.0 slice-start.2
  1594.6 9.5 copy.11
  1604.1 0.0 slice-done
  1604.1 0.0 slice-done.1
  1604.1 0.0 slice-done.2
  1604.2 4.1 copy.12
  1608.2 7.8 copy.13
  (1 shorter events, 0.0 us)
Async XLA Ops:
  1586.6 17.5 %slice-start = ((s8[10485760]{0:T(1024)(128)(4,1)}), s8[4194304]{0:T(1024)(128)(4,1)S(1)}, s32[]{:S(2)}) async-start(s8[10485760]{0:T(1024)(128)(4,1)} %bitcast.2), calls=%async_computation | async-start | bytes 8388608
  1586.7 17.5 %slice-start.1 = ((s8[10485760]{0:T(1024)(128)(4,1)}), s8[2097152]{0:T(1024)(128)(4,1)S(1)}, s32[]{:S(2)}) async-start(s8[10485760]{0:T(1024)(128)(4,1)} %bitcast.2), calls=%async_computation.1 | async-start | bytes 4194304
  1594.6 9.5 slice-start.2

commit v8 on v7

--- a/solution.py
+++ b/solution.py
@@ -1001,12 +1001,13 @@
 
     def layer_step(q, carry):
         n = layers - 1 - q
+        fetch(n, 0, 0)
+
+        @pl.when(n > 0)
+        def _():
+            fetch(n - 1, 1, 0)
+
         lax.fori_loop(0, STEPS, lambda s, c: (step(q, s), c)[1], 0)
-        fetch(n, 0, 0)
-
-        @pl.when(n > 0)
-        def _():
-            fetch(n - 1, 1, 0)
 
         def close(t, carry):
             @pl.when(t + 1 < tiles)

time: 1630 us -> 1630 us (level)
  no operation moved by 1% of the time
where the time goes in v8:
time: 1630 us; the launch traced here: 1610 us
  Pallas kernels  1580 us (97%)
  local copies, waits for them, and re-layouts  29.3 us (2%)
    pallas_call x1, Pallas kernels, backward_stack(): pl.pallas_call(functools.partial(backward_stack_kernel, layers), in_specs...  1140 us
    pallas_call x1, Pallas kernels, forward_stack(): pl.pallas_call(functools.partial(forward_stack_kernel, layers), in_specs=...  442 us

profile of v8, /device:TPU:0, one launch (start us, length us, event | category | flops | bytes accessed | tf_op | source)
XLA Modules:
  0.0 1612.2 jit_solution(12226994130040951432)
XLA Ops:
  0.6 441.9 %forward_stack.1 = (bf16[5,4096,1024]{2,1,0:T(8,128)(2,1)}, bf16[5,32,128,128]{3,2,1,0:T(8,128)(2,1)}, bf16[5,8,512,128]{3,2,1,0:T(8,128)(2,1)}, bf16[5,32,128,1...) custom-call(bf16[4096,1024]{1,0:T(8,128)(2,1)} %x_ref.3, ...), custom_call_target="tpu_custom_call" | custom-call | flops 343597383680 | bytes 100000000 | tf_op jit(solution)/shard_map/forward_stack/pallas_call | solution.py:1098
  442.5 1140.0 %backward_stack.1 = (f32[5,128,4096]{2,1,0:T(8,128)}, f32[5,512,1024]{2,1,0:T(8,128)}, bf16[4096,1024]{1,0:T(8,128)(2,1)}, bf16[2,2,32,128,128]{4,3,2,1,0:T(8,12...) custom-call(bf16[4096,1024]{1,0:T(8,128)(2,1)} %x_ref.3, ...), custom_call_target="tpu_custom_call" | custom-call | flops 858993459200 | bytes 300000000 | tf_op jit(solution)/shard_map/backward_stack/pallas_call | solution.py:1148
  1582.5 0.0 slice-start
  1582.5 0.0 slice-start.1
  1582.5 8.0 slice_bitcast_fusion
  1590.5 0.0 slice-start.2
  1590.5 9.5 copy.11
  1600.0 0.0 slice-done
  1600.0 0.0 slice-done.1
  1600.0 0.0 slice-done.2
  1600.0 4.1 copy.12
  1604.1 7.8 copy.13
  (1 shorter events, 0.0 us)
Async XLA Ops:
  1582.5 17.5 %slice-start = ((s8[10485760]{0:T(1024)(128)(4,1)}), s8[4194304]{0:T(1024)(128)(4,1)S(1)}, s32[]{:S(2)}) async-start(s8[10485760]{0:T(1024)(128)(4,1)} %bitcast.2), calls=%async_computation | async-start | bytes 8388608
  1582.5 17.5 %slice-start.1 = ((s8[10485760]{0:T(1024)(128)(4,1)}), s8[2097152]{0:T(1024)(128)(4,1)S(1)}, s32[]{:S(2)}) async-start(s8[10485760]{0:T(1024)(128)(4,1)} %bitcast.2), calls=%async_computation.1 | async-start | bytes 4194304
  1590.5 9.5 slice-start.2
